TPU v7x, 128 devices: a whole 4x4x4 slice. The times are simulated.
128 devices in a mesh: px: 8 (over z_hi, y), py: 16 (over x, z_lo, core).
Axes of the slice: x: 4, y: 4, z: 4 (z_hi: 2, z_lo: 2; z = z_hi * 2 + z_lo), core: 2. Of those that a mesh axis runs over, the one named last changes fastest.
Arguments:
- white_noise: float32 [2, 128, 512, 256], P(None, 'px', 'py'), may hold values from -6 to 6
- spectrum: float32 [128, 512, 256], P('px', 'py'), may hold values from 0.1 to 2, as said below
- group_table: int32 [3, 16], replicated, may hold values from 0 to 15, each once within a row
Outputs:
- modulus: float32 [2, 128, 512, 256], P(None, 'px', 'py')
- level_one: float32 [2, 64, 256, 128], P(None, 'px', 'py')
- level_two: float32 [2, 32, 128, 64], P(None, 'px', 'py')
- level_three: float32 [2, 16, 64, 32], P(None, 'px', 'py')
Inputs may be any that keep to these rules, and one draw needn't show every extreme that they name: spectrum[j, m, k] equals spectrum[(128 - j) % 128, (512 - m) % 512, (256 - k) % 256]. `group_table`: each row is a permutation of 0 to 15.
All inputs are finite; a program needn't handle non-finite values.
Results may differ from a plain program's by a relative error of at most 0.000088.
Values sent between devices are 32-bit elements; how exact they have to be, the bound alone decides.
No kernel may reach another device: no remote copies, remote signals or barrier semaphores. Data moves between devices by JAX's collectives and lax.ppermute only.
A program may use at most 192 MiB of HBM per device.

v0:
```python
import math

import jax
import jax.numpy as jnp
from jax import lax
from jax.sharding import Mesh
from jax.sharding import PartitionSpec as P

PX = ("px_0", "px_1")
PY = ("py_0", "py_1", "py_2")
PX_PY = ("px_0", "px_1", "py_0", "py_1", "py_2")


def in_blocks(x, dim, size):
    before, after = (x.shape[:dim], x.shape[dim + 1 :])
    return jnp.moveaxis(x.reshape(*before, size, -1, *after), dim, 0)


def joined_along(blocks, dim):
    shape = list(blocks.shape[1:])
    shape[dim] *= blocks.shape[0]
    return jnp.moveaxis(blocks, 0, dim).reshape(shape)


def moved_by_axis(blocks, axes, order):
    inside = blocks.shape[1:]
    whole = blocks.reshape(*(lax.axis_size(a) for a in axes), *inside)
    for k in order:
        whole = lax.all_to_all(whole, axes[k], k, k, tiled=True)
    return whole.reshape(-1, *inside)


def core_and_chips(x, groups, order, split_dim, concat_dim):
    size = lax.axis_size(groups[0]) * lax.axis_size(groups[1])
    blocks = in_blocks(x, split_dim, size)
    return joined_along(moved_by_axis(blocks, groups, order), concat_dim)


def gather_together(arrays, axis, dims):
    line = jnp.concatenate([a.reshape(-1) for a in arrays])
    lines, at, gathered = (lax.all_gather(line, axis), 0, [])
    for a, dim in zip(arrays, dims):
        blocks = lines[:, at : at + a.size].reshape(-1, *a.shape)
        gathered.append(joined_along(blocks, dim))
        at += a.size
    return tuple(gathered)


def dft_tables(length, direction):
    positions = lax.iota(jnp.int32, length)
    products = positions[:, None] * positions[None, :] % length
    angles = products.astype(jnp.float32) * (2.0 * math.pi / length)
    return (jnp.cos(angles), direction * jnp.sin(angles))


def complex_apply(stacked, table_cos, table_sin, pattern):
    half_count = stacked.shape[0] // 2
    real_part = stacked[:half_count]
    imag_part = stacked[half_count:]
    real_cos = jnp.einsum(pattern, real_part, table_cos, precision=lax.Precision.HIGHEST)
    imag_sin = jnp.einsum(pattern, imag_part, table_sin, precision=lax.Precision.HIGHEST)
    imag_cos = jnp.einsum(pattern, imag_part, table_cos, precision=lax.Precision.HIGHEST)
    real_sin = jnp.einsum(pattern, real_part, table_sin, precision=lax.Precision.HIGHEST)
    return jnp.concatenate([real_cos - imag_sin, imag_cos + real_sin], 0)


def forward(payload, direction, carried_count):
    leading, length_z, cells_x, cells_y = payload.shape
    size_px = lax.axis_size(PX)
    size_py = lax.axis_size(PY)
    length_x = size_px * cells_x
    length_y = size_py * cells_y
    kept = leading - carried_count
    y_cos, y_sin = dft_tables(length_y, direction)
    x_cos, x_sin = dft_tables(length_x, direction)
    devices_all = size_px * size_py
    part_z = length_z // devices_all
    flat = payload.reshape(leading, length_z, cells_x * cells_y)
    received = lax.all_to_all(flat, PX_PY, split_axis=1, concat_axis=2, tiled=True)
    received = received.reshape(leading, part_z, size_px, size_py, cells_x, cells_y)
    along_y = complex_apply(
        received[:kept],
        y_cos.reshape(size_py, cells_y, length_y),
        y_sin.reshape(size_py, cells_y, length_y),
        "lkpqxb,qbm->lkpxm",
    )
    spectral = complex_apply(
        along_y,
        x_cos.reshape(size_px, cells_x, length_x),
        x_sin.reshape(size_px, cells_x, length_x),
        "lkpxm,pxj->lkjm",
    )
    carried = jnp.transpose(received[kept:], (0, 1, 2, 4, 3, 5)).reshape(
        carried_count, part_z, length_x, length_y
    )
    return (spectral, carried)


def backward(spectral, direction):
    leading, part_z, length_x, length_y = spectral.shape
    size_px = lax.axis_size(PX)
    size_py = lax.axis_size(PY)
    cells_x = length_x // size_px
    cells_y = length_y // size_py
    x_cos, x_sin = dft_tables(length_x, direction)
    y_cos, y_sin = dft_tables(length_y, direction)
    devices_all = size_px * size_py
    along_x = complex_apply(
        spectral,
        x_cos.reshape(length_x, size_px, cells_x),
        x_sin.reshape(length_x, size_px, cells_x),
        "lkjm,jpx->lkpxm",
    )
    arranged = complex_apply(
        along_x,
        y_cos.reshape(length_y, size_py, cells_y),
        y_sin.reshape(length_y, size_py, cells_y),
        "lkpxm,mqb->lkpqxb",
    )
    arranged = arranged.reshape(leading, part_z, devices_all * cells_x * cells_y)
    received = core_and_chips(arranged, (("px_0", "px_1", "py_0", "py_1"), "py_2"), (1, 0), 2, 1)
    return received.reshape(leading, devices_all * part_z, cells_x, cells_y)


def coarsen(values):
    members, size_x, size_y, size_z = values.shape
    blocks = values.reshape(members, size_x // 2, 2, size_y // 2, 2, size_z // 2, 2)
    return blocks.mean(axis=(2, 4, 6))


def on_device(white_noise, spectrum, group_table):
    members, cells_x, cells_y, length_z = white_noise.shape
    length_x = cells_x * lax.axis_size(PX)
    length_y = cells_y * lax.axis_size(PY)
    z_cos, z_sin = dft_tables(length_z, -1.0)
    paired = complex_apply(white_noise, z_cos, z_sin, "fxyz,zk->fkxy")
    spectrum_rows = jnp.transpose(spectrum, (2, 0, 1))[None]
    inverse_cos, inverse_sin = dft_tables(length_z, 1.0)
    payload = jnp.concatenate([paired, spectrum_rows], 0)
    spectral, carried = forward(payload, -1.0, 1)
    restored = backward(spectral * carried, 1.0)
    fields = complex_apply(restored, inverse_cos, inverse_sin, "lkxy,kz->lxyz")
    fields = fields * (1.0 / (length_x * length_y * length_z))
    modulus = jnp.exp(0.5 * fields)
    coarse_one = coarsen(modulus)
    coarse_two = coarsen(coarse_one)
    coarse_three = coarsen(coarse_two)
    gathered = gather_together((coarse_one, coarse_two, coarse_three), PY, (2, 2, 2))
    column = lax.axis_index(PY)
    routed = []
    for level_index in range(3):
        width = gathered[level_index].shape[2] // lax.axis_size(PY)
        source_row = group_table[level_index, column]
        routed.append(lax.dynamic_slice_in_dim(gathered[level_index], source_row * width, width, 2))
    return (modulus, routed[0], routed[1], routed[2])


def solution(mesh):
    split = Mesh(mesh.devices.reshape(2, 4, 4, 2, 2), ("px_0", "px_1", "py_0", "py_1", "py_2"))
    placed = (P(None, PX, PY, None), P(PX, PY, None), P())
    return jax.shard_map(
        on_device,
        mesh=split,
        in_specs=placed,
        out_specs=(
            P(None, PX, PY, None),
            P(None, PX, PY, None),
            P(None, PX, PY, None),
            P(None, PX, PY, None),
        ),
        check_vma=False,
    )
```

profile of v0, /device:TPU:1, one launch (start us, length us, event | category | flops | bytes accessed | tf_op | source)
XLA Modules:
  0.0 350.6 jit_solution(2391356412556793110)
XLA Ops:
  7.2 2.7 fusion.41
  9.9 2.7 fusion.37
  12.6 1.6 convolution_subtract_fusion.2
  14.2 1.6 convolution_add_fusion.2
  15.9 1.9 copy.71
  17.9 11.5 %all-to-all-start = ((f32[3,256,512]{2,0,1:T(4,128)}), f32[3,256,512]{2,0,1:T(4,128)S(1)}, u32[]{:S(2)}, u32[]{:S(2)}) async-start(f32[3,256,512]{2,0,1:T(4,128)} %copy.71), calls=%async_computation | async-start | bytes 4194304 | tf_op jit(solution)/shard_map/all_to_all | solution.py:79
  29.7 29.4 %all-to-all-done = f32[3,256,512]{2,0,1:T(4,128)S(1)} async-done(((f32[3,256,512]{2,0,1:T(4,128)}), f32[3,256,512]{2,0,1:T(4,128)S(1)}, u32[]{:S(2)}, u32[]{:S(2)}) %all-to-all-start) | async-done | bytes 1572896 | tf_op jit(solution)/shard_map/all_to_all | solution.py:79
  59.8 1.3 fusion.231
  61.9 1.9 reshape.435
  63.8 6.0 %convolution_bitcast_fusion.3 = f32[2,8,16,512]{3,2,1,0:T(8,128)S(1)} fusion(f32[2,8,16,16,32]{4,3,2,1,0:T(8,128)S(1)} %reshape.434, s32[16,32]{1,0:T(8,128)S(1)} %multiply_add_fusion), kind=kOutput, calls=%fused_computation.16 | convolution fusion | flops 809238528 | bytes 1050624 | tf_op jit(solution)/shard_map/lkpqxb,qbm->lkpxm/dot_general | solution.py:63
  69.8 6.4 %convolution_bitcast_fusion.6 = f32[2,8,16,512]{3,2,1,0:T(8,128)S(1)} fusion(f32[2,8,16,16,32]{4,3,2,1,0:T(8,128)S(1)} %copy-done, s32[16,32]{1,0:T(8,128)S(1)} %multiply_add_fusion), kind=kOutput, calls=%fused_computation.19 | convolution fusion | flops 809238528 | bytes 1050624 | tf_op jit(solution)/shard_map/lkpqxb,qbm->lkpxm/dot_general | solution.py:61
  76.2 6.0 %fusion.7 = f32[2,8,16,512]{3,2,1,0:T(8,128)S(1)} fusion(f32[2,8,16,512]{3,2,1,0:T(8,128)S(1)} %convolution_bitcast_fusion.3, f32[2,8,16,16,32]{4,3,2,1,0:T(8,128)S(1)} %copy-done, s32[16,32]{1,0:T(8,128)S(1)} %multiply_add_fusion), kind=kOutput, calls=%fused_computation.34 | convolution fusion | flops 809107456 | bytes 1574912 | tf_op jit(solution)/shard_map/lkpqxb,qbm->lkpxm/dot_general | solution.py:62
  82.2 6.1 %fusion.6 = f32[2,8,16,512]{3,2,1,0:T(8,128)S(1)} fusion(f32[2,8,16,512]{3,2,1,0:T(8,128)S(1)} %convolution_bitcast_fusion.6, f32[2,8,16,16,32]{4,3,2,1,0:T(8,128)S(1)} %reshape.434, s32[16,32]{1,0:T(8,128)S(1)} %multiply_add_fusion), kind=kOutput, calls=%fused_computation.33 | convolution fusion | flops 809107456 | bytes 1574912 | tf_op jit(solution)/shard_map/lkpqxb,qbm->lkpxm/dot_general | solution.py:60
  88.3 0.9 convolution_bitcast_fusion.2
  89.3 0.9 convolution_bitcast_fusion
  90.2 0.9 fusion.3
  91.2 0.9 fusion.5
  92.1 1.9 slice.52
  94.0 2.5 copy.75
  96.5 2.5 mul.576
  99.2 0.9 fusion.56
  100.1 0.9 fusion.57
  101.0 0.9 fusion.1
  101.8 7.1 %fusion.21 = f32[16,32,2,8,16]{1,4,3,2,0:T(8,128)S(1)} fusion(s32[16,32]{1,0:T(8,128)S(1)} %multiply_add_fusion, f32[2,8,16,512]{3,2,0,1:T(8,128)S(1)} %fusion.1), kind=kOutput, calls=%fused_computation.51 | convolution fusion | flops 808976384 | bytes 1050624 | tf_op jit(solution)/shard_map/lkpxm,mqb->lkpqxb/dot_general | solution.py:60
  108.9 0.9 fusion
  109.8 7.5 %fusion.19 = f32[16,32,2,8,16]{1,4,3,2,0:T(8,128)S(1)} fusion(s32[16,32]{1,0:T(8,128)S(1)} %multiply_add_fusion, f32[2,8,16,512]{3,2,0,1:T(8,128)S(1)} %fusion), kind=kOutput, calls=%fused_computation.49 | convolution fusion | flops 808976384 | bytes 1050624 | tf_op jit(solution)/shard_map/lkpxm,mqb->lkpqxb/dot_general | solution.py:62
  117.3 7.3 %subtract_bitcast_fusion = f32[1,2,8,16,16,32]{5,4,2,1,3,0:T(8,128)S(1)} fusion(f32[16,32,2,8,16]{1,4,3,2,0:T(8,128)S(1)} %fusion.21, s32[16,32]{1,0:T(8,128)S(1)} %multiply_add_fusion, f32[2,8,16,512]{3,2,0,1:T(8,128)S(1)} %fusion), kind=kOutput, calls=%fused_computation.4 | convolution fusion | flops 809107456 | bytes 1574912 | tf_op jit(solution)/shard_map/lkpxm,mqb->lkpqxb/dot_general | solution.py:61
  124.6 7.1 %add_bitcast_fusion = f32[1,2,8,16,16,32]{5,4,2,1,3,0:T(8,128)S(1)} fusion(f32[16,32,2,8,16]{1,4,3,2,0:T(8,128)S(1)} %fusion.19, s32[16,32]{1,0:T(8,128)S(1)} %multiply_add_fusion, f32[2,8,16,512]{3,2,0,1:T(8,128)S(1)} %fusion.1), kind=kOutput, calls=%fused_computation.3 | convolution fusion | flops 809107456 | bytes 1574912 | tf_op jit(solution)/shard_map/lkpxm,mqb->lkpqxb/dot_general | solution.py:63
  132.2 2.5 copy.80
  134.8 3.5 %reshape_reshape.4 = f32[2,2,128,512]{3,2,1,0:T(8,128)S(1)} reshape(f32[2,2,8,16,16,32]{5,4,3,2,1,0:T(8,128)} %copy.80) | data formatting | bytes 2097152 | tf_op jit(solution)/shard_map/reshape;reshape | solution.py:16
  139.2 5.5 %all_to_all.25 = f32[64,2,2,2,512]{4,0,3,2,1:T(8,128)S(1)} all-to-all(f32[64,2,2,2,512]{4,0,3,2,1:T(8,128)S(1)} %copy.81), channel_id=1, replica_groups=mesh['px_0'=2,'px_1'=4,'py_0'=4,'py_1'=2,'py_2'=2] {'py_2'}, dimensions={1} | all-to-all | bytes 2097152 | tf_op jit(solution)/shard_map/all_to_all | solution.py:29
  145.5 22.0 %all_to_all.26 = f32[64,2,2,2,512]{4,1,3,2,0:T(2,128)S(1)} all-to-all(f32[64,2,2,2,512]{4,1,3,2,0:T(2,128)S(1)} %copy.82), channel_id=1, replica_groups=mesh['px_0'=2,'px_1'=4,'py_0'=4,'py_1'=2,'py_2'=2] {'px_0','px_1','py_0'..., dimensions={0} | all-to-all | bytes 2097152 | tf_op jit(solution)/shard_map/all_to_all | solution.py:29
  169.2 1.0 copy.84
  170.2 2.3 fusion.75
  173.4 1.0 copy.85
  174.4 1.6 fusion.73
  176.0 2.6 convolution_subtract_fusion.1
  178.6 34.9 %concatenate.36 = f32[1,8,2,16,2,128,2]{6,5,4,3,2,1,0:T(8,128)} reshape(f32[16,32,256]{2,1,0:T(8,128)S(1)} %convolution_subtract_fusion.1) | data formatting | bytes 1048576 | tf_op jit(solution)/shard_map/concatenate | solution.py:64
  213.5 19.7 %copy.88 = f32[1,8,2,16,2,128,2]{5,3,6,4,2,1,0:T(8,128)S(1)} copy(f32[1,8,2,16,2,128,2]{6,5,4,3,2,1,0:T(8,128)} %concatenate.36) | data formatting | bytes 1048576 | tf_op jit(solution)/shard_map/concatenate | solution.py:64
  233.1 1.6 convolution_add_fusion.1
  234.7 34.9 %concatenate.37 = f32[1,8,2,16,2,128,2]{6,5,4,3,2,1,0:T(8,128)} reshape(f32[16,32,256]{2,1,0:T(8,128)S(1)} %convolution_add_fusion.1) | data formatting | bytes 1048576 | tf_op jit(solution)/shard_map/concatenate | solution.py:64
  269.6 19.4 %copy.89 = f32[1,8,2,16,2,128,2]{5,3,6,4,2,1,0:T(8,128)S(1)} copy(f32[1,8,2,16,2,128,2]{6,5,4,3,2,1,0:T(8,128)} %concatenate.37) | data formatting | bytes 1048576 | tf_op jit(solution)/shard_map/concatenate | solution.py:64
  289.2 9.7 %div.31 = f32[2,4,2,8,2,64,2]{6,5,4,3,2,1,0:T(8,128)} reshape(f32[2,8,16,128]{3,2,1,0:T(8,128)S(1)} %broadcast_multiply_fusion) | data formatting | bytes 262144 | tf_op jit(solution)/shard_map/div | solution.py:128
  298.9 4.0 %reduce_sum.28 = f32[2,4,8,64]{3,2,1,0:T(8,128)S(1)} reduce(f32[2,4,2,8,2,64,2]{6,5,4,3,2,1,0:T(8,128)} %div.31, f32[]{:T(128)} %constant.105.clone.1), dimensions={2,4,6}, to_apply=%region_1.2 | reduce | flops 28672 | bytes 147460 | tf_op jit(solution)/shard_map/reduce_sum | solution.py:128
  302.9 1.1 div.35
  307.7 1.1 fusion.14
  308.9 29.5 %all-gather.4.cloned.1.call-done = f32[16,1,37376]{2,1,0:T(1,128)} async-done(((f32[1,1,37376]{2,1,0:T(1,128)}), f32[16,1,37376]{2,1,0:T(1,128)}) %all-gather.4.cloned.1.call-update) | async-done | bytes 2392080 | tf_op jit(solution)/shard_map/all_gather | solution.py:41
  338.4 1.8 copy.129
  (48 shorter events, 11.7 us)
Async XLA Ops:
  7.2 5.4 %copy-start.1 = (f32[2,16,32,256]{3,2,1,0:T(8,128)S(1)}, f32[2,16,32,256]{3,2,1,0:T(8,128)}, u32[]{:S(2)}) copy-start(f32[2,16,32,256]{3,2,1,0:T(8,128)} %param.3) | copy-start | bytes 3145732
  9.9 5.9 %copy-start.2 = (f32[16,32,256]{2,1,0:T(8,128)S(1)}, f32[16,32,256]{2,1,0:T(8,128)}, u32[]{:S(2)}) copy-start(f32[16,32,256]{2,1,0:T(8,128)} %param.4) | copy-start | bytes 1572868
  17.9 41.2 %all-to-all-start = ((f32[3,256,512]{2,0,1:T(4,128)}), f32[3,256,512]{2,0,1:T(4,128)S(1)}, u32[]{:S(2)}, u32[]{:S(2)}) async-start(f32[3,256,512]{2,0,1:T(4,128)} %copy.71), calls=%async_computation | async-start | bytes 4194304 | tf_op jit(solution)/shard_map/all_to_all | solution.py:79
  29.4 309.0 %all-gather.4.cloned.1.call-start = ((), (), s32[]{:S(2)}) async-start(), calls=%async_computation.3 | async-start | bytes 2541568 | tf_op jit(solution)/shard_map/all_gather | solution.py:41
  63.8 6.0 %copy-start = (f32[2,8,16,16,32]{4,3,2,1,0:T(8,128)S(1)}, f32[2,8,16,16,32]{4,3,2,1,0:T(8,128)}, u32[]{:S(2)}) copy-start(f32[2,8,16,16,32]{4,3,2,1,0:T(8,128)} %reshape.435) | copy-start | bytes 1572868
  302.9 2.3 copy-start.3
Sparse Core Ops, SparseCore 0:
  305.3 33.0 all-gather.3
where the time goes:
time: 357 us; the launch traced here: 351 us
  local copies, waits for them, and re-layouts  152 us (43%)
  matrix products  77.3 us (22%)
  waiting for transfers between devices  58.9 us (16%)
  blocking collectives  27.5 us (8%)
  between operations  16.9 us (5%)
  starting transfers between devices  11.7 us (3%)
  other arithmetic  6.3 us (2%)
    concatenate x5, local copies, waits for them, and re-layouts, complex_apply(): return jnp.concatenate([real_cos - imag_sin, imag_cos + real_sin], 0)  111 us
    all_gather x1, waiting for transfers between devices, gather_together(): lines, at, gathered = (lax.all_gather(line, axis), 0, [])  29.5 us
    all_to_all x1, waiting for transfers between devices, forward(): lax.all_to_all(flat, PX_PY, split_axis=1, concat_axis=2, tiled=True)  29.4 us
    all_to_all x2, blocking collectives, moved_by_axis(): whole = lax.all_to_all(whole, axes[k], k, k, tiled=True)  27.5 us
    dot_general x6, matrix products, complex_apply(): jnp.einsum(pattern, real_part, table_cos, precision=lax.Precision.HIGHEST)  20 us
    dot_general x6, matrix products, complex_apply(): jnp.einsum(pattern, imag_part, table_sin, precision=lax.Precision.HIGHEST)  19.7 us
    dot_general x6, matrix products, complex_apply(): jnp.einsum(pattern, imag_part, table_cos, precision=lax.Precision.HIGHEST)  19.5 us
    dot_general x6, matrix products, complex_apply(): jnp.einsum(pattern, real_part, table_sin, precision=lax.Precision.HIGHEST)  18 us
  transfers between devices with their start and end apart: 2, of which 2 were waited for; matrix products, arithmetic and copies ran while one was open for 0% of the time, Pallas kernels for 0%

commit v1 on v0

v1 whole, which is shorter than its diff:
```python
import math

import jax
import jax.numpy as jnp
import ml_dtypes
import numpy as np
from jax import lax
from jax.experimental import pallas as pl
from jax.experimental.pallas import tpu as pltpu
from jax.sharding import PartitionSpec as P

NX, NY, NZ = 128, 512, 256
N_PX, N_PY = 8, 16
DEVICES = N_PX * N_PY
SEND_ROWS = 24
BACK_ROWS = 16
ROUTE_ROWS = 24
F32 = jnp.float32
BF16 = jnp.bfloat16


def halves(table):
    high = table.astype(np.float32).astype(ml_dtypes.bfloat16)
    low = (table - high.astype(np.float64)).astype(np.float32).astype(ml_dtypes.bfloat16)
    return high, low


def angle_tables(rows, columns, length):
    angles = 2.0 * math.pi * ((rows[:, None] * columns[None, :]) % length) / length
    return np.cos(angles), np.sin(angles)


def make_tables():
    d, z = np.arange(NZ // 2), np.arange(NZ)
    cos_z, sin_z = angle_tables(d, z, NZ)
    alternating = (1.0 - 2.0 * (z % 2))[None, :]
    into = np.concatenate([cos_z, alternating, -sin_z[1:]], 0)
    weight = np.where(d == 0, 1.0, 2.0)[:, None]
    back = np.concatenate([weight * cos_z, alternating, -2.0 * sin_z[1:]], 0)
    back = back * (0.5 / (NX * NY * NZ))
    y = np.arange(NY)
    cos_y, sin_y = angle_tables(y, y, NY)
    row = np.arange(NX)
    x_of = (row // 8 % 8) * 16 + (row % 8) * 2 + row // 64
    j_of = (row % 8) * 16 + (row // 8 % 4) * 4 + row // 32
    cos_x, sin_x = angle_tables(j_of, x_of, NX)
    x_into = np.block([[cos_x, sin_x], [-sin_x, cos_x]])
    x_back = x_into.T
    return dict(
        into=halves(into),
        back=halves(back),
        cos_y=halves(cos_y),
        sin_y=halves(sin_y),
        x_into=halves(x_into),
        x_back=halves(x_back),
    )


def pair_mean(size):
    rows, columns = np.arange(size), np.arange(128)
    return (0.125 * (rows[:, None] // 2 == columns[None, :])).astype(ml_dtypes.bfloat16)


def split(values):
    high = values.astype(BF16)
    return high, (values - high.astype(F32)).astype(BF16)


def product(a, b, dims=(((1,), (0,)), ((), ()))):
    return lax.dot_general(a, b, dims, preferred_element_type=F32)


def product3(a, b, dims=(((1,), (0,)), ((), ()))):
    return product(a[0], b[0], dims) + product(a[1], b[0], dims) + product(a[0], b[1], dims)


def swapped_parts(part0, part1):
    first = lax.broadcasted_iota(jnp.int32, part0.shape, 1) // 32 % 2 == 0
    new0 = jnp.where(first, part0, pltpu.roll(part1, 32, 1))
    new1 = jnp.where(first, pltpu.roll(part0, 96, 1), part1)
    return new0, new1


def blocks_transposed(parts):
    lane = lax.broadcasted_iota(jnp.int32, parts[0].shape, 1)
    low, even = lane < 64, lane // 32 % 2 == 0
    a, b, c, d = parts
    ac = jnp.where(low, a, pltpu.roll(c, 64, 1)), jnp.where(low, pltpu.roll(a, 64, 1), c)
    bd = jnp.where(low, b, pltpu.roll(d, 64, 1)), jnp.where(low, pltpu.roll(b, 64, 1), d)
    out = []
    for u, v in zip(ac, bd):
        out.append(jnp.where(even, u, pltpu.roll(v, 32, 1)))
        out.append(jnp.where(even, pltpu.roll(u, 96, 1), v))
    return out


def into_kernel(noise, spectrum, t_high, t_low, out):
    table = t_high[...], t_low[...]
    nt = (((1,), (1,)), ((), ()))
    for pair in range(4):
        starts = [f * 512 + (4 * pair + x) * 32 for x in range(4) for f in range(2)]
        block = jnp.concatenate([noise[s : s + 32, :] for s in starts], 0)
        made = product3(table, split(block), nt)
        for at in range(2):
            xh = 2 * pair + at
            part0 = made[:128, at * 128 : at * 128 + 128]
            part1 = made[128:, at * 128 : at * 128 + 128]
            out[pl.ds(xh, DEVICES, stride=SEND_ROWS), :] = part0
            out[pl.ds(8 + xh, DEVICES, stride=SEND_ROWS), :] = part1
            new0, new1 = swapped_parts(part0[:8], part1[:8])
            out[xh : xh + 1, :] = new0[:1]
            out[8 + xh : 9 + xh, :] = new1[:1]
    for q in range(4):
        rows = spectrum[q * 128 : q * 128 + 128, :]
        plane = rows[:, :128].T
        out[pl.ds(16 + q, DEVICES, stride=SEND_ROWS), :] = plane
        out[pl.ds(20 + q, DEVICES, stride=SEND_ROWS), :] = plane
        out[20 + q : 21 + q, :] = rows[:, 128:].T[:1]


def middle_kernel(got, cy_high, cy_low, sy_high, sy_low, xi_high, xi_low, xb_high, xb_low, out, high, low, scale):
    cos_y = cy_high[...], cy_low[...]
    sin_y = sy_high[...], sy_low[...]
    x_into = xi_high[...], xi_low[...]
    x_back = xb_high[...], xb_low[...]
    for q in range(4):
        lanes = slice(q * 128, q * 128 + 128)
        for part in range(2):
            pieces = []
            for i in range(4):
                at = [(px * N_PY + 4 * q + i) * SEND_ROWS + 8 * part for px in range(N_PX)]
                pieces.append(jnp.concatenate([got[s : s + 8, :] for s in at], 0))
            for b, block in enumerate(blocks_transposed(pieces)):
                xl, f = b // 2, b % 2
                row = f * 256 + part * 128 + xl * 64
                h, l = split(block)
                high[row : row + 64, lanes] = h
                low[row : row + 64, lanes] = l
        for f in range(2):
            pieces = []
            for i in range(4):
                at = [(4 * q + i) * SEND_ROWS + 16 + 4 * f + r for r in range(4)]
                step = N_PY * SEND_ROWS
                pieces.append(jnp.concatenate([got[pl.ds(s, N_PX, stride=step), :] for s in at], 0))
            for b, block in enumerate(blocks_transposed(pieces)):
                scale[f * 128 + b * 32 : f * 128 + b * 32 + 32, lanes] = block
    for f in range(2):
        rows = slice(f * 256, f * 256 + 256)
        values = high[rows, :], low[rows, :]
        by_cos = product3(values, cos_y)
        by_sin = product3(values, sin_y)
        along_y = jnp.concatenate([by_cos[:128] + by_sin[128:], by_cos[128:] - by_sin[:128]], 0)
        along_x = product3(x_into, split(along_y))
        s = scale[f * 128 : f * 128 + 128, :]
        scaled = jnp.concatenate([along_x[:128] * s, along_x[128:] * s], 0)
        values = split(product3(x_back, split(scaled)))
        high[rows, :] = values[0]
        low[rows, :] = values[1]
    done = []
    for f in range(2):
        rows = slice(f * 256, f * 256 + 256)
        values = high[rows, :], low[rows, :]
        by_cos = product3(values, cos_y)
        by_sin = product3(values, sin_y)
        done.append((by_cos[:128] - by_sin[128:], by_cos[128:] + by_sin[:128]))
    for q in range(4):
        lanes = slice(q * 128, q * 128 + 128)
        for part in range(2):
            pieces = [done[b % 2][part][(b // 2) * 64 : (b // 2) * 64 + 64, lanes] for b in range(4)]
            for i, block in enumerate(blocks_transposed(pieces)):
                for px in range(N_PX):
                    at = (px * N_PY + 4 * q + i) * BACK_ROWS + 8 * part
                    out[at : at + 8, :] = block[px * 8 : px * 8 + 8]


def last_kernel(got, b_high, b_low, mean1, mean2, mean3, modulus, route, sums, sums2, sums3):
    table = b_high[...], b_low[...]
    first_row = lax.broadcasted_iota(jnp.int32, (128, 128), 0) == 0
    for pair in range(4):
        rows = []
        for at in range(2):
            xh = 2 * pair + at
            part0 = got[pl.ds(xh, DEVICES, stride=BACK_ROWS), :]
            part1 = got[pl.ds(8 + xh, DEVICES, stride=BACK_ROWS), :]
            new0, new1 = swapped_parts(part0, part1)
            part0 = jnp.where(first_row, new0, part0)
            part1 = jnp.where(first_row, new1, part1)
            rows.append(jnp.concatenate([part0.T, part1.T], 1))
        values = jnp.exp(product3(split(jnp.concatenate(rows, 0)), table))
        for at in range(2):
            xh = 2 * pair + at
            for f in range(2):
                first = values[at * 128 + f * 32 : at * 128 + f * 32 + 32]
                second = values[at * 128 + 64 + f * 32 : at * 128 + 64 + f * 32 + 32]
                base = f * 512 + xh * 64
                modulus[base : base + 32, :] = first
                modulus[base + 32 : base + 64, :] = second
                both = first + second
                sums[0, f * 256 + xh * 32 : f * 256 + xh * 32 + 32, :] = both[:, :128]
                sums[1, f * 256 + xh * 32 : f * 256 + xh * 32 + 32, :] = both[:, 128:]
    one = jnp.zeros((256, 128), F32)
    for half in range(2):
        cells = sums[half, pl.ds(0, 256, stride=2), :] + sums[half, pl.ds(1, 256, stride=2), :]
        weights = mean1[half * 128 : half * 128 + 128, :]
        h, l = split(cells)
        one = one + (product(h, weights) + product(l, weights))
    for p in range(N_PY):
        route[p * ROUTE_ROWS : p * ROUTE_ROWS + 16, :] = one[p * 16 : p * 16 + 16]
    for k in range(8):
        sums2[k * 16 : k * 16 + 16, :] = one[k * 32 : k * 32 + 16] + one[k * 32 + 16 : k * 32 + 32]
    h, l = split(sums2[pl.ds(0, 64, stride=2), :] + sums2[pl.ds(1, 64, stride=2), :])
    two = product(h, mean2[...]) + product(l, mean2[...])
    sums2[0:64, :] = two
    for i in range(4):
        route[pl.ds(16 + i, N_PY, stride=ROUTE_ROWS), :] = sums2[pl.ds(i, N_PY, stride=4), :]
    for k in range(4):
        sums3[k * 8 : k * 8 + 8, :] = two[k * 16 : k * 16 + 8] + two[k * 16 + 8 : k * 16 + 16]
    h, l = split(sums3[pl.ds(0, 16, stride=2), :] + sums3[pl.ds(1, 16, stride=2), :])
    route[pl.ds(20, N_PY, stride=ROUTE_ROWS), :] = product(h, mean3[...]) + product(l, mean3[...])
    for i in range(3):
        route[pl.ds(21 + i, N_PY, stride=ROUTE_ROWS), :] = jnp.zeros((N_PY, 128), F32)


def pick_kernel(table, got, out):
    for g in range(N_PY):
        out[g, 0:16, :] = got[table[0, g], 0:16, :]
        out[g, 16:20, :] = got[table[1, g], 16:20, :]
        out[g, 20:24, :] = got[table[2, g], 20:24, :]


def unpack_kernel(got, one, two, three):
    for p in range(N_PY):
        one[p * 16 : p * 16 + 16, :] = got[p, 0:16, :]
        two[p * 4 : p * 4 + 4, :] = got[p, 16:20, 0:64]
        three[p : p + 1, :] = got[p, 20:21, 0:32]


def call(body, name, outs, *operands, scratch=(), **options):
    return pl.pallas_call(
        body,
        out_shape=[jax.ShapeDtypeStruct(s, F32) for s in outs],
        scratch_shapes=list(scratch),
        name=name,
        **options,
    )(*operands)


def on_device(white_noise, spectrum, group_table):
    tables = {k: tuple(jnp.asarray(t) for t in v) for k, v in make_tables().items()}
    noise = white_noise.reshape(1024, NZ)
    (sent,) = call(
        into_kernel,
        "into_z",
        [(DEVICES * SEND_ROWS, 128)],
        noise,
        spectrum.reshape(512, NZ),
        *tables["into"],
    )
    got = lax.all_to_all(sent.reshape(DEVICES, SEND_ROWS, 128), ("px", "py"), 0, 0, tiled=True)
    (restored,) = call(
        middle_kernel,
        "planes",
        [(DEVICES * BACK_ROWS, 128)],
        got.reshape(DEVICES * SEND_ROWS, 128),
        *tables["cos_y"],
        *tables["sin_y"],
        *tables["x_into"],
        *tables["x_back"],
        scratch=(pltpu.VMEM((512, 512), BF16), pltpu.VMEM((512, 512), BF16), pltpu.VMEM((256, 512), F32)),
    )
    back = lax.all_to_all(restored.reshape(DEVICES, BACK_ROWS, 128), ("px", "py"), 0, 0, tiled=True)
    modulus, route = call(
        last_kernel,
        "back_z",
        [(1024, NZ), (N_PY * ROUTE_ROWS, 128)],
        back.reshape(DEVICES * BACK_ROWS, 128),
        *tables["back"],
        jnp.asarray(pair_mean(256)[:, :128]),
        jnp.asarray(pair_mean(128)),
        jnp.asarray(pair_mean(128) * (np.arange(128) < 64)[:, None].astype(ml_dtypes.bfloat16)),
        scratch=(pltpu.VMEM((2, 512, 128), F32), pltpu.VMEM((128, 128), F32), pltpu.VMEM((32, 128), F32)),
    )
    spread = lax.all_to_all(route.reshape(N_PY, ROUTE_ROWS, 128), "py", 0, 0, tiled=True)
    vmem = pl.BlockSpec(memory_space=pltpu.VMEM)
    (picked,) = call(
        pick_kernel,
        "pick",
        [(N_PY, ROUTE_ROWS, 128)],
        group_table,
        spread,
        in_specs=[pl.BlockSpec(memory_space=pltpu.SMEM), vmem],
    )
    levels = lax.all_to_all(picked, "py", 0, 0, tiled=True)
    one, two, three = call(unpack_kernel, "unpack", [(256, 128), (64, 64), (16, 32)], levels)
    return (
        modulus.reshape(2, 16, 32, NZ),
        one.reshape(2, 8, 16, 128),
        two.reshape(2, 4, 8, 64),
        three.reshape(2, 2, 4, 32),
    )


def solution(mesh):
    block = P(None, "px", "py", None)
    return jax.shard_map(
        on_device,
        mesh=mesh,
        in_specs=(block, P("px", "py", None), P()),
        out_specs=(block, block, block, block),
        check_vma=False,
    )
```

time: 357 us -> 103 us (0.29); the launches traced: 351 us -> 102 us
  local copies, waits for them, and re-layouts: 152 us -> 0 us
  matrix products: 77.3 us -> 0 us
  waiting for transfers between devices: 58.9 us -> 0 us
  blocking collectives: 27.5 us -> 83.1 us
  Pallas kernels: 0 us -> 18.7 us
  between operations: 16.9 us -> 0.63 us
  starting transfers between devices: 11.7 us -> 0 us
  other arithmetic: 6.3 us -> 0 us
    concatenate x6 -> x0, local copies, waits for them, and re-layouts: 113 us -> none  [the longest x5 111 us: complex_apply(): return jnp.concatenate([real_cos - imag_sin, imag_cos + real_sin], 0)]
    dot_general x24 -> x0, matrix products: 77.3 us -> none  [the longest x6 20 us: complex_apply(): jnp.einsum(pattern, real_part, table_cos, precision=lax.Precision.HIGHEST)]
    all_to_all x2 -> x4, blocking collectives: 27.5 us -> 83.1 us  [the longest x1 35.6 us: on_device(): lax.all_to_all(sent.reshape(DEVICES, SEND_ROWS, 128), ('px', 'py'), 0, 0,...]
    all_gather x1 -> x0, waiting for transfers between devices: 29.5 us -> none  [gather_together(): lines, at, gathered = (lax.all_gather(line, axis), 0, [])]
    all_to_all x1 -> x0, waiting for transfers between devices: 29.4 us -> none  [forward(): lax.all_to_all(flat, PX_PY, split_axis=1, concat_axis=2, tiled=True)]
    pallas_call x0 -> x5, Pallas kernels: none -> 18.7 us  [call(): pl.pallas_call(body, out_shape=[jax.ShapeDtypeStruct(s, F32) for s in out...]
    all_to_all x1 -> x0, starting transfers between devices: 11.5 us -> none  [forward(): lax.all_to_all(flat, PX_PY, split_axis=1, concat_axis=2, tiled=True)]
    div x4 -> x0, local copies, waits for them, and re-layouts: 11 us -> none  [coarsen(): return blocks.mean(axis=(2, 4, 6))]
  transfers between devices with their start and end apart: 2 -> 0, of which waited for: 2 -> 0; matrix products, arithmetic and copies ran while one was open for 0% -> 0% of each run, Pallas kernels for 0% -> 0%
where the time goes in v1:
time: 103 us; the launch traced here: 102 us
  blocking collectives  83.1 us (81%)
  Pallas kernels  18.7 us (18%)
    all_to_all x1, blocking collectives, on_device(): lax.all_to_all(sent.reshape(DEVICES, SEND_ROWS, 128), ('px', 'py'), 0, 0,...  35.6 us
    all_to_all x1, blocking collectives, on_device(): lax.all_to_all(restored.reshape(DEVICES, BACK_ROWS, 128), ('px', 'py'), 0...  24.7 us
    pallas_call x5, Pallas kernels, call(): pl.pallas_call(body, out_shape=[jax.ShapeDtypeStruct(s, F32) for s in out...  18.7 us
    all_to_all x1, blocking collectives, on_device(): lax.all_to_all(route.reshape(N_PY, ROUTE_ROWS, 128), 'py', 0, 0, tiled=True)  11.6 us
    all_to_all x1, blocking collectives, on_device(): levels = lax.all_to_all(picked, 'py', 0, 0, tiled=True)  11.2 us

profile of v1, /device:TPU:1, one launch (start us, length us, event | category | flops | bytes accessed | tf_op | source)
XLA Modules:
  0.0 102.4 jit_solution(4880431210553097879)
XLA Ops:
  0.6 3.3 %into_z.1 = f32[3072,128]{1,0:T(8,128)} custom-call(f32[1024,256]{1,0:T(8,128)} %bitcast.15, f32[512,256]{1,0:T(8,128)} %bitcast.16, bf16[256,256]{1,0:T(8,128)(2,1)} %constant.30.clone.t_high, bf16[256,256]{1,0:T(8,128)(2,1)} %constant.31.clone.t_low), custom_call_target="tpu_custom_call" | custom-call | tf_op jit(solution)/shard_map/into_z/pallas_call | solution.py:239
  4.0 35.6 %all_to_all.20 = f32[128,24,128]{2,1,0:T(8,128)} all-to-all(f32[128,24,128]{2,1,0:T(8,128)} %bitcast.12), channel_id=1, replica_groups=mesh['px'=8,'py'=16] {'px','py'}, dimensions={0} | all-to-all | bytes 3145728 | tf_op jit(solution)/shard_map/all_to_all | solution.py:259
  39.6 8.7 %planes.1 = f32[2048,128]{1,0:T(8,128)} custom-call(f32[3072,128]{1,0:T(8,128)} %bitcast.11, bf16[512,512]{1,0:T(8,128)(2,1)} %constant.34.clone.cy_high, bf16[512,512]{1,0:T(8,128)(2,1)} %constant.35.clone.cy_low, bf16[512,512]{1,0:T(8,128)(2,1)} %constant.36.clone.sy_high, bf16[512,512]{1,0:T(8,128)(2,1)} %constant.37.clone.sy_low, ...), custom_call_target="tpu_custom_call" | custom-call | tf_op jit(solution)/shard_map/planes/pallas_call | solution.py:239
  48.3 24.7 %all_to_all.21 = f32[128,16,128]{2,1,0:T(8,128)} all-to-all(f32[128,16,128]{2,1,0:T(8,128)} %bitcast.13), channel_id=1, replica_groups=mesh['px'=8,'py'=16] {'px','py'}, dimensions={0} | all-to-all | bytes 2097152 | tf_op jit(solution)/shard_map/all_to_all | solution.py:271
  73.0 3.4 %back_z.1 = (f32[1024,256]{1,0:T(8,128)}, f32[384,128]{1,0:T(8,128)}) custom-call(f32[2048,128]{1,0:T(8,128)} %bitcast.14, bf16[256,256]{1,0:T(8,128)(2,1)} %constant.32.clone.b_high, bf16[256,256]{1,0:T(8,128)(2,1)} %constant.33.clone.b_low, bf16[256,128]{1,0:T(8,128)(2,1)} %constant.42.clone.mean1, bf16[128,128]{1,0:T(8,128)(2,1)} %constant.43.clone.mean2, ...), custom_call_target="tpu_custom_call" | custom-call | tf_op jit(solution)/shard_map/back_z/pallas_call | solution.py:239
  76.4 11.6 %all_to_all.22.got = f32[16,24,128]{2,1,0:T(8,128)} all-to-all(f32[16,24,128]{2,1,0:T(8,128)} %bitcast.17), channel_id=1, replica_groups=mesh['px'=8,'py'=16] {'py'}, dimensions={0} | all-to-all | bytes 393216 | tf_op jit(solution)/shard_map/all_to_all | solution.py:283
  87.9 1.7 %pick.1 = f32[16,24,128]{2,1,0:T(8,128)} custom-call(s32[3,16]{1,0:T(4,128)} %table.1, f32[16,24,128]{2,1,0:T(8,128)} %all_to_all.22.got), custom_call_target="tpu_custom_call" | custom-call | tf_op jit(solution)/shard_map/pick/pallas_call | solution.py:239
  89.6 11.2 %all_to_all.23.got = f32[16,24,128]{2,1,0:T(8,128)} all-to-all(f32[16,24,128]{2,1,0:T(8,128)} %pick.1), channel_id=1, replica_groups=mesh['px'=8,'py'=16] {'py'}, dimensions={0} | all-to-all | bytes 393216 | tf_op jit(solution)/shard_map/all_to_all | solution.py:293
  100.8 1.6 %unpack.1 = (f32[256,128]{1,0:T(8,128)}, f32[64,64]{1,0:T(8,128)}, f32[16,32]{1,0:T(8,128)}) custom-call(f32[16,24,128]{2,1,0:T(8,128)} %all_to_all.23.got), custom_call_target="tpu_custom_call" | custom-call | tf_op jit(solution)/shard_map/unpack/pallas_call | solution.py:239

commit v2 on v1

--- a/solution.py
+++ b/solution.py
@@ -15,8 +15,11 @@
 SEND_ROWS = 24
 BACK_ROWS = 16
 ROUTE_ROWS = 24
+VMEM_BYTES = 24 << 20
 F32 = jnp.float32
 BF16 = jnp.bfloat16
+NEAR = pl.BlockSpec(memory_space=pltpu.VMEM)
+FAR = pl.BlockSpec(memory_space=pltpu.HBM)
 
 
 def halves(table):
@@ -35,9 +38,6 @@
     cos_z, sin_z = angle_tables(d, z, NZ)
     alternating = (1.0 - 2.0 * (z % 2))[None, :]
     into = np.concatenate([cos_z, alternating, -sin_z[1:]], 0)
-    weight = np.where(d == 0, 1.0, 2.0)[:, None]
-    back = np.concatenate([weight * cos_z, alternating, -2.0 * sin_z[1:]], 0)
-    back = back * (0.5 / (NX * NY * NZ))
     y = np.arange(NY)
     cos_y, sin_y = angle_tables(y, y, NY)
     row = np.arange(NX)
@@ -48,7 +48,6 @@
     x_back = x_into.T
     return dict(
         into=halves(into),
-        back=halves(back),
         cos_y=halves(cos_y),
         sin_y=halves(sin_y),
         x_into=halves(x_into),
@@ -94,10 +93,22 @@
     return out
 
 
-def into_kernel(noise, spectrum, t_high, t_low, out):
+def into_kernel(noise_far, spectrum_far, high_far, low_far, out, noise, spectrum, t_high, t_low, arrived):
+    moves = [(high_far, t_high, 0, 256), (low_far, t_low, 0, 256)]
+    moves += [(noise_far, noise, f * 512 + pair * 128, 128) for pair in range(4) for f in range(2)]
+    moves += [(spectrum_far, spectrum, q * 128, 128) for q in range(4)]
+    copies = []
+    for far, near, at, count in moves:
+        rows = pl.ds(at, count)
+        copies.append(pltpu.make_async_copy(far.at[rows, :], near.at[rows, :], arrived.at[len(copies)]))
+        copies[-1].start()
+    copies[0].wait()
+    copies[1].wait()
     table = t_high[...], t_low[...]
     nt = (((1,), (1,)), ((), ()))
     for pair in range(4):
+        copies[2 + 2 * pair].wait()
+        copies[3 + 2 * pair].wait()
         starts = [f * 512 + (4 * pair + x) * 32 for x in range(4) for f in range(2)]
         block = jnp.concatenate([noise[s : s + 32, :] for s in starts], 0)
         made = product3(table, split(block), nt)
@@ -111,6 +122,7 @@
             out[xh : xh + 1, :] = new0[:1]
             out[8 + xh : 9 + xh, :] = new1[:1]
     for q in range(4):
+        copies[10 + q].wait()
         rows = spectrum[q * 128 : q * 128 + 128, :]
         plane = rows[:, :128].T
         out[pl.ds(16 + q, DEVICES, stride=SEND_ROWS), :] = plane
@@ -151,7 +163,7 @@
         by_sin = product3(values, sin_y)
         along_y = jnp.concatenate([by_cos[:128] + by_sin[128:], by_cos[128:] - by_sin[:128]], 0)
         along_x = product3(x_into, split(along_y))
-        s = scale[f * 128 : f * 128 + 128, :]
+        s = scale[f * 128 : f * 128 + 128, :] * (1.0 / (NX * NY * NZ))
         scaled = jnp.concatenate([along_x[:128] * s, along_x[128:] * s], 0)
         values = split(product3(x_back, split(scaled)))
         high[rows, :] = values[0]
@@ -173,7 +185,8 @@
                     out[at : at + 8, :] = block[px * 8 : px * 8 + 8]
 
 
-def last_kernel(got, b_high, b_low, mean1, mean2, mean3, modulus, route, sums, sums2, sums3):
+def last_kernel(got, b_high, b_low, mean1, mean2, mean3, modulus_far, route, sums, sums2, sums3, modulus, left):
+    copies = []
     table = b_high[...], b_low[...]
     first_row = lax.broadcasted_iota(jnp.int32, (128, 128), 0) == 0
     for pair in range(4):
@@ -183,8 +196,8 @@
             part0 = got[pl.ds(xh, DEVICES, stride=BACK_ROWS), :]
             part1 = got[pl.ds(8 + xh, DEVICES, stride=BACK_ROWS), :]
             new0, new1 = swapped_parts(part0, part1)
-            part0 = jnp.where(first_row, new0, part0)
-            part1 = jnp.where(first_row, new1, part1)
+            part0 = jnp.where(first_row, 0.5 * new0, part0)
+            part1 = jnp.where(first_row, 0.5 * new1, part1)
             rows.append(jnp.concatenate([part0.T, part1.T], 1))
         values = jnp.exp(product3(split(jnp.concatenate(rows, 0)), table))
         for at in range(2):
@@ -198,6 +211,10 @@
                 both = first + second
                 sums[0, f * 256 + xh * 32 : f * 256 + xh * 32 + 32, :] = both[:, :128]
                 sums[1, f * 256 + xh * 32 : f * 256 + xh * 32 + 32, :] = both[:, 128:]
+        for f in range(2):
+            rows = pl.ds(f * 512 + pair * 128, 128)
+            copies.append(pltpu.make_async_copy(modulus.at[rows, :], modulus_far.at[rows, :], left.at[len(copies)]))
+            copies[-1].start()
     one = jnp.zeros((256, 128), F32)
     for half in range(2):
         cells = sums[half, pl.ds(0, 256, stride=2), :] + sums[half, pl.ds(1, 256, stride=2), :]
@@ -219,6 +236,8 @@
     route[pl.ds(20, N_PY, stride=ROUTE_ROWS), :] = product(h, mean3[...]) + product(l, mean3[...])
     for i in range(3):
         route[pl.ds(21 + i, N_PY, stride=ROUTE_ROWS), :] = jnp.zeros((N_PY, 128), F32)
+    for copy in copies:
+        copy.wait()
 
 
 def pick_kernel(table, got, out):
@@ -235,33 +254,49 @@
         three[p : p + 1, :] = got[p, 20:21, 0:32]
 
 
+def on_chip(x):
+    return pltpu.with_memory_space_constraint(x, pltpu.VMEM)
+
+
+def off_chip(x):
+    return pltpu.with_memory_space_constraint(x, pltpu.HBM)
+
+
 def call(body, name, outs, *operands, scratch=(), **options):
     return pl.pallas_call(
         body,
-        out_shape=[jax.ShapeDtypeStruct(s, F32) for s in outs],
+        out_shape=outs,
         scratch_shapes=list(scratch),
         name=name,
+        compiler_params=pltpu.CompilerParams(vmem_limit_bytes=VMEM_BYTES),
         **options,
     )(*operands)
 
 
 def on_device(white_noise, spectrum, group_table):
-    tables = {k: tuple(jnp.asarray(t) for t in v) for k, v in make_tables().items()}
+    far = {k: tuple(jnp.asarray(t) for t in v) for k, v in make_tables().items()}
+    tables = {k: tuple(on_chip(t) for t in v) for k, v in far.items()}
     noise = white_noise.reshape(1024, NZ)
     (sent,) = call(
         into_kernel,
         "into_z",
-        [(DEVICES * SEND_ROWS, 128)],
-        noise,
-        spectrum.reshape(512, NZ),
-        *tables["into"],
+        [pltpu.VMEM((DEVICES * SEND_ROWS, 128), F32)],
+        *(off_chip(a) for a in (noise, spectrum.reshape(512, NZ), *far["into"])),
+        in_specs=[FAR] * 4,
+        scratch=(
+            pltpu.VMEM((1024, NZ), F32),
+            pltpu.VMEM((512, NZ), F32),
+            pltpu.VMEM((256, NZ), BF16),
+            pltpu.VMEM((256, NZ), BF16),
+            pltpu.SemaphoreType.DMA((14,)),
+        ),
     )
     got = lax.all_to_all(sent.reshape(DEVICES, SEND_ROWS, 128), ("px", "py"), 0, 0, tiled=True)
     (restored,) = call(
         middle_kernel,
         "planes",
-        [(DEVICES * BACK_ROWS, 128)],
-        got.reshape(DEVICES * SEND_ROWS, 128),
+        [pltpu.VMEM((DEVICES * BACK_ROWS, 128), F32)],
+        on_chip(got.reshape(DEVICES * SEND_ROWS, 128)),
         *tables["cos_y"],
         *tables["sin_y"],
         *tables["x_into"],
@@ -272,26 +307,32 @@
     modulus, route = call(
         last_kernel,
         "back_z",
-        [(1024, NZ), (N_PY * ROUTE_ROWS, 128)],
-        back.reshape(DEVICES * BACK_ROWS, 128),
-        *tables["back"],
+        [jax.ShapeDtypeStruct((1024, NZ), F32), pltpu.VMEM((N_PY * ROUTE_ROWS, 128), F32)],
+        on_chip(back.reshape(DEVICES * BACK_ROWS, 128)),
+        *tables["into"],
         jnp.asarray(pair_mean(256)[:, :128]),
         jnp.asarray(pair_mean(128)),
         jnp.asarray(pair_mean(128) * (np.arange(128) < 64)[:, None].astype(ml_dtypes.bfloat16)),
-        scratch=(pltpu.VMEM((2, 512, 128), F32), pltpu.VMEM((128, 128), F32), pltpu.VMEM((32, 128), F32)),
+        out_specs=[FAR, NEAR],
+        scratch=(
+            pltpu.VMEM((2, 512, 128), F32),
+            pltpu.VMEM((128, 128), F32),
+            pltpu.VMEM((32, 128), F32),
+            pltpu.VMEM((1024, NZ), F32),
+            pltpu.SemaphoreType.DMA((8,)),
+        ),
     )
     spread = lax.all_to_all(route.reshape(N_PY, ROUTE_ROWS, 128), "py", 0, 0, tiled=True)
-    vmem = pl.BlockSpec(memory_space=pltpu.VMEM)
     (picked,) = call(
         pick_kernel,
         "pick",
-        [(N_PY, ROUTE_ROWS, 128)],
+        [pltpu.VMEM((N_PY, ROUTE_ROWS, 128), F32)],
         group_table,
-        spread,
-        in_specs=[pl.BlockSpec(memory_space=pltpu.SMEM), vmem],
+        on_chip(spread),
+        in_specs=[pl.BlockSpec(memory_space=pltpu.SMEM), NEAR],
     )
     levels = lax.all_to_all(picked, "py", 0, 0, tiled=True)
-    one, two, three = call(unpack_kernel, "unpack", [(256, 128), (64, 64), (16, 32)], levels)
+    one, two, three = call(unpack_kernel, "unpack", [jax.ShapeDtypeStruct(s, F32) for s in ((256, 128), (64, 64), (16, 32))], on_chip(levels))
     return (
         modulus.reshape(2, 16, 32, NZ),
         one.reshape(2, 8, 16, 128),

time: 103 us -> 92.3 us (0.90)
  Pallas kernels: 18.7 us -> 11.8 us
  blocking collectives: 83.1 us -> 79.3 us
    pallas_call x5, Pallas kernels: 18.7 us -> 11.8 us  [call(): pl.pallas_call(body, out_shape=outs, scratch_shapes=list(scratch), name=n...]
    all_to_all x1, blocking collectives: 11.2 us -> 9.63 us  [on_device(): levels = lax.all_to_all(picked, 'py', 0, 0, tiled=True)]
    all_to_all x1, blocking collectives: 11.6 us -> 10.1 us  [on_device(): lax.all_to_all(route.reshape(N_PY, ROUTE_ROWS, 128), 'py', 0, 0, tiled=True)]
where the time goes in v2:
time: 92.3 us; the launch traced here: 92.1 us
  blocking collectives  79.3 us (86%)
  Pallas kernels  11.8 us (13%)
    all_to_all x1, blocking collectives, on_device(): lax.all_to_all(sent.reshape(DEVICES, SEND_ROWS, 128), ('px', 'py'), 0, 0,...  35.3 us
    all_to_all x1, blocking collectives, on_device(): lax.all_to_all(restored.reshape(DEVICES, BACK_ROWS, 128), ('px', 'py'), 0...  24.2 us
    pallas_call x5, Pallas kernels, call(): pl.pallas_call(body, out_shape=outs, scratch_shapes=list(scratch), name=n...  11.8 us
    all_to_all x1, blocking collectives, on_device(): lax.all_to_all(route.reshape(N_PY, ROUTE_ROWS, 128), 'py', 0, 0, tiled=True)  10.1 us
    all_to_all x1, blocking collectives, on_device(): levels = lax.all_to_all(picked, 'py', 0, 0, tiled=True)  9.63 us

profile of v2, /device:TPU:1, one launch (start us, length us, event | category | flops | bytes accessed | tf_op | source)
XLA Modules:
  0.0 92.1 jit_solution(11734011649353222031)
XLA Ops:
  0.6 3.3 %into_z.1 = f32[3072,128]{1,0:T(8,128)S(1)} custom-call(f32[1024,256]{1,0:T(8,128)} %bitcast.16, f32[512,256]{1,0:T(8,128)} %bitcast.17, bf16[256,256]{1,0:T(8,128)(2,1)} %constant.26.clone.high_far.b_high, bf16[256,256]{1,0:T(8,128)(2,1)} %constant.27.clone.low_far.b_low), custom_call_target="tpu_custom_call" | custom-call | tf_op jit(solution)/shard_map/into_z/pallas_call | solution.py:266
  4.0 0.0 copy-start
  4.0 0.0 copy-start.1
  4.0 0.0 copy-start.2
  4.0 0.0 copy-start.3
  4.0 0.0 copy-start.6
  4.0 0.0 copy-start.7
  4.0 0.0 copy-start.8
  4.1 0.0 copy-start.9
  4.1 35.3 %all_to_all.20 = f32[128,24,128]{2,1,0:T(8,128)S(1)} all-to-all(f32[128,24,128]{2,1,0:T(8,128)S(1)} %bitcast.12), channel_id=1, replica_groups=mesh['px'=8,'py'=16] {'px','py'}, dimensions={0} | all-to-all | bytes 3145728 | tf_op jit(solution)/shard_map/all_to_all | solution.py:294
  39.4 0.0 copy-done
  39.4 0.0 copy-done.1
  39.4 0.0 copy-done.2
  39.4 0.0 copy-done.3
  39.4 0.0 copy-done.6
  39.4 0.0 copy-done.7
  39.4 0.0 copy-done.8
  39.4 0.0 copy-done.9
  39.4 5.6 %planes.1 = f32[2048,128]{1,0:T(8,128)S(1)} custom-call(f32[3072,128]{1,0:T(8,128)S(1)} %bitcast.11, bf16[512,512]{1,0:T(8,128)(2,1)S(1)} %copy-done.3, bf16[512,512]{1,0:T(8,128)(2,1)S(1)} %copy-done.2, bf16[512,512]{1,0:T(8,128)(2,1)S(1)} %copy-done.1, bf16[512,512]{1,0:T(8,128)(2,1)S(1)} %copy-done, bf16[256,256]{1,0:T(8,128)(2,1)S(1)} %copy-done.9, ...), custom_call_target="tpu_custom_call" | custom-call | tf_op jit(solution)/shard_map/planes/pallas_call | solution.py:266
  45.0 0.0 copy-start.4
  45.1 0.0 copy-start.5
  45.1 0.0 copy-start.10
  45.1 0.0 copy-start.11
  45.1 0.0 copy-start.12
  45.1 0.0 copy-start.13
  45.1 24.2 %all_to_all.21 = f32[128,16,128]{2,1,0:T(8,128)S(1)} all-to-all(f32[128,16,128]{2,1,0:T(8,128)S(1)} %bitcast.13), channel_id=1, replica_groups=mesh['px'=8,'py'=16] {'px','py'}, dimensions={0} | all-to-all | bytes 2097152 | tf_op jit(solution)/shard_map/all_to_all | solution.py:306
  69.4 0.0 copy-done.4
  69.4 0.0 copy-done.5
  69.4 0.0 copy-done.10
  69.4 0.0 copy-done.11
  69.4 0.0 copy-done.12
  69.4 1.6 %back_z.1 = (f32[1024,256]{1,0:T(8,128)}, f32[384,128]{1,0:T(8,128)S(1)}) custom-call(f32[2048,128]{1,0:T(8,128)S(1)} %bitcast.14, bf16[256,256]{1,0:T(8,128)(2,1)S(1)} %copy-done.5, bf16[256,256]{1,0:T(8,128)(2,1)S(1)} %copy-done.4, bf16[256,128]{1,0:T(8,128)(2,1)S(1)} %copy-done.10, bf16[128,128]{1,0:T(8,128)(2,1)S(1)} %copy-done.12, ...), custom_call_target="tpu_custom_call" | custom-call | tf_op jit(solution)/shard_map/back_z/pallas_call | solution.py:266
  71.0 10.1 %all_to_all.22.got = f32[16,24,128]{2,1,0:T(8,128)S(1)} all-to-all(f32[16,24,128]{2,1,0:T(8,128)S(1)} %bitcast.15), channel_id=1, replica_groups=mesh['px'=8,'py'=16] {'py'}, dimensions={0} | all-to-all | bytes 393216 | tf_op jit(solution)/shard_map/all_to_all | solution.py:325
  81.1 0.0 copy-done.13
  81.1 0.6 pick.1
  81.8 9.6 %all_to_all.23.got = f32[16,24,128]{2,1,0:T(8,128)S(1)} all-to-all(f32[16,24,128]{2,1,0:T(8,128)S(1)} %pick.1), channel_id=1, replica_groups=mesh['px'=8,'py'=16] {'py'}, dimensions={0} | all-to-all | bytes 393216 | tf_op jit(solution)/shard_map/all_to_all | solution.py:334
  91.4 0.7 unpack.1
Async XLA Ops:
  4.0 35.4 %copy-start = (bf16[512,512]{1,0:T(8,128)(2,1)S(1)}, bf16[512,512]{1,0:T(8,128)(2,1)}, u32[]{:S(2)}) copy-start(bf16[512,512]{1,0:T(8,128)(2,1)} %constant.31.clone.sy_low) | copy-start | bytes 1572868
  4.0 35.4 %copy-start.1 = (bf16[512,512]{1,0:T(8,128)(2,1)S(1)}, bf16[512,512]{1,0:T(8,128)(2,1)}, u32[]{:S(2)}) copy-start(bf16[512,512]{1,0:T(8,128)(2,1)} %constant.30.clone.sy_high) | copy-start | bytes 1572868
  4.0 35.4 %copy-start.2 = (bf16[512,512]{1,0:T(8,128)(2,1)S(1)}, bf16[512,512]{1,0:T(8,128)(2,1)}, u32[]{:S(2)}) copy-start(bf16[512,512]{1,0:T(8,128)(2,1)} %constant.29.clone.cy_low) | copy-start | bytes 1572868
  4.0 35.4 %copy-start.3 = (bf16[512,512]{1,0:T(8,128)(2,1)S(1)}, bf16[512,512]{1,0:T(8,128)(2,1)}, u32[]{:S(2)}) copy-start(bf16[512,512]{1,0:T(8,128)(2,1)} %constant.28.clone.cy_high) | copy-start | bytes 1572868
  4.0 35.4 %copy-start.6 = (bf16[256,256]{1,0:T(8,128)(2,1)S(1)}, bf16[256,256]{1,0:T(8,128)(2,1)}, u32[]{:S(2)}) copy-start(bf16[256,256]{1,0:T(8,128)(2,1)} %constant.35.clone.xb_low) | copy-start | bytes 393220
  4.0 35.4 %copy-start.7 = (bf16[256,256]{1,0:T(8,128)(2,1)S(1)}, bf16[256,256]{1,0:T(8,128)(2,1)}, u32[]{:S(2)}) copy-start(bf16[256,256]{1,0:T(8,128)(2,1)} %constant.34.clone.xb_high) | copy-start | bytes 393220
  4.0 35.4 %copy-start.8 = (bf16[256,256]{1,0:T(8,128)(2,1)S(1)}, bf16[256,256]{1,0:T(8,128)(2,1)}, u32[]{:S(2)}) copy-start(bf16[256,256]{1,0:T(8,128)(2,1)} %constant.33.clone.xi_low) | copy-start | bytes 393220
  4.1 35.4 %copy-start.9 = (bf16[256,256]{1,0:T(8,128)(2,1)S(1)}, bf16[256,256]{1,0:T(8,128)(2,1)}, u32[]{:S(2)}) copy-start(bf16[256,256]{1,0:T(8,128)(2,1)} %constant.32.clone.xi_high) | copy-start | bytes 393220
  45.0 24.3 %copy-start.4 = (bf16[256,256]{1,0:T(8,128)(2,1)S(1)}, bf16[256,256]{1,0:T(8,128)(2,1)}, u32[]{:S(2)}) copy-start(bf16[256,256]{1,0:T(8,128)(2,1)} %constant.27.clone.low_far.b_low) | copy-start | bytes 393220
  45.1 24.3 %copy-start.5 = (bf16[256,256]{1,0:T(8,128)(2,1)S(1)}, bf16[256,256]{1,0:T(8,128)(2,1)}, u32[]{:S(2)}) copy-start(bf16[256,256]{1,0:T(8,128)(2,1)} %constant.26.clone.high_far.b_high) | copy-start | bytes 393220
  45.1 24.3 %copy-start.10 = (bf16[256,128]{1,0:T(8,128)(2,1)S(1)}, bf16[256,128]{1,0:T(8,128)(2,1)}, u32[]{:S(2)}) copy-start(bf16[256,128]{1,0:T(8,128)(2,1)} %constant.36.clone.mean1) | copy-start | bytes 196612
  45.1 24.3 %copy-start.11 = (bf16[128,128]{1,0:T(8,128)(2,1)S(1)}, bf16[128,128]{1,0:T(8,128)(2,1)}, u32[]{:S(2)}) copy-start(bf16[128,128]{1,0:T(8,128)(2,1)} %constant.38.clone.mean3) | copy-start | bytes 98308
  45.1 24.3 %copy-start.12 = (bf16[128,128]{1,0:T(8,128)(2,1)S(1)}, bf16[128,128]{1,0:T(8,128)(2,1)}, u32[]{:S(2)}) copy-start(bf16[128,128]{1,0:T(8,128)(2,1)} %constant.37.clone.mean2) | copy-start | bytes 98308
  45.1 36.0 %copy-start.13 = (s32[3,16]{1,0:T(4,128)S(1)}, s32[3,16]{1,0:T(4,128)}, u32[]{:S(2)}) copy-start(s32[3,16]{1,0:T(4,128)} %table.1) | copy-start | bytes 580

commit v3 on v2

--- a/solution.py
+++ b/solution.py
@@ -15,6 +15,7 @@
 SEND_ROWS = 24
 BACK_ROWS = 16
 ROUTE_ROWS = 24
+SCALE_ROWS = 136
 VMEM_BYTES = 24 << 20
 F32 = jnp.float32
 BF16 = jnp.bfloat16
@@ -38,20 +39,20 @@
     cos_z, sin_z = angle_tables(d, z, NZ)
     alternating = (1.0 - 2.0 * (z % 2))[None, :]
     into = np.concatenate([cos_z, alternating, -sin_z[1:]], 0)
-    y = np.arange(NY)
-    cos_y, sin_y = angle_tables(y, y, NY)
+    y, m = np.arange(NY // 4), np.arange(NY // 4)
+    along_y = []
+    for r in range(4):
+        cos_y, sin_y = angle_tables(y, 4 * m + r, NY)
+        along_y.append(np.block([[cos_y, -sin_y], [sin_y, cos_y]]))
     row = np.arange(NX)
-    x_of = (row // 8 % 8) * 16 + (row % 8) * 2 + row // 64
-    j_of = (row % 8) * 16 + (row // 8 % 4) * 4 + row // 32
-    cos_x, sin_x = angle_tables(j_of, x_of, NX)
+    x_of = (row // 16) * 16 + (row % 8) * 2 + row // 8 % 2
+    cos_x, sin_x = angle_tables(row, x_of, NX)
     x_into = np.block([[cos_x, sin_x], [-sin_x, cos_x]])
-    x_back = x_into.T
     return dict(
         into=halves(into),
-        cos_y=halves(cos_y),
-        sin_y=halves(sin_y),
-        x_into=halves(x_into),
-        x_back=halves(x_back),
+        along_y=halves(np.concatenate(along_y, 0)),
+        x_into=(np.concatenate(halves(x_into), 0),),
+        x_back=(np.concatenate(halves(x_into.T), 0),),
     )
 
 
@@ -81,27 +82,53 @@
 
 
 def blocks_transposed(parts):
-    lane = lax.broadcasted_iota(jnp.int32, parts[0].shape, 1)
-    low, even = lane < 64, lane // 32 % 2 == 0
-    a, b, c, d = parts
-    ac = jnp.where(low, a, pltpu.roll(c, 64, 1)), jnp.where(low, pltpu.roll(a, 64, 1), c)
-    bd = jnp.where(low, b, pltpu.roll(d, 64, 1)), jnp.where(low, pltpu.roll(b, 64, 1), d)
-    out = []
-    for u, v in zip(ac, bd):
-        out.append(jnp.where(even, u, pltpu.roll(v, 32, 1)))
-        out.append(jnp.where(even, pltpu.roll(u, 96, 1), v))
-    return out
+    parts = list(parts)
+    width = 128 // len(parts)
+    lane = lax.broadcasted_iota(jnp.int32, parts[0].shape, 1) // width
+    step = len(parts) // 2
+    while step:
+        stays = lane // step % 2 == 0
+        for i in range(len(parts)):
+            if i // step % 2 == 0:
+                a, b = parts[i], parts[i + step]
+                parts[i] = jnp.where(stays, a, pltpu.roll(b, step * width, 1))
+                parts[i + step] = jnp.where(stays, pltpu.roll(a, 128 - step * width, 1), b)
+        step //= 2
+    return parts
+
+
+def quarters(values, sign):
+    (ar, ai), (br, bi), (cr, ci), (dr, di) = values
+    sr, si, tr, ti = ar + cr, ai + ci, br + dr, bi + di
+    ur, ui, vr, vi = ar - cr, ai - ci, sign * (br - dr), sign * (bi - di)
+    return [(sr + tr, si + ti), (ur - vi, ui + vr), (sr - tr, si - ti), (ur + vi, ui - vr)]
+
+
+def left_product(table, values):
+    high, low = split(values)
+    count = table.shape[0] // 2
+    both = product(table, high)
+    return both[:count] + both[count:] + product(table[:count], low)
+
+
+def right_product(values, table_high, table_low, dims):
+    count = values.shape[0] // 2
+    both = product(values, table_high, dims)
+    return both[:count] + both[count:] + product(values[:count], table_low, dims)
 
 
 def into_kernel(noise_far, spectrum_far, high_far, low_far, out, noise, spectrum, t_high, t_low, arrived):
     moves = [(high_far, t_high, 0, 256), (low_far, t_low, 0, 256)]
     moves += [(noise_far, noise, f * 512 + pair * 128, 128) for pair in range(4) for f in range(2)]
-    moves += [(spectrum_far, spectrum, q * 128, 128) for q in range(4)]
     copies = []
     for far, near, at, count in moves:
         rows = pl.ds(at, count)
         copies.append(pltpu.make_async_copy(far.at[rows, :], near.at[rows, :], arrived.at[len(copies)]))
-        copies[-1].start()
+    for half in range(2):
+        columns = spectrum_far.at[:, pl.ds(half * 128, 128)]
+        copies.append(pltpu.make_async_copy(columns, spectrum.at[half], arrived.at[len(copies)]))
+    for copy in copies:
+        copy.start()
     copies[0].wait()
     copies[1].wait()
     table = t_high[...], t_low[...]
@@ -121,68 +148,68 @@
             new0, new1 = swapped_parts(part0[:8], part1[:8])
             out[xh : xh + 1, :] = new0[:1]
             out[8 + xh : 9 + xh, :] = new1[:1]
-    for q in range(4):
-        copies[10 + q].wait()
-        rows = spectrum[q * 128 : q * 128 + 128, :]
-        plane = rows[:, :128].T
-        out[pl.ds(16 + q, DEVICES, stride=SEND_ROWS), :] = plane
-        out[pl.ds(20 + q, DEVICES, stride=SEND_ROWS), :] = plane
-        out[20 + q : 21 + q, :] = rows[:, 128:].T[:1]
-
-
-def middle_kernel(got, cy_high, cy_low, sy_high, sy_low, xi_high, xi_low, xb_high, xb_low, out, high, low, scale):
-    cos_y = cy_high[...], cy_low[...]
-    sin_y = sy_high[...], sy_low[...]
-    x_into = xi_high[...], xi_low[...]
-    x_back = xb_high[...], xb_low[...]
-    for q in range(4):
-        lanes = slice(q * 128, q * 128 + 128)
-        for part in range(2):
-            pieces = []
-            for i in range(4):
-                at = [(px * N_PY + 4 * q + i) * SEND_ROWS + 8 * part for px in range(N_PX)]
-                pieces.append(jnp.concatenate([got[s : s + 8, :] for s in at], 0))
-            for b, block in enumerate(blocks_transposed(pieces)):
-                xl, f = b // 2, b % 2
-                row = f * 256 + part * 128 + xl * 64
-                h, l = split(block)
-                high[row : row + 64, lanes] = h
-                low[row : row + 64, lanes] = l
+    copies[10].wait()
+    copies[11].wait()
+    for r in range(4):
+        plane = spectrum[0, pl.ds(r, 128, stride=4), :].T
+        out[pl.ds(16 + r, DEVICES, stride=SEND_ROWS), :] = plane
+        out[pl.ds(20 + r, DEVICES, stride=SEND_ROWS), :] = plane
+        out[20 + r : 21 + r, :] = spectrum[1, pl.ds(r, 128, stride=4), :].T[:1]
+
+
+def middle_kernel(got, y_high, y_low, x_into, x_back, out, left, scale):
+    plain, turned = (((1,), (0,)), ((), ())), (((1,), (1,)), ((), ()))
+    for px in range(N_PX):
+        pieces = [got[(px * N_PY + i) * SEND_ROWS + 16 : (px * N_PY + i) * SEND_ROWS + 24, :] for i in range(N_PY)]
+        for j, block in enumerate(blocks_transposed(pieces)):
+            scale[pl.ds(px * 16 + j, 8, stride=SCALE_ROWS), :] = block
+    for px in range(N_PX):
+        blocks = []
+        for q in range(4):
+            at = [(px * N_PY + 4 * q + i) * SEND_ROWS for i in range(4)]
+            parts = [blocks_transposed([got[s + 8 * part : s + 8 * part + 8, :] for s in at]) for part in range(2)]
+            blocks.append(parts)
         for f in range(2):
-            pieces = []
-            for i in range(4):
-                at = [(4 * q + i) * SEND_ROWS + 16 + 4 * f + r for r in range(4)]
-                step = N_PY * SEND_ROWS
-                pieces.append(jnp.concatenate([got[pl.ds(s, N_PX, stride=step), :] for s in at], 0))
-            for b, block in enumerate(blocks_transposed(pieces)):
-                scale[f * 128 + b * 32 : f * 128 + b * 32 + 32, lanes] = block
+            pair = []
+            for xl in range(2):
+                b = 2 * xl + f
+                pair.append(quarters([(blocks[q][0][b], blocks[q][1][b]) for q in range(4)], -1.0))
+            row = f * 128 + px * 16
+            for r in range(4):
+                for part in range(2):
+                    high, low = split(jnp.concatenate([pair[0][r][part], pair[1][r][part]], 0))
+                    left[r, row : row + 16, part * 128 : part * 128 + 128] = high
+                    left[r, 256 + row : 272 + row, part * 128 : part * 128 + 128] = low
+    along_y = []
+    for r in range(4):
+        rows = slice(r * 256, r * 256 + 256)
+        along_y.append(right_product(left[r], y_high[rows, :], y_low[rows, :], plain))
+    restored = []
     for f in range(2):
-        rows = slice(f * 256, f * 256 + 256)
-        values = high[rows, :], low[rows, :]
-        by_cos = product3(values, cos_y)
-        by_sin = product3(values, sin_y)
-        along_y = jnp.concatenate([by_cos[:128] + by_sin[128:], by_cos[128:] - by_sin[:128]], 0)
-        along_x = product3(x_into, split(along_y))
-        s = scale[f * 128 : f * 128 + 128, :] * (1.0 / (NX * NY * NZ))
-        scaled = jnp.concatenate([along_x[:128] * s, along_x[128:] * s], 0)
-        values = split(product3(x_back, split(scaled)))
-        high[rows, :] = values[0]
-        low[rows, :] = values[1]
-    done = []
-    for f in range(2):
-        rows = slice(f * 256, f * 256 + 256)
-        values = high[rows, :], low[rows, :]
-        by_cos = product3(values, cos_y)
-        by_sin = product3(values, sin_y)
-        done.append((by_cos[:128] - by_sin[128:], by_cos[128:] + by_sin[:128]))
-    for q in range(4):
-        lanes = slice(q * 128, q * 128 + 128)
-        for part in range(2):
-            pieces = [done[b % 2][part][(b // 2) * 64 : (b // 2) * 64 + 64, lanes] for b in range(4)]
-            for i, block in enumerate(blocks_transposed(pieces)):
-                for px in range(N_PX):
+        rows = slice(f * 128, f * 128 + 128)
+        sides = [jnp.concatenate([a[rows, part * 128 : part * 128 + 128] for a in along_y], 1) for part in range(2)]
+        spectral = left_product(x_into[...], jnp.concatenate(sides, 0))
+        at = [(f * 4 + r) * SCALE_ROWS for r in range(4)]
+        s = jnp.concatenate([scale[k : k + 128, :] for k in at], 1) * (1.0 / (NX * NY * NZ))
+        scaled = jnp.concatenate([spectral[:128] * s, spectral[128:] * s], 0)
+        restored.append(left_product(x_back[...], scaled))
+    back = []
+    for r in range(4):
+        lanes = slice(r * 128, r * 128 + 128)
+        rows = [jnp.concatenate([z[:128, lanes], z[128:, lanes]], 1) for z in restored]
+        values = jnp.concatenate(split(jnp.concatenate(rows, 0)), 0)
+        at = slice(r * 256, r * 256 + 256)
+        back.append(right_product(values, y_high[at, :], y_low[at, :], turned))
+    for px in range(N_PX):
+        blocks = []
+        for b in range(4):
+            row = (b % 2) * 128 + px * 16 + (b // 2) * 8
+            blocks.append(quarters([(u[row : row + 8, :128], u[row : row + 8, 128:]) for u in back], 1.0))
+        for q in range(4):
+            for part in range(2):
+                for i, block in enumerate(blocks_transposed([blocks[b][q][part] for b in range(4)])):
                     at = (px * N_PY + 4 * q + i) * BACK_ROWS + 8 * part
-                    out[at : at + 8, :] = block[px * 8 : px * 8 + 8]
+                    out[at : at + 8, :] = block
 
 
 def last_kernel(got, b_high, b_low, mean1, mean2, mean3, modulus_far, route, sums, sums2, sums3, modulus, left):
@@ -285,10 +312,10 @@
         in_specs=[FAR] * 4,
         scratch=(
             pltpu.VMEM((1024, NZ), F32),
-            pltpu.VMEM((512, NZ), F32),
+            pltpu.VMEM((2, 512, 128), F32),
             pltpu.VMEM((256, NZ), BF16),
             pltpu.VMEM((256, NZ), BF16),
-            pltpu.SemaphoreType.DMA((14,)),
+            pltpu.SemaphoreType.DMA((12,)),
         ),
     )
     got = lax.all_to_all(sent.reshape(DEVICES, SEND_ROWS, 128), ("px", "py"), 0, 0, tiled=True)
@@ -297,11 +324,10 @@
         "planes",
         [pltpu.VMEM((DEVICES * BACK_ROWS, 128), F32)],
         on_chip(got.reshape(DEVICES * SEND_ROWS, 128)),
-        *tables["cos_y"],
-        *tables["sin_y"],
+        *tables["along_y"],
         *tables["x_into"],
         *tables["x_back"],
-        scratch=(pltpu.VMEM((512, 512), BF16), pltpu.VMEM((512, 512), BF16), pltpu.VMEM((256, 512), F32)),
+        scratch=(pltpu.VMEM((4, 512, 256), BF16), pltpu.VMEM((8 * SCALE_ROWS, 128), F32)),
     )
     back = lax.all_to_all(restored.reshape(DEVICES, BACK_ROWS, 128), ("px", "py"), 0, 0, tiled=True)
     modulus, route = call(

time: 92.3 us -> 89.7 us (0.972)
  Pallas kernels: 11.8 us -> 9.3 us
    pallas_call x5, Pallas kernels: 11.8 us -> 9.3 us  [call(): pl.pallas_call(body, out_shape=outs, scratch_shapes=list(scratch), name=n...]
where the time goes in v3:
time: 89.7 us; the launch traced here: 89.4 us
  blocking collectives  79.3 us (88%)
  Pallas kernels  9.3 us (10%)
    all_to_all x1, blocking collectives, on_device(): lax.all_to_all(sent.reshape(DEVICES, SEND_ROWS, 128), ('px', 'py'), 0, 0,...  35.3 us
    all_to_all x1, blocking collectives, on_device(): lax.all_to_all(restored.reshape(DEVICES, BACK_ROWS, 128), ('px', 'py'), 0...  24.2 us
    all_to_all x1, blocking collectives, on_device(): lax.all_to_all(route.reshape(N_PY, ROUTE_ROWS, 128), 'py', 0, 0, tiled=True)  10.1 us
    all_to_all x1, blocking collectives, on_device(): levels = lax.all_to_all(picked, 'py', 0, 0, tiled=True)  9.63 us
    pallas_call x5, Pallas kernels, call(): pl.pallas_call(body, out_shape=outs, scratch_shapes=list(scratch), name=n...  9.3 us

profile of v3, /device:TPU:1, one launch (start us, length us, event | category | flops | bytes accessed | tf_op | source)
XLA Modules:
  0.0 89.4 jit_solution(9665017157236853014)
XLA Ops:
  0.6 3.1 %into_z.1 = f32[3072,128]{1,0:T(8,128)S(1)} custom-call(f32[1024,256]{1,0:T(8,128)} %bitcast.16, f32[512,256]{1,0:T(8,128)} %bitcast.17, bf16[256,256]{1,0:T(8,128)(2,1)} %constant.18.clone.high_far.b_high, bf16[256,256]{1,0:T(8,128)(2,1)} %constant.19.clone.low_far.b_low), custom_call_target="tpu_custom_call" | custom-call | tf_op jit(solution)/shard_map/into_z/pallas_call | solution.py:293
  3.7 0.0 copy-start
  3.8 0.0 copy-start.1
  3.8 0.0 copy-start.4
  3.8 0.0 copy-start.5
  3.8 35.3 %all_to_all.20 = f32[128,24,128]{2,1,0:T(8,128)S(1)} all-to-all(f32[128,24,128]{2,1,0:T(8,128)S(1)} %bitcast.12), channel_id=1, replica_groups=mesh['px'=8,'py'=16] {'px','py'}, dimensions={0} | all-to-all | bytes 3145728 | tf_op jit(solution)/shard_map/all_to_all | solution.py:321
  39.1 0.0 copy-done
  39.1 0.0 copy-done.1
  39.1 0.0 copy-done.4
  39.1 0.0 copy-done.5
  39.1 3.3 %planes.1 = f32[2048,128]{1,0:T(8,128)S(1)} custom-call(f32[3072,128]{1,0:T(8,128)S(1)} %bitcast.11, bf16[1024,256]{1,0:T(8,128)(2,1)S(1)} %copy-done.1, bf16[1024,256]{1,0:T(8,128)(2,1)S(1)} %copy-done, bf16[512,256]{1,0:T(8,128)(2,1)S(1)} %copy-done.5, bf16[512,256]{1,0:T(8,128)(2,1)S(1)} %copy-done.4), custom_call_target="tpu_custom_call" | custom-call | tf_op jit(solution)/shard_map/planes/pallas_call | solution.py:293
  42.4 0.0 copy-start.2
  42.4 0.0 copy-start.3
  42.4 0.0 copy-start.6
  42.4 0.0 copy-start.7
  42.5 0.0 copy-start.8
  42.5 0.0 copy-start.9
  42.5 24.2 %all_to_all.21 = f32[128,16,128]{2,1,0:T(8,128)S(1)} all-to-all(f32[128,16,128]{2,1,0:T(8,128)S(1)} %bitcast.14), channel_id=1, replica_groups=mesh['px'=8,'py'=16] {'px','py'}, dimensions={0} | all-to-all | bytes 2097152 | tf_op jit(solution)/shard_map/all_to_all | solution.py:332
  66.7 0.0 copy-done.2
  66.7 0.0 copy-done.3
  66.7 0.0 copy-done.6
  66.7 0.0 copy-done.7
  66.7 0.0 copy-done.8
  66.7 1.6 %back_z.1 = (f32[1024,256]{1,0:T(8,128)}, f32[384,128]{1,0:T(8,128)S(1)}) custom-call(f32[2048,128]{1,0:T(8,128)S(1)} %bitcast.13, bf16[256,256]{1,0:T(8,128)(2,1)S(1)} %copy-done.3, bf16[256,256]{1,0:T(8,128)(2,1)S(1)} %copy-done.2, bf16[256,128]{1,0:T(8,128)(2,1)S(1)} %copy-done.6, bf16[128,128]{1,0:T(8,128)(2,1)S(1)} %copy-done.8, ...), custom_call_target="tpu_custom_call" | custom-call | tf_op jit(solution)/shard_map/back_z/pallas_call | solution.py:293
  68.4 10.1 %all_to_all.22.got = f32[16,24,128]{2,1,0:T(8,128)S(1)} all-to-all(f32[16,24,128]{2,1,0:T(8,128)S(1)} %bitcast.15), channel_id=1, replica_groups=mesh['px'=8,'py'=16] {'py'}, dimensions={0} | all-to-all | bytes 393216 | tf_op jit(solution)/shard_map/all_to_all | solution.py:351
  78.5 0.0 copy-done.9
  78.5 0.6 pick.1
  79.1 9.6 %all_to_all.23.got = f32[16,24,128]{2,1,0:T(8,128)S(1)} all-to-all(f32[16,24,128]{2,1,0:T(8,128)S(1)} %pick.1), channel_id=1, replica_groups=mesh['px'=8,'py'=16] {'py'}, dimensions={0} | all-to-all | bytes 393216 | tf_op jit(solution)/shard_map/all_to_all | solution.py:360
  88.7 0.7 unpack.1
Async XLA Ops:
  3.7 35.3 %copy-start = (bf16[1024,256]{1,0:T(8,128)(2,1)S(1)}, bf16[1024,256]{1,0:T(8,128)(2,1)}, u32[]{:S(2)}) copy-start(bf16[1024,256]{1,0:T(8,128)(2,1)} %constant.21.clone.y_low) | copy-start | bytes 1572868
  3.8 35.3 %copy-start.1 = (bf16[1024,256]{1,0:T(8,128)(2,1)S(1)}, bf16[1024,256]{1,0:T(8,128)(2,1)}, u32[]{:S(2)}) copy-start(bf16[1024,256]{1,0:T(8,128)(2,1)} %constant.20.clone.y_high) | copy-start | bytes 1572868
  3.8 35.3 %copy-start.4 = (bf16[512,256]{1,0:T(8,128)(2,1)S(1)}, bf16[512,256]{1,0:T(8,128)(2,1)}, u32[]{:S(2)}) copy-start(bf16[512,256]{1,0:T(8,128)(2,1)} %constant.23.clone.x_back) | copy-start | bytes 786436
  3.8 35.3 %copy-start.5 = (bf16[512,256]{1,0:T(8,128)(2,1)S(1)}, bf16[512,256]{1,0:T(8,128)(2,1)}, u32[]{:S(2)}) copy-start(bf16[512,256]{1,0:T(8,128)(2,1)} %constant.22.clone.x_into) | copy-start | bytes 786436
  42.4 24.3 %copy-start.2 = (bf16[256,256]{1,0:T(8,128)(2,1)S(1)}, bf16[256,256]{1,0:T(8,128)(2,1)}, u32[]{:S(2)}) copy-start(bf16[256,256]{1,0:T(8,128)(2,1)} %constant.19.clone.low_far.b_low) | copy-start | bytes 393220
  42.4 24.3 %copy-start.3 = (bf16[256,256]{1,0:T(8,128)(2,1)S(1)}, bf16[256,256]{1,0:T(8,128)(2,1)}, u32[]{:S(2)}) copy-start(bf16[256,256]{1,0:T(8,128)(2,1)} %constant.18.clone.high_far.b_high) | copy-start | bytes 393220
  42.4 24.3 %copy-start.6 = (bf16[256,128]{1,0:T(8,128)(2,1)S(1)}, bf16[256,128]{1,0:T(8,128)(2,1)}, u32[]{:S(2)}) copy-start(bf16[256,128]{1,0:T(8,128)(2,1)} %constant.24.clone.mean1) | copy-start | bytes 196612
  42.4 24.3 %copy-start.7 = (bf16[128,128]{1,0:T(8,128)(2,1)S(1)}, bf16[128,128]{1,0:T(8,128)(2,1)}, u32[]{:S(2)}) copy-start(bf16[128,128]{1,0:T(8,128)(2,1)} %constant.26.clone.mean3) | copy-start | bytes 98308
  42.5 24.3 %copy-start.8 = (bf16[128,128]{1,0:T(8,128)(2,1)S(1)}, bf16[128,128]{1,0:T(8,128)(2,1)}, u32[]{:S(2)}) copy-start(bf16[128,128]{1,0:T(8,128)(2,1)} %constant.25.clone.mean2) | copy-start | bytes 98308
  42.5 36.0 %copy-start.9 = (s32[3,16]{1,0:T(4,128)S(1)}, s32[3,16]{1,0:T(4,128)}, u32[]{:S(2)}) copy-start(s32[3,16]{1,0:T(4,128)} %table.1) | copy-start | bytes 580

commit v4 on v3

--- a/solution.py
+++ b/solution.py
@@ -12,7 +12,7 @@
 NX, NY, NZ = 128, 512, 256
 N_PX, N_PY = 8, 16
 DEVICES = N_PX * N_PY
-SEND_ROWS = 24
+SEND_ROWS = 21
 BACK_ROWS = 16
 ROUTE_ROWS = 24
 SCALE_ROWS = 136
@@ -119,7 +119,7 @@
 
 def into_kernel(noise_far, spectrum_far, high_far, low_far, out, noise, spectrum, t_high, t_low, arrived):
     moves = [(high_far, t_high, 0, 256), (low_far, t_low, 0, 256)]
-    moves += [(noise_far, noise, f * 512 + pair * 128, 128) for pair in range(4) for f in range(2)]
+    moves += [(noise_far, noise, quarter * 256, 256) for quarter in range(4)]
     copies = []
     for far, near, at, count in moves:
         rows = pl.ds(at, count)
@@ -129,13 +129,11 @@
         copies.append(pltpu.make_async_copy(columns, spectrum.at[half], arrived.at[len(copies)]))
     for copy in copies:
         copy.start()
-    copies[0].wait()
-    copies[1].wait()
+    for copy in copies[:6]:
+        copy.wait()
     table = t_high[...], t_low[...]
     nt = (((1,), (1,)), ((), ()))
     for pair in range(4):
-        copies[2 + 2 * pair].wait()
-        copies[3 + 2 * pair].wait()
         starts = [f * 512 + (4 * pair + x) * 32 for x in range(4) for f in range(2)]
         block = jnp.concatenate([noise[s : s + 32, :] for s in starts], 0)
         made = product3(table, split(block), nt)
@@ -148,26 +146,58 @@
             new0, new1 = swapped_parts(part0[:8], part1[:8])
             out[xh : xh + 1, :] = new0[:1]
             out[8 + xh : 9 + xh, :] = new1[:1]
-    copies[10].wait()
-    copies[11].wait()
+    for copy in copies[6:]:
+        copy.wait()
+    lower = lax.axis_index("py") < N_PY // 2
     for r in range(4):
         plane = spectrum[0, pl.ds(r, 128, stride=4), :].T
+        other = spectrum[1, pl.ds(r, 128, stride=4), :].T[:1]
         out[pl.ds(16 + r, DEVICES, stride=SEND_ROWS), :] = plane
-        out[pl.ds(20 + r, DEVICES, stride=SEND_ROWS), :] = plane
-        out[20 + r : 21 + r, :] = spectrum[1, pl.ds(r, 128, stride=4), :].T[:1]
+        out[16 + r : 17 + r, :] = jnp.where(lower, plane[:1], other)
+        if r == 0:
+            out[pl.ds(20, DEVICES, stride=SEND_ROWS), :] = plane
+            out[20:21, :] = jnp.where(lower, other, plane[:1])
+
+
+def unfold(scale):
+    row = lax.broadcasted_iota(jnp.int32, (128, 128), 0)
+    lane = lax.broadcasted_iota(jnp.int32, (128, 128), 1)
+    around = jnp.where((row + lane) % 128 == 0, 1.0, 0.0).astype(BF16)
+    mirrored = jnp.where(row + lane == 127, 1.0, 0.0).astype(BF16)
+    column = scale[7 * SCALE_ROWS : 7 * SCALE_ROWS + 128, :]
+    for r in range(4):
+        own = scale[(3 + r) * SCALE_ROWS : (3 + r) * SCALE_ROWS + 128, :]
+        at = (3 + (4 - r) % 4) * SCALE_ROWS
+        high, low = split(scale[at : at + 128, :])
+        turn = mirrored if r else around
+        sides = [product(product(around, part).astype(BF16), turn) for part in (high, low)]
+        partner = sides[0] + sides[1]
+        zero = jnp.where(lane < 64, own, partner)
+        half = jnp.where(lane < 64, partner, own)
+        if r == 0:
+            zero = jnp.where(lane == 64, column, zero)
+            half = jnp.where(lane == 0, column, half)
+        scale[(8 + r) * SCALE_ROWS : (8 + r) * SCALE_ROWS + 128, :] = zero
+        scale[(12 + r) * SCALE_ROWS : (12 + r) * SCALE_ROWS + 128, :] = half
 
 
 def middle_kernel(got, y_high, y_low, x_into, x_back, out, left, scale):
     plain, turned = (((1,), (0,)), ((), ())), (((1,), (1,)), ((), ()))
     for px in range(N_PX):
-        pieces = [got[(px * N_PY + i) * SEND_ROWS + 16 : (px * N_PY + i) * SEND_ROWS + 24, :] for i in range(N_PY)]
+        pieces = [got[pl.ds((px * N_PY + i) * SEND_ROWS + 13, 8), :] for i in range(N_PY)]
         for j, block in enumerate(blocks_transposed(pieces)):
             scale[pl.ds(px * 16 + j, 8, stride=SCALE_ROWS), :] = block
+    first = (lax.axis_index("px") == 0) & (lax.axis_index("py") == 0)
+
+    @pl.when(first)
+    def _():
+        unfold(scale)
+
     for px in range(N_PX):
         blocks = []
         for q in range(4):
             at = [(px * N_PY + 4 * q + i) * SEND_ROWS for i in range(4)]
-            parts = [blocks_transposed([got[s + 8 * part : s + 8 * part + 8, :] for s in at]) for part in range(2)]
+            parts = [blocks_transposed([got[pl.ds(s + 8 * part, 8), :] for s in at]) for part in range(2)]
             blocks.append(parts)
         for f in range(2):
             pair = []
@@ -189,8 +219,9 @@
         rows = slice(f * 128, f * 128 + 128)
         sides = [jnp.concatenate([a[rows, part * 128 : part * 128 + 128] for a in along_y], 1) for part in range(2)]
         spectral = left_product(x_into[...], jnp.concatenate(sides, 0))
-        at = [(f * 4 + r) * SCALE_ROWS for r in range(4)]
-        s = jnp.concatenate([scale[k : k + 128, :] for k in at], 1) * (1.0 / (NX * NY * NZ))
+        base = jnp.where(first, 8 + 4 * f, 3)
+        at = [pl.multiple_of((base + r) * SCALE_ROWS, 8) for r in range(4)]
+        s = jnp.concatenate([scale[pl.ds(k, 128), :] for k in at], 1) * (1.0 / (NX * NY * NZ))
         scaled = jnp.concatenate([spectral[:128] * s, spectral[128:] * s], 0)
         restored.append(left_product(x_back[...], scaled))
     back = []
@@ -315,10 +346,10 @@
             pltpu.VMEM((2, 512, 128), F32),
             pltpu.VMEM((256, NZ), BF16),
             pltpu.VMEM((256, NZ), BF16),
-            pltpu.SemaphoreType.DMA((12,)),
+            pltpu.SemaphoreType.DMA((8,)),
         ),
     )
-    got = lax.all_to_all(sent.reshape(DEVICES, SEND_ROWS, 128), ("px", "py"), 0, 0, tiled=True)
+    got = lax.all_to_all(sent.reshape(DEVICES, SEND_ROWS, 1, 128), ("px", "py"), 0, 0, tiled=True)
     (restored,) = call(
         middle_kernel,
         "planes",
@@ -327,7 +358,7 @@
         *tables["along_y"],
         *tables["x_into"],
         *tables["x_back"],
-        scratch=(pltpu.VMEM((4, 512, 256), BF16), pltpu.VMEM((8 * SCALE_ROWS, 128), F32)),
+        scratch=(pltpu.VMEM((4, 512, 256), BF16), pltpu.VMEM((16 * SCALE_ROWS, 128), F32)),
     )
     back = lax.all_to_all(restored.reshape(DEVICES, BACK_ROWS, 128), ("px", "py"), 0, 0, tiled=True)
     modulus, route = call(

time: 89.7 us -> 88.1 us (0.982)
  blocking collectives: 79.3 us -> 77.2 us
    all_to_all x1, blocking collectives: 35.3 us -> 33.3 us  [on_device(): lax.all_to_all(sent.reshape(DEVICES, SEND_ROWS, 1, 128), ('px', 'py'), 0,...]
where the time goes in v4:
time: 88.1 us; the launch traced here: 87.8 us
  blocking collectives  77.2 us (88%)
  Pallas kernels  9.76 us (11%)
    all_to_all x1, blocking collectives, on_device(): lax.all_to_all(sent.reshape(DEVICES, SEND_ROWS, 1, 128), ('px', 'py'), 0,...  33.3 us
    all_to_all x1, blocking collectives, on_device(): lax.all_to_all(restored.reshape(DEVICES, BACK_ROWS, 128), ('px', 'py'), 0...  24.2 us
    all_to_all x1, blocking collectives, on_device(): lax.all_to_all(route.reshape(N_PY, ROUTE_ROWS, 128), 'py', 0, 0, tiled=True)  10.1 us
    pallas_call x5, Pallas kernels, call(): pl.pallas_call(body, out_shape=outs, scratch_shapes=list(scratch), name=n...  9.76 us
    all_to_all x1, blocking collectives, on_device(): levels = lax.all_to_all(picked, 'py', 0, 0, tiled=True)  9.63 us

profile of v4, /device:TPU:1, one launch (start us, length us, event | category | flops | bytes accessed | tf_op | source)
XLA Modules:
  0.0 87.8 jit_solution(131398120052877833)
XLA Ops:
  0.6 2.2 %into_z.1 = f32[2688,128]{1,0:T(8,128)S(1)} custom-call(f32[1024,256]{1,0:T(8,128)} %bitcast.16, f32[512,256]{1,0:T(8,128)} %bitcast.17, bf16[256,256]{1,0:T(8,128)(2,1)} %constant.18.clone.high_far.b_high, bf16[256,256]{1,0:T(8,128)(2,1)} %constant.19.clone.low_far.b_low), custom_call_target="tpu_custom_call" | custom-call | tf_op jit(solution)/shard_map/into_z/pallas_call | solution.py:324
  2.9 0.0 copy-start
  2.9 0.0 copy-start.1
  2.9 0.0 copy-start.4
  2.9 0.0 copy-start.5
  2.9 33.3 %all_to_all.20 = f32[128,21,1,128]{3,2,1,0:T(1,128)S(1)} all-to-all(f32[128,21,1,128]{3,2,1,0:T(1,128)S(1)} %bitcast.11), channel_id=1, replica_groups=mesh['px'=8,'py'=16] {'px','py'}, dimensions={0} | all-to-all | bytes 2752512 | tf_op jit(solution)/shard_map/all_to_all | solution.py:352
  36.2 0.0 copy-done
  36.2 0.0 copy-done.1
  36.2 0.0 copy-done.4
  36.2 0.0 copy-done.5
  36.2 4.6 %planes.1 = f32[2048,128]{1,0:T(8,128)S(1)} custom-call(f32[2688,128]{1,0:T(8,128)S(1)} %bitcast.12, bf16[1024,256]{1,0:T(8,128)(2,1)S(1)} %copy-done.1, bf16[1024,256]{1,0:T(8,128)(2,1)S(1)} %copy-done, bf16[512,256]{1,0:T(8,128)(2,1)S(1)} %copy-done.5, bf16[512,256]{1,0:T(8,128)(2,1)S(1)} %copy-done.4), custom_call_target="tpu_custom_call" | custom-call | tf_op jit(solution)/shard_map/planes/pallas_call | solution.py:324
  40.8 0.0 copy-start.2
  40.8 0.0 copy-start.3
  40.9 0.0 copy-start.6
  40.9 0.0 copy-start.7
  40.9 0.0 copy-start.8
  40.9 24.2 %all_to_all.21 = f32[128,16,128]{2,1,0:T(8,128)S(1)} all-to-all(f32[128,16,128]{2,1,0:T(8,128)S(1)} %bitcast.14), channel_id=1, replica_groups=mesh['px'=8,'py'=16] {'px','py'}, dimensions={0} | all-to-all | bytes 2097152 | tf_op jit(solution)/shard_map/all_to_all | solution.py:363
  65.1 0.0 copy-start.9
  65.1 0.0 copy-done.2
  65.1 0.0 copy-done.3
  65.1 0.0 copy-done.6
  65.1 0.0 copy-done.7
  65.1 0.0 copy-done.8
  65.1 1.6 %back_z.1 = (f32[1024,256]{1,0:T(8,128)}, f32[384,128]{1,0:T(8,128)S(1)}) custom-call(f32[2048,128]{1,0:T(8,128)S(1)} %bitcast.13, bf16[256,256]{1,0:T(8,128)(2,1)S(1)} %copy-done.3, bf16[256,256]{1,0:T(8,128)(2,1)S(1)} %copy-done.2, bf16[256,128]{1,0:T(8,128)(2,1)S(1)} %copy-done.6, bf16[128,128]{1,0:T(8,128)(2,1)S(1)} %copy-done.8, ...), custom_call_target="tpu_custom_call" | custom-call | tf_op jit(solution)/shard_map/back_z/pallas_call | solution.py:324
  66.7 10.1 %all_to_all.22.got = f32[16,24,128]{2,1,0:T(8,128)S(1)} all-to-all(f32[16,24,128]{2,1,0:T(8,128)S(1)} %bitcast.15), channel_id=1, replica_groups=mesh['px'=8,'py'=16] {'py'}, dimensions={0} | all-to-all | bytes 393216 | tf_op jit(solution)/shard_map/all_to_all | solution.py:382
  76.9 0.0 copy-done.9
  76.9 0.6 pick.1
  77.5 9.6 %all_to_all.23.got = f32[16,24,128]{2,1,0:T(8,128)S(1)} all-to-all(f32[16,24,128]{2,1,0:T(8,128)S(1)} %pick.1), channel_id=1, replica_groups=mesh['px'=8,'py'=16] {'py'}, dimensions={0} | all-to-all | bytes 393216 | tf_op jit(solution)/shard_map/all_to_all | solution.py:391
  87.1 0.7 unpack.1
Async XLA Ops:
  2.9 33.3 %copy-start = (bf16[1024,256]{1,0:T(8,128)(2,1)S(1)}, bf16[1024,256]{1,0:T(8,128)(2,1)}, u32[]{:S(2)}) copy-start(bf16[1024,256]{1,0:T(8,128)(2,1)} %constant.21.clone.y_low) | copy-start | bytes 1572868
  2.9 33.3 %copy-start.1 = (bf16[1024,256]{1,0:T(8,128)(2,1)S(1)}, bf16[1024,256]{1,0:T(8,128)(2,1)}, u32[]{:S(2)}) copy-start(bf16[1024,256]{1,0:T(8,128)(2,1)} %constant.20.clone.y_high) | copy-start | bytes 1572868
  2.9 33.3 %copy-start.4 = (bf16[512,256]{1,0:T(8,128)(2,1)S(1)}, bf16[512,256]{1,0:T(8,128)(2,1)}, u32[]{:S(2)}) copy-start(bf16[512,256]{1,0:T(8,128)(2,1)} %constant.23.clone.x_back) | copy-start | bytes 786436
  2.9 33.3 %copy-start.5 = (bf16[512,256]{1,0:T(8,128)(2,1)S(1)}, bf16[512,256]{1,0:T(8,128)(2,1)}, u32[]{:S(2)}) copy-start(bf16[512,256]{1,0:T(8,128)(2,1)} %constant.22.clone.x_into) | copy-start | bytes 786436
  40.8 24.2 %copy-start.2 = (bf16[256,256]{1,0:T(8,128)(2,1)S(1)}, bf16[256,256]{1,0:T(8,128)(2,1)}, u32[]{:S(2)}) copy-start(bf16[256,256]{1,0:T(8,128)(2,1)} %constant.19.clone.low_far.b_low) | copy-start | bytes 393220
  40.8 24.2 %copy-start.3 = (bf16[256,256]{1,0:T(8,128)(2,1)S(1)}, bf16[256,256]{1,0:T(8,128)(2,1)}, u32[]{:S(2)}) copy-start(bf16[256,256]{1,0:T(8,128)(2,1)} %constant.18.clone.high_far.b_high) | copy-start | bytes 393220
  40.9 24.2 %copy-start.6 = (bf16[256,128]{1,0:T(8,128)(2,1)S(1)}, bf16[256,128]{1,0:T(8,128)(2,1)}, u32[]{:S(2)}) copy-start(bf16[256,128]{1,0:T(8,128)(2,1)} %constant.24.clone.mean1) | copy-start | bytes 196612
  40.9 24.2 %copy-start.7 = (bf16[128,128]{1,0:T(8,128)(2,1)S(1)}, bf16[128,128]{1,0:T(8,128)(2,1)}, u32[]{:S(2)}) copy-start(bf16[128,128]{1,0:T(8,128)(2,1)} %constant.26.clone.mean3) | copy-start | bytes 98308
  40.9 24.2 %copy-start.8 = (bf16[128,128]{1,0:T(8,128)(2,1)S(1)}, bf16[128,128]{1,0:T(8,128)(2,1)}, u32[]{:S(2)}) copy-start(bf16[128,128]{1,0:T(8,128)(2,1)} %constant.25.clone.mean2) | copy-start | bytes 98308
  65.1 11.8 %copy-start.9 = (s32[3,16]{1,0:T(4,128)S(1)}, s32[3,16]{1,0:T(4,128)}, u32[]{:S(2)}) copy-start(s32[3,16]{1,0:T(4,128)} %table.1) | copy-start | bytes 580

commit v5 on v4

--- a/solution.py
+++ b/solution.py
@@ -159,7 +159,7 @@
             out[20:21, :] = jnp.where(lower, other, plane[:1])
 
 
-def unfold(scale):
+def unfold(scale, first):
     row = lax.broadcasted_iota(jnp.int32, (128, 128), 0)
     lane = lax.broadcasted_iota(jnp.int32, (128, 128), 1)
     around = jnp.where((row + lane) % 128 == 0, 1.0, 0.0).astype(BF16)
@@ -177,22 +177,12 @@
         if r == 0:
             zero = jnp.where(lane == 64, column, zero)
             half = jnp.where(lane == 0, column, half)
-        scale[(8 + r) * SCALE_ROWS : (8 + r) * SCALE_ROWS + 128, :] = zero
-        scale[(12 + r) * SCALE_ROWS : (12 + r) * SCALE_ROWS + 128, :] = half
+        scale[(8 + r) * SCALE_ROWS : (8 + r) * SCALE_ROWS + 128, :] = jnp.where(first, zero, own)
+        scale[(12 + r) * SCALE_ROWS : (12 + r) * SCALE_ROWS + 128, :] = jnp.where(first, half, own)
 
 
 def middle_kernel(got, y_high, y_low, x_into, x_back, out, left, scale):
     plain, turned = (((1,), (0,)), ((), ())), (((1,), (1,)), ((), ()))
-    for px in range(N_PX):
-        pieces = [got[pl.ds((px * N_PY + i) * SEND_ROWS + 13, 8), :] for i in range(N_PY)]
-        for j, block in enumerate(blocks_transposed(pieces)):
-            scale[pl.ds(px * 16 + j, 8, stride=SCALE_ROWS), :] = block
-    first = (lax.axis_index("px") == 0) & (lax.axis_index("py") == 0)
-
-    @pl.when(first)
-    def _():
-        unfold(scale)
-
     for px in range(N_PX):
         blocks = []
         for q in range(4):
@@ -214,14 +204,18 @@
     for r in range(4):
         rows = slice(r * 256, r * 256 + 256)
         along_y.append(right_product(left[r], y_high[rows, :], y_low[rows, :], plain))
+    for px in range(N_PX):
+        pieces = [got[pl.ds((px * N_PY + i) * SEND_ROWS + 13, 8), :] for i in range(N_PY)]
+        for j, block in enumerate(blocks_transposed(pieces)):
+            scale[pl.ds(px * 16 + j, 8, stride=SCALE_ROWS), :] = block
+    unfold(scale, (lax.axis_index("px") == 0) & (lax.axis_index("py") == 0))
     restored = []
     for f in range(2):
         rows = slice(f * 128, f * 128 + 128)
         sides = [jnp.concatenate([a[rows, part * 128 : part * 128 + 128] for a in along_y], 1) for part in range(2)]
         spectral = left_product(x_into[...], jnp.concatenate(sides, 0))
-        base = jnp.where(first, 8 + 4 * f, 3)
-        at = [pl.multiple_of((base + r) * SCALE_ROWS, 8) for r in range(4)]
-        s = jnp.concatenate([scale[pl.ds(k, 128), :] for k in at], 1) * (1.0 / (NX * NY * NZ))
+        at = [(8 + f * 4 + r) * SCALE_ROWS for r in range(4)]
+        s = jnp.concatenate([scale[k : k + 128, :] for k in at], 1) * (1.0 / (NX * NY * NZ))
         scaled = jnp.concatenate([spectral[:128] * s, spectral[128:] * s], 0)
         restored.append(left_product(x_back[...], scaled))
     back = []

time: 88.1 us -> 87.1 us (0.989)
  Pallas kernels: 9.76 us -> 8.84 us
    pallas_call x5, Pallas kernels: 9.76 us -> 8.84 us  [call(): pl.pallas_call(body, out_shape=outs, scratch_shapes=list(scratch), name=n...]
where the time goes in v5:
time: 87.1 us; the launch traced here: 86.9 us
  blocking collectives  77.2 us (89%)
  Pallas kernels  8.84 us (10%)
    all_to_all x1, blocking collectives, on_device(): lax.all_to_all(sent.reshape(DEVICES, SEND_ROWS, 1, 128), ('px', 'py'), 0,...  33.3 us
    all_to_all x1, blocking collectives, on_device(): lax.all_to_all(restored.reshape(DEVICES, BACK_ROWS, 128), ('px', 'py'), 0...  24.2 us
    all_to_all x1, blocking collectives, on_device(): lax.all_to_all(route.reshape(N_PY, ROUTE_ROWS, 128), 'py', 0, 0, tiled=True)  10.1 us
    all_to_all x1, blocking collectives, on_device(): levels = lax.all_to_all(picked, 'py', 0, 0, tiled=True)  9.63 us
    pallas_call x5, Pallas kernels, call(): pl.pallas_call(body, out_shape=outs, scratch_shapes=list(scratch), name=n...  8.84 us

profile of v5, /device:TPU:1, one launch (start us, length us, event | category | flops | bytes accessed | tf_op | source)
XLA Modules:
  0.0 86.9 jit_solution(4671661764946619933)
XLA Ops:
  0.6 2.2 %into_z.1 = f32[2688,128]{1,0:T(8,128)S(1)} custom-call(f32[1024,256]{1,0:T(8,128)} %bitcast.16, f32[512,256]{1,0:T(8,128)} %bitcast.17, bf16[256,256]{1,0:T(8,128)(2,1)} %constant.18.clone.high_far.b_high, bf16[256,256]{1,0:T(8,128)(2,1)} %constant.19.clone.low_far.b_low), custom_call_target="tpu_custom_call" | custom-call | tf_op jit(solution)/shard_map/into_z/pallas_call | solution.py:318
  2.9 0.0 copy-start
  2.9 0.0 copy-start.1
  2.9 0.0 copy-start.4
  2.9 0.0 copy-start.5
  2.9 33.3 %all_to_all.20 = f32[128,21,1,128]{3,2,1,0:T(1,128)S(1)} all-to-all(f32[128,21,1,128]{3,2,1,0:T(1,128)S(1)} %bitcast.11), channel_id=1, replica_groups=mesh['px'=8,'py'=16] {'px','py'}, dimensions={0} | all-to-all | bytes 2752512 | tf_op jit(solution)/shard_map/all_to_all | solution.py:346
  36.2 0.0 copy-done
  36.2 0.0 copy-done.1
  36.2 0.0 copy-done.4
  36.2 0.0 copy-done.5
  36.2 3.7 %planes.1 = f32[2048,128]{1,0:T(8,128)S(1)} custom-call(f32[2688,128]{1,0:T(8,128)S(1)} %bitcast.12, bf16[1024,256]{1,0:T(8,128)(2,1)S(1)} %copy-done.1, bf16[1024,256]{1,0:T(8,128)(2,1)S(1)} %copy-done, bf16[512,256]{1,0:T(8,128)(2,1)S(1)} %copy-done.5, bf16[512,256]{1,0:T(8,128)(2,1)S(1)} %copy-done.4), custom_call_target="tpu_custom_call" | custom-call | tf_op jit(solution)/shard_map/planes/pallas_call | solution.py:318
  39.9 0.0 copy-start.2
  39.9 0.0 copy-start.3
  39.9 0.0 copy-start.6
  40.0 0.0 copy-start.7
  40.0 0.0 copy-start.8
  40.0 24.2 %all_to_all.21 = f32[128,16,128]{2,1,0:T(8,128)S(1)} all-to-all(f32[128,16,128]{2,1,0:T(8,128)S(1)} %bitcast.14), channel_id=1, replica_groups=mesh['px'=8,'py'=16] {'px','py'}, dimensions={0} | all-to-all | bytes 2097152 | tf_op jit(solution)/shard_map/all_to_all | solution.py:357
  64.2 0.0 copy-start.9
  64.2 0.0 copy-done.2
  64.2 0.0 copy-done.3
  64.2 0.0 copy-done.6
  64.2 0.0 copy-done.7
  64.2 0.0 copy-done.8
  64.2 1.6 %back_z.1 = (f32[1024,256]{1,0:T(8,128)}, f32[384,128]{1,0:T(8,128)S(1)}) custom-call(f32[2048,128]{1,0:T(8,128)S(1)} %bitcast.13, bf16[256,256]{1,0:T(8,128)(2,1)S(1)} %copy-done.3, bf16[256,256]{1,0:T(8,128)(2,1)S(1)} %copy-done.2, bf16[256,128]{1,0:T(8,128)(2,1)S(1)} %copy-done.6, bf16[128,128]{1,0:T(8,128)(2,1)S(1)} %copy-done.8, ...), custom_call_target="tpu_custom_call" | custom-call | tf_op jit(solution)/shard_map/back_z/pallas_call | solution.py:318
  65.8 10.1 %all_to_all.22.got = f32[16,24,128]{2,1,0:T(8,128)S(1)} all-to-all(f32[16,24,128]{2,1,0:T(8,128)S(1)} %bitcast.15), channel_id=1, replica_groups=mesh['px'=8,'py'=16] {'py'}, dimensions={0} | all-to-all | bytes 393216 | tf_op jit(solution)/shard_map/all_to_all | solution.py:376
  75.9 0.0 copy-done.9
  75.9 0.6 pick.1
  76.6 9.6 %all_to_all.23.got = f32[16,24,128]{2,1,0:T(8,128)S(1)} all-to-all(f32[16,24,128]{2,1,0:T(8,128)S(1)} %pick.1), channel_id=1, replica_groups=mesh['px'=8,'py'=16] {'py'}, dimensions={0} | all-to-all | bytes 393216 | tf_op jit(solution)/shard_map/all_to_all | solution.py:385
  86.2 0.7 unpack.1
Async XLA Ops:
  2.9 33.3 %copy-start = (bf16[1024,256]{1,0:T(8,128)(2,1)S(1)}, bf16[1024,256]{1,0:T(8,128)(2,1)}, u32[]{:S(2)}) copy-start(bf16[1024,256]{1,0:T(8,128)(2,1)} %constant.21.clone.y_low) | copy-start | bytes 1572868
  2.9 33.3 %copy-start.1 = (bf16[1024,256]{1,0:T(8,128)(2,1)S(1)}, bf16[1024,256]{1,0:T(8,128)(2,1)}, u32[]{:S(2)}) copy-start(bf16[1024,256]{1,0:T(8,128)(2,1)} %constant.20.clone.y_high) | copy-start | bytes 1572868
  2.9 33.3 %copy-start.4 = (bf16[512,256]{1,0:T(8,128)(2,1)S(1)}, bf16[512,256]{1,0:T(8,128)(2,1)}, u32[]{:S(2)}) copy-start(bf16[512,256]{1,0:T(8,128)(2,1)} %constant.23.clone.x_back) | copy-start | bytes 786436
  2.9 33.3 %copy-start.5 = (bf16[512,256]{1,0:T(8,128)(2,1)S(1)}, bf16[512,256]{1,0:T(8,128)(2,1)}, u32[]{:S(2)}) copy-start(bf16[512,256]{1,0:T(8,128)(2,1)} %constant.22.clone.x_into) | copy-start | bytes 786436
  39.9 24.2 %copy-start.2 = (bf16[256,256]{1,0:T(8,128)(2,1)S(1)}, bf16[256,256]{1,0:T(8,128)(2,1)}, u32[]{:S(2)}) copy-start(bf16[256,256]{1,0:T(8,128)(2,1)} %constant.19.clone.low_far.b_low) | copy-start | bytes 393220
  39.9 24.2 %copy-start.3 = (bf16[256,256]{1,0:T(8,128)(2,1)S(1)}, bf16[256,256]{1,0:T(8,128)(2,1)}, u32[]{:S(2)}) copy-start(bf16[256,256]{1,0:T(8,128)(2,1)} %constant.18.clone.high_far.b_high) | copy-start | bytes 393220
  39.9 24.2 %copy-start.6 = (bf16[256,128]{1,0:T(8,128)(2,1)S(1)}, bf16[256,128]{1,0:T(8,128)(2,1)}, u32[]{:S(2)}) copy-start(bf16[256,128]{1,0:T(8,128)(2,1)} %constant.24.clone.mean1) | copy-start | bytes 196612
  40.0 24.2 %copy-start.7 = (bf16[128,128]{1,0:T(8,128)(2,1)S(1)}, bf16[128,128]{1,0:T(8,128)(2,1)}, u32[]{:S(2)}) copy-start(bf16[128,128]{1,0:T(8,128)(2,1)} %constant.26.clone.mean3) | copy-start | bytes 98308
  40.0 24.2 %copy-start.8 = (bf16[128,128]{1,0:T(8,128)(2,1)S(1)}, bf16[128,128]{1,0:T(8,128)(2,1)}, u32[]{:S(2)}) copy-start(bf16[128,128]{1,0:T(8,128)(2,1)} %constant.25.clone.mean2) | copy-start | bytes 98308
  64.2 11.8 %copy-start.9 = (s32[3,16]{1,0:T(4,128)S(1)}, s32[3,16]{1,0:T(4,128)}, u32[]{:S(2)}) copy-start(s32[3,16]{1,0:T(4,128)} %table.1) | copy-start | bytes 580

commit v6 on v5

--- a/solution.py
+++ b/solution.py
@@ -15,10 +15,12 @@
 SEND_ROWS = 21
 BACK_ROWS = 16
 ROUTE_ROWS = 24
-SCALE_ROWS = 136
+SIDES = 2
+SIDE_ROWS = NX // SIDES
 VMEM_BYTES = 24 << 20
 F32 = jnp.float32
 BF16 = jnp.bfloat16
+PLANE_SCRATCH = (pltpu.VMEM((SIDES, 4, 4 * SIDE_ROWS, 256), BF16), pltpu.VMEM((1536, 128), F32))
 NEAR = pl.BlockSpec(memory_space=pltpu.VMEM)
 FAR = pl.BlockSpec(memory_space=pltpu.HBM)
 
@@ -46,7 +48,8 @@
         along_y.append(np.block([[cos_y, -sin_y], [sin_y, cos_y]]))
     row = np.arange(NX)
     x_of = (row // 16) * 16 + (row % 8) * 2 + row // 8 % 2
-    cos_x, sin_x = angle_tables(row, x_of, NX)
+    j_of = (row % 8) * 16 + row // 8
+    cos_x, sin_x = angle_tables(j_of, x_of, NX)
     x_into = np.block([[cos_x, sin_x], [-sin_x, cos_x]])
     return dict(
         into=halves(into),
@@ -159,82 +162,102 @@
             out[20:21, :] = jnp.where(lower, other, plane[:1])
 
 
-def unfold(scale, first):
+def unfold(got, scale, first):
     row = lax.broadcasted_iota(jnp.int32, (128, 128), 0)
     lane = lax.broadcasted_iota(jnp.int32, (128, 128), 1)
+    j_sum = row % 8 * 16 + row // 8 + lane % 8 * 16 + lane // 8
+    rows_turned = jnp.where(j_sum % 128 == 0, 1.0, 0.0).astype(BF16)
     around = jnp.where((row + lane) % 128 == 0, 1.0, 0.0).astype(BF16)
     mirrored = jnp.where(row + lane == 127, 1.0, 0.0).astype(BF16)
-    column = scale[7 * SCALE_ROWS : 7 * SCALE_ROWS + 128, :]
+    columns = []
+    for py in (8, 0):
+        v = got[pl.ds(py * SEND_ROWS + 20, N_PX, stride=N_PY * SEND_ROWS), :]
+        columns.append(jnp.concatenate([jnp.broadcast_to(v[:, 8 * j : 8 * j + 1], (8, 128)) for j in range(16)], 0))
     for r in range(4):
-        own = scale[(3 + r) * SCALE_ROWS : (3 + r) * SCALE_ROWS + 128, :]
-        at = (3 + (4 - r) % 4) * SCALE_ROWS
+        own = scale[r * 128 : r * 128 + 128, :]
+        at = (4 - r) % 4 * 128
         high, low = split(scale[at : at + 128, :])
         turn = mirrored if r else around
-        sides = [product(product(around, part).astype(BF16), turn) for part in (high, low)]
+        sides = [product(product(rows_turned, part).astype(BF16), turn) for part in (high, low)]
         partner = sides[0] + sides[1]
         zero = jnp.where(lane < 64, own, partner)
         half = jnp.where(lane < 64, partner, own)
         if r == 0:
-            zero = jnp.where(lane == 64, column, zero)
-            half = jnp.where(lane == 0, column, half)
-        scale[(8 + r) * SCALE_ROWS : (8 + r) * SCALE_ROWS + 128, :] = jnp.where(first, zero, own)
-        scale[(12 + r) * SCALE_ROWS : (12 + r) * SCALE_ROWS + 128, :] = jnp.where(first, half, own)
+            zero = jnp.where(lane == 64, columns[0], zero)
+            half = jnp.where(lane == 0, columns[1], half)
+        scale[512 + r * 128 : 640 + r * 128, :] = jnp.where(first, zero, own)
+        scale[1024 + r * 128 : 1152 + r * 128, :] = jnp.where(first, half, own)
 
 
 def middle_kernel(got, y_high, y_low, x_into, x_back, out, left, scale):
     plain, turned = (((1,), (0,)), ((), ())), (((1,), (1,)), ((), ()))
-    for px in range(N_PX):
-        blocks = []
-        for q in range(4):
-            at = [(px * N_PY + 4 * q + i) * SEND_ROWS for i in range(4)]
-            parts = [blocks_transposed([got[pl.ds(s + 8 * part, 8), :] for s in at]) for part in range(2)]
-            blocks.append(parts)
-        for f in range(2):
-            pair = []
-            for xl in range(2):
-                b = 2 * xl + f
-                pair.append(quarters([(blocks[q][0][b], blocks[q][1][b]) for q in range(4)], -1.0))
-            row = f * 128 + px * 16
-            for r in range(4):
-                for part in range(2):
-                    high, low = split(jnp.concatenate([pair[0][r][part], pair[1][r][part]], 0))
-                    left[r, row : row + 16, part * 128 : part * 128 + 128] = high
-                    left[r, 256 + row : 272 + row, part * 128 : part * 128 + 128] = low
     along_y = []
+    for side in range(SIDES):
+        for at_px in range(N_PX // SIDES):
+            px = side * (N_PX // SIDES) + at_px
+            blocks = []
+            for q in range(4):
+                at = [(px * N_PY + 4 * q + i) * SEND_ROWS for i in range(4)]
+                parts = [blocks_transposed([got[pl.ds(s + 8 * part, 8), :] for s in at]) for part in range(2)]
+                blocks.append(parts)
+            for f in range(2):
+                pair = []
+                for xl in range(2):
+                    b = 2 * xl + f
+                    pair.append(quarters([(blocks[q][0][b], blocks[q][1][b]) for q in range(4)], -1.0))
+                row = f * SIDE_ROWS + at_px * 16
+                for r in range(4):
+                    for part in range(2):
+                        lanes = slice(part * 128, part * 128 + 128)
+                        high, low = split(jnp.concatenate([pair[0][r][part], pair[1][r][part]], 0))
+                        left[side, r, row : row + 16, lanes] = high
+                        left[side, r, 2 * SIDE_ROWS + row : 2 * SIDE_ROWS + row + 16, lanes] = low
+        made = []
+        for r in range(4):
+            rows = slice(r * 256, r * 256 + 256)
+            made.append(right_product(left[side, r], y_high[rows, :], y_low[rows, :], plain))
+        along_y.append(made)
+    spectral = []
+    for f in range(2):
+        rows = slice(f * SIDE_ROWS, f * SIDE_ROWS + SIDE_ROWS)
+        parts = []
+        for part in range(2):
+            lanes = slice(part * 128, part * 128 + 128)
+            for made in along_y:
+                parts.append(jnp.concatenate([a[rows, lanes] for a in made], 1))
+        spectral.append(left_product(x_into[...], jnp.concatenate(parts, 0)))
     for r in range(4):
-        rows = slice(r * 256, r * 256 + 256)
-        along_y.append(right_product(left[r], y_high[rows, :], y_low[rows, :], plain))
-    for px in range(N_PX):
-        pieces = [got[pl.ds((px * N_PY + i) * SEND_ROWS + 13, 8), :] for i in range(N_PY)]
+        step = N_PY * SEND_ROWS
+        pieces = [got[pl.ds(py * SEND_ROWS + 16 + r, N_PX, stride=step), :] for py in range(N_PY)]
         for j, block in enumerate(blocks_transposed(pieces)):
-            scale[pl.ds(px * 16 + j, 8, stride=SCALE_ROWS), :] = block
-    unfold(scale, (lax.axis_index("px") == 0) & (lax.axis_index("py") == 0))
+            scale[r * 128 + j * 8 : r * 128 + j * 8 + 8, :] = block
+    unfold(got, scale, (lax.axis_index("px") == 0) & (lax.axis_index("py") == 0))
     restored = []
     for f in range(2):
-        rows = slice(f * 128, f * 128 + 128)
-        sides = [jnp.concatenate([a[rows, part * 128 : part * 128 + 128] for a in along_y], 1) for part in range(2)]
-        spectral = left_product(x_into[...], jnp.concatenate(sides, 0))
-        at = [(8 + f * 4 + r) * SCALE_ROWS for r in range(4)]
+        at = [512 + (f * 4 + r) * 128 for r in range(4)]
         s = jnp.concatenate([scale[k : k + 128, :] for k in at], 1) * (1.0 / (NX * NY * NZ))
-        scaled = jnp.concatenate([spectral[:128] * s, spectral[128:] * s], 0)
+        scaled = jnp.concatenate([spectral[f][:128] * s, spectral[f][128:] * s], 0)
         restored.append(left_product(x_back[...], scaled))
-    back = []
-    for r in range(4):
-        lanes = slice(r * 128, r * 128 + 128)
-        rows = [jnp.concatenate([z[:128, lanes], z[128:, lanes]], 1) for z in restored]
-        values = jnp.concatenate(split(jnp.concatenate(rows, 0)), 0)
-        at = slice(r * 256, r * 256 + 256)
-        back.append(right_product(values, y_high[at, :], y_low[at, :], turned))
-    for px in range(N_PX):
-        blocks = []
-        for b in range(4):
-            row = (b % 2) * 128 + px * 16 + (b // 2) * 8
-            blocks.append(quarters([(u[row : row + 8, :128], u[row : row + 8, 128:]) for u in back], 1.0))
-        for q in range(4):
-            for part in range(2):
-                for i, block in enumerate(blocks_transposed([blocks[b][q][part] for b in range(4)])):
-                    at = (px * N_PY + 4 * q + i) * BACK_ROWS + 8 * part
-                    out[at : at + 8, :] = block
+    for side in range(SIDES):
+        back = []
+        for r in range(4):
+            lanes = slice(r * 128, r * 128 + 128)
+            at, end = side * SIDE_ROWS, side * SIDE_ROWS + SIDE_ROWS
+            rows = [jnp.concatenate([z[at:end, lanes], z[128 + at : 128 + end, lanes]], 1) for z in restored]
+            values = jnp.concatenate(split(jnp.concatenate(rows, 0)), 0)
+            table = slice(r * 256, r * 256 + 256)
+            back.append(right_product(values, y_high[table, :], y_low[table, :], turned))
+        for at_px in range(N_PX // SIDES):
+            px = side * (N_PX // SIDES) + at_px
+            blocks = []
+            for b in range(4):
+                row = (b % 2) * SIDE_ROWS + at_px * 16 + (b // 2) * 8
+                blocks.append(quarters([(u[row : row + 8, :128], u[row : row + 8, 128:]) for u in back], 1.0))
+            for q in range(4):
+                for part in range(2):
+                    for i, block in enumerate(blocks_transposed([blocks[b][q][part] for b in range(4)])):
+                        at = (px * N_PY + 4 * q + i) * BACK_ROWS + 8 * part
+                        out[at : at + 8, :] = block
 
 
 def last_kernel(got, b_high, b_low, mean1, mean2, mean3, modulus_far, route, sums, sums2, sums3, modulus, left):
@@ -299,11 +322,18 @@
         out[g, 20:24, :] = got[table[2, g], 20:24, :]
 
 
-def unpack_kernel(got, one, two, three):
+def unpack_kernel(got, one_far, two_far, three_far, two, three, left):
+    copies = [pltpu.make_async_copy(got.at[:, pl.ds(0, 16), :], one_far, left.at[0])]
+    copies[0].start()
     for p in range(N_PY):
-        one[p * 16 : p * 16 + 16, :] = got[p, 0:16, :]
         two[p * 4 : p * 4 + 4, :] = got[p, 16:20, 0:64]
         three[p : p + 1, :] = got[p, 20:21, 0:32]
+    copies.append(pltpu.make_async_copy(two, two_far, left.at[1]))
+    copies.append(pltpu.make_async_copy(three, three_far, left.at[2]))
+    copies[1].start()
+    copies[2].start()
+    for copy in copies:
+        copy.wait()
 
 
 def on_chip(x):
@@ -352,7 +382,7 @@
         *tables["along_y"],
         *tables["x_into"],
         *tables["x_back"],
-        scratch=(pltpu.VMEM((4, 512, 256), BF16), pltpu.VMEM((16 * SCALE_ROWS, 128), F32)),
+        scratch=PLANE_SCRATCH,
     )
     back = lax.all_to_all(restored.reshape(DEVICES, BACK_ROWS, 128), ("px", "py"), 0, 0, tiled=True)
     modulus, route = call(
@@ -383,7 +413,14 @@
         in_specs=[pl.BlockSpec(memory_space=pltpu.SMEM), NEAR],
     )
     levels = lax.all_to_all(picked, "py", 0, 0, tiled=True)
-    one, two, three = call(unpack_kernel, "unpack", [jax.ShapeDtypeStruct(s, F32) for s in ((256, 128), (64, 64), (16, 32))], on_chip(levels))
+    one, two, three = call(
+        unpack_kernel,
+        "unpack",
+        [jax.ShapeDtypeStruct(s, F32) for s in ((16, 16, 128), (64, 64), (16, 32))],
+        on_chip(levels),
+        out_specs=[FAR] * 3,
+        scratch=(pltpu.VMEM((64, 64), F32), pltpu.VMEM((16, 32), F32), pltpu.SemaphoreType.DMA((3,))),
+    )
     return (
         modulus.reshape(2, 16, 32, NZ),
         one.reshape(2, 8, 16, 128),

time: 87.1 us -> 86.8 us (level)
  no operation moved by 1% of the time
where the time goes in v6:
time: 86.8 us; the launch traced here: 86.5 us
  blocking collectives  77.2 us (89%)
  Pallas kernels  8.46 us (10%)
    all_to_all x1, blocking collectives, on_device(): lax.all_to_all(sent.reshape(DEVICES, SEND_ROWS, 1, 128), ('px', 'py'), 0,...  33.3 us
    all_to_all x1, blocking collectives, on_device(): lax.all_to_all(restored.reshape(DEVICES, BACK_ROWS, 128), ('px', 'py'), 0...  24.2 us
    all_to_all x1, blocking collectives, on_device(): lax.all_to_all(route.reshape(N_PY, ROUTE_ROWS, 128), 'py', 0, 0, tiled=True)  10.1 us
    all_to_all x1, blocking collectives, on_device(): levels = lax.all_to_all(picked, 'py', 0, 0, tiled=True)  9.63 us
    pallas_call x5, Pallas kernels, call(): pl.pallas_call(body, out_shape=outs, scratch_shapes=list(scratch), name=n...  8.46 us

profile of v6, /device:TPU:1, one launch (start us, length us, event | category | flops | bytes accessed | tf_op | source)
XLA Modules:
  0.0 86.5 jit_solution(12373062751810223889)
XLA Ops:
  0.6 2.2 %into_z.1 = f32[2688,128]{1,0:T(8,128)S(1)} custom-call(f32[1024,256]{1,0:T(8,128)} %bitcast.16, f32[512,256]{1,0:T(8,128)} %bitcast.17, bf16[256,256]{1,0:T(8,128)(2,1)} %constant.18.clone.high_far.b_high, bf16[256,256]{1,0:T(8,128)(2,1)} %constant.19.clone.low_far.b_low), custom_call_target="tpu_custom_call" | custom-call | tf_op jit(solution)/shard_map/into_z/pallas_call | solution.py:348
  2.9 0.0 copy-start
  2.9 0.0 copy-start.1
  2.9 0.0 copy-start.4
  2.9 0.0 copy-start.5
  2.9 33.3 %all_to_all.20 = f32[128,21,1,128]{3,2,1,0:T(1,128)S(1)} all-to-all(f32[128,21,1,128]{3,2,1,0:T(1,128)S(1)} %bitcast.11), channel_id=1, replica_groups=mesh['px'=8,'py'=16] {'px','py'}, dimensions={0} | all-to-all | bytes 2752512 | tf_op jit(solution)/shard_map/all_to_all | solution.py:376
  36.2 0.0 copy-done
  36.2 0.0 copy-done.1
  36.2 0.0 copy-done.4
  36.2 0.0 copy-done.5
  36.2 3.3 %planes.1 = f32[2048,128]{1,0:T(8,128)S(1)} custom-call(f32[2688,128]{1,0:T(8,128)S(1)} %bitcast.12, bf16[1024,256]{1,0:T(8,128)(2,1)S(1)} %copy-done.1, bf16[1024,256]{1,0:T(8,128)(2,1)S(1)} %copy-done, bf16[512,256]{1,0:T(8,128)(2,1)S(1)} %copy-done.5, bf16[512,256]{1,0:T(8,128)(2,1)S(1)} %copy-done.4), custom_call_target="tpu_custom_call" | custom-call | tf_op jit(solution)/shard_map/planes/pallas_call | solution.py:348
  39.5 0.0 copy-start.2
  39.6 0.0 copy-start.3
  39.6 0.0 copy-start.6
  39.6 0.0 copy-start.7
  39.6 0.0 copy-start.8
  39.6 24.2 %all_to_all.21 = f32[128,16,128]{2,1,0:T(8,128)S(1)} all-to-all(f32[128,16,128]{2,1,0:T(8,128)S(1)} %bitcast.14), channel_id=1, replica_groups=mesh['px'=8,'py'=16] {'px','py'}, dimensions={0} | all-to-all | bytes 2097152 | tf_op jit(solution)/shard_map/all_to_all | solution.py:387
  63.8 0.0 copy-start.9
  63.8 0.0 copy-done.2
  63.8 0.0 copy-done.3
  63.8 0.0 copy-done.6
  63.8 0.0 copy-done.7
  63.8 0.0 copy-done.8
  63.8 1.6 %back_z.1 = (f32[1024,256]{1,0:T(8,128)}, f32[384,128]{1,0:T(8,128)S(1)}) custom-call(f32[2048,128]{1,0:T(8,128)S(1)} %bitcast.13, bf16[256,256]{1,0:T(8,128)(2,1)S(1)} %copy-done.3, bf16[256,256]{1,0:T(8,128)(2,1)S(1)} %copy-done.2, bf16[256,128]{1,0:T(8,128)(2,1)S(1)} %copy-done.6, bf16[128,128]{1,0:T(8,128)(2,1)S(1)} %copy-done.8, ...), custom_call_target="tpu_custom_call" | custom-call | tf_op jit(solution)/shard_map/back_z/pallas_call | solution.py:348
  65.4 10.1 %all_to_all.22.got = f32[16,24,128]{2,1,0:T(8,128)S(1)} all-to-all(f32[16,24,128]{2,1,0:T(8,128)S(1)} %bitcast.15), channel_id=1, replica_groups=mesh['px'=8,'py'=16] {'py'}, dimensions={0} | all-to-all | bytes 393216 | tf_op jit(solution)/shard_map/all_to_all | solution.py:406
  75.6 0.0 copy-done.9
  75.6 0.6 pick.1
  76.2 9.6 %all_to_all.23.got = f32[16,24,128]{2,1,0:T(8,128)S(1)} all-to-all(f32[16,24,128]{2,1,0:T(8,128)S(1)} %pick.1), channel_id=1, replica_groups=mesh['px'=8,'py'=16] {'py'}, dimensions={0} | all-to-all | bytes 393216 | tf_op jit(solution)/shard_map/all_to_all | solution.py:415
  85.8 0.7 unpack.1
Async XLA Ops:
  2.9 33.3 %copy-start = (bf16[1024,256]{1,0:T(8,128)(2,1)S(1)}, bf16[1024,256]{1,0:T(8,128)(2,1)}, u32[]{:S(2)}) copy-start(bf16[1024,256]{1,0:T(8,128)(2,1)} %constant.21.clone.y_low) | copy-start | bytes 1572868
  2.9 33.3 %copy-start.1 = (bf16[1024,256]{1,0:T(8,128)(2,1)S(1)}, bf16[1024,256]{1,0:T(8,128)(2,1)}, u32[]{:S(2)}) copy-start(bf16[1024,256]{1,0:T(8,128)(2,1)} %constant.20.clone.y_high) | copy-start | bytes 1572868
  2.9 33.3 %copy-start.4 = (bf16[512,256]{1,0:T(8,128)(2,1)S(1)}, bf16[512,256]{1,0:T(8,128)(2,1)}, u32[]{:S(2)}) copy-start(bf16[512,256]{1,0:T(8,128)(2,1)} %constant.23.clone.x_back) | copy-start | bytes 786436
  2.9 33.3 %copy-start.5 = (bf16[512,256]{1,0:T(8,128)(2,1)S(1)}, bf16[512,256]{1,0:T(8,128)(2,1)}, u32[]{:S(2)}) copy-start(bf16[512,256]{1,0:T(8,128)(2,1)} %constant.22.clone.x_into) | copy-start | bytes 786436
  39.5 24.3 %copy-start.2 = (bf16[256,256]{1,0:T(8,128)(2,1)S(1)}, bf16[256,256]{1,0:T(8,128)(2,1)}, u32[]{:S(2)}) copy-start(bf16[256,256]{1,0:T(8,128)(2,1)} %constant.19.clone.low_far.b_low) | copy-start | bytes 393220
  39.6 24.2 %copy-start.3 = (bf16[256,256]{1,0:T(8,128)(2,1)S(1)}, bf16[256,256]{1,0:T(8,128)(2,1)}, u32[]{:S(2)}) copy-start(bf16[256,256]{1,0:T(8,128)(2,1)} %constant.18.clone.high_far.b_high) | copy-start | bytes 393220
  39.6 24.2 %copy-start.6 = (bf16[256,128]{1,0:T(8,128)(2,1)S(1)}, bf16[256,128]{1,0:T(8,128)(2,1)}, u32[]{:S(2)}) copy-start(bf16[256,128]{1,0:T(8,128)(2,1)} %constant.24.clone.mean1) | copy-start | bytes 196612
  39.6 24.2 %copy-start.7 = (bf16[128,128]{1,0:T(8,128)(2,1)S(1)}, bf16[128,128]{1,0:T(8,128)(2,1)}, u32[]{:S(2)}) copy-start(bf16[128,128]{1,0:T(8,128)(2,1)} %constant.26.clone.mean3) | copy-start | bytes 98308
  39.6 24.2 %copy-start.8 = (bf16[128,128]{1,0:T(8,128)(2,1)S(1)}, bf16[128,128]{1,0:T(8,128)(2,1)}, u32[]{:S(2)}) copy-start(bf16[128,128]{1,0:T(8,128)(2,1)} %constant.25.clone.mean2) | copy-start | bytes 98308
  63.8 11.8 %copy-start.9 = (s32[3,16]{1,0:T(4,128)S(1)}, s32[3,16]{1,0:T(4,128)}, u32[]{:S(2)}) copy-start(s32[3,16]{1,0:T(4,128)} %table.1) | copy-start | bytes 580

commit v7 on v6

--- a/solution.py
+++ b/solution.py
@@ -77,8 +77,13 @@
     return product(a[0], b[0], dims) + product(a[1], b[0], dims) + product(a[0], b[1], dims)
 
 
-def swapped_parts(part0, part1):
-    first = lax.broadcasted_iota(jnp.int32, part0.shape, 1) // 32 % 2 == 0
+def places(turn):
+    numbers = [(p + 4 - turn) % 4 for p in range(4)]
+    return [b % 2 * 512 + b // 2 * 32 for b in numbers]
+
+
+def swapped_parts(part0, part1, turn):
+    first = (lax.broadcasted_iota(jnp.int32, part0.shape, 1) // 32 + turn) % 2 == 0
     new0 = jnp.where(first, part0, pltpu.roll(part1, 32, 1))
     new1 = jnp.where(first, pltpu.roll(part0, 96, 1), part1)
     return new0, new1
@@ -98,6 +103,25 @@
                 parts[i + step] = jnp.where(stays, pltpu.roll(a, 128 - step * width, 1), b)
         step //= 2
     return parts
+
+
+def picked_blocks(parts):
+    block = lax.broadcasted_iota(jnp.int32, parts[0].shape, 1) // 32
+    picked = []
+    for k in range(4):
+        value = parts[-k % 4]
+        for p in range(1, 4):
+            value = jnp.where(block == p, parts[(p - k) % 4], value)
+        picked.append(value)
+    return picked
+
+
+def gathered_blocks(parts):
+    return [pltpu.roll(v, 128 - 32 * b, 1) if b else v for b, v in enumerate(picked_blocks(parts))]
+
+
+def scattered_blocks(parts):
+    return picked_blocks([pltpu.roll(v, 32 * b, 1) if b else v for b, v in enumerate(parts)])
 
 
 def quarters(values, sign):
@@ -136,9 +160,10 @@
         copy.wait()
     table = t_high[...], t_low[...]
     nt = (((1,), (1,)), ((), ()))
+    turn = lax.axis_index("py") % 4
     for pair in range(4):
-        starts = [f * 512 + (4 * pair + x) * 32 for x in range(4) for f in range(2)]
-        block = jnp.concatenate([noise[s : s + 32, :] for s in starts], 0)
+        starts = [pl.multiple_of(base + (2 * pair + at) * 64, 32) for at in range(2) for base in places(turn)]
+        block = jnp.concatenate([noise[pl.ds(s, 32), :] for s in starts], 0)
         made = product3(table, split(block), nt)
         for at in range(2):
             xh = 2 * pair + at
@@ -146,7 +171,7 @@
             part1 = made[128:, at * 128 : at * 128 + 128]
             out[pl.ds(xh, DEVICES, stride=SEND_ROWS), :] = part0
             out[pl.ds(8 + xh, DEVICES, stride=SEND_ROWS), :] = part1
-            new0, new1 = swapped_parts(part0[:8], part1[:8])
+            new0, new1 = swapped_parts(part0[:8], part1[:8], turn)
             out[xh : xh + 1, :] = new0[:1]
             out[8 + xh : 9 + xh, :] = new1[:1]
     for copy in copies[6:]:
@@ -198,7 +223,7 @@
             blocks = []
             for q in range(4):
                 at = [(px * N_PY + 4 * q + i) * SEND_ROWS for i in range(4)]
-                parts = [blocks_transposed([got[pl.ds(s + 8 * part, 8), :] for s in at]) for part in range(2)]
+                parts = [gathered_blocks([got[pl.ds(s + 8 * part, 8), :] for s in at]) for part in range(2)]
                 blocks.append(parts)
             for f in range(2):
                 pair = []
@@ -255,7 +280,7 @@
                 blocks.append(quarters([(u[row : row + 8, :128], u[row : row + 8, 128:]) for u in back], 1.0))
             for q in range(4):
                 for part in range(2):
-                    for i, block in enumerate(blocks_transposed([blocks[b][q][part] for b in range(4)])):
+                    for i, block in enumerate(scattered_blocks([blocks[b][q][part] for b in range(4)])):
                         at = (px * N_PY + 4 * q + i) * BACK_ROWS + 8 * part
                         out[at : at + 8, :] = block
 
@@ -263,6 +288,7 @@
 def last_kernel(got, b_high, b_low, mean1, mean2, mean3, modulus_far, route, sums, sums2, sums3, modulus, left):
     copies = []
     table = b_high[...], b_low[...]
+    turn = lax.axis_index("py") % 4
     first_row = lax.broadcasted_iota(jnp.int32, (128, 128), 0) == 0
     for pair in range(4):
         rows = []
@@ -270,22 +296,21 @@
             xh = 2 * pair + at
             part0 = got[pl.ds(xh, DEVICES, stride=BACK_ROWS), :]
             part1 = got[pl.ds(8 + xh, DEVICES, stride=BACK_ROWS), :]
-            new0, new1 = swapped_parts(part0, part1)
+            new0, new1 = swapped_parts(part0, part1, turn)
             part0 = jnp.where(first_row, 0.5 * new0, part0)
             part1 = jnp.where(first_row, 0.5 * new1, part1)
             rows.append(jnp.concatenate([part0.T, part1.T], 1))
         values = jnp.exp(product3(split(jnp.concatenate(rows, 0)), table))
         for at in range(2):
             xh = 2 * pair + at
-            for f in range(2):
-                first = values[at * 128 + f * 32 : at * 128 + f * 32 + 32]
-                second = values[at * 128 + 64 + f * 32 : at * 128 + 64 + f * 32 + 32]
-                base = f * 512 + xh * 64
-                modulus[base : base + 32, :] = first
-                modulus[base + 32 : base + 64, :] = second
-                both = first + second
-                sums[0, f * 256 + xh * 32 : f * 256 + xh * 32 + 32, :] = both[:, :128]
-                sums[1, f * 256 + xh * 32 : f * 256 + xh * 32 + 32, :] = both[:, 128:]
+            cells = [values[at * 128 + p * 32 : at * 128 + p * 32 + 32] for p in range(4)]
+            for p, base in enumerate(places(turn)):
+                modulus[pl.ds(pl.multiple_of(base + xh * 64, 32), 32), :] = cells[p]
+            for p in range(2):
+                both = cells[p] + cells[p + 2]
+                rows = pl.ds(pl.multiple_of((p + turn) % 2 * 256 + xh * 32, 32), 32)
+                sums[0, rows, :] = both[:, :128]
+                sums[1, rows, :] = both[:, 128:]
         for f in range(2):
             rows = pl.ds(f * 512 + pair * 128, 128)
             copies.append(pltpu.make_async_copy(modulus.at[rows, :], modulus_far.at[rows, :], left.at[len(copies)]))

time: 86.8 us -> 86.6 us (level)
  no operation moved by 1% of the time
where the time goes in v7:
time: 86.6 us; the launch traced here: 86.3 us
  blocking collectives  77.2 us (89%)
  Pallas kernels  8.25 us (10%)
    all_to_all x1, blocking collectives, on_device(): lax.all_to_all(sent.reshape(DEVICES, SEND_ROWS, 1, 128), ('px', 'py'), 0,...  33.3 us
    all_to_all x1, blocking collectives, on_device(): lax.all_to_all(restored.reshape(DEVICES, BACK_ROWS, 128), ('px', 'py'), 0...  24.2 us
    all_to_all x1, blocking collectives, on_device(): lax.all_to_all(route.reshape(N_PY, ROUTE_ROWS, 128), 'py', 0, 0, tiled=True)  10.1 us
    all_to_all x1, blocking collectives, on_device(): levels = lax.all_to_all(picked, 'py', 0, 0, tiled=True)  9.63 us
    pallas_call x5, Pallas kernels, call(): pl.pallas_call(body, out_shape=outs, scratch_shapes=list(scratch), name=n...  8.25 us

profile of v7, /device:TPU:1, one launch (start us, length us, event | category | flops | bytes accessed | tf_op | source)
XLA Modules:
  0.0 86.3 jit_solution(4461585638163848924)
XLA Ops:
  0.6 2.2 %into_z.1 = f32[2688,128]{1,0:T(8,128)S(1)} custom-call(f32[1024,256]{1,0:T(8,128)} %bitcast.16, f32[512,256]{1,0:T(8,128)} %bitcast.17, bf16[256,256]{1,0:T(8,128)(2,1)} %constant.18.clone.high_far.b_high, bf16[256,256]{1,0:T(8,128)(2,1)} %constant.19.clone.low_far.b_low), custom_call_target="tpu_custom_call" | custom-call | tf_op jit(solution)/shard_map/into_z/pallas_call | solution.py:373
  2.9 0.0 copy-start
  2.9 0.0 copy-start.1
  2.9 0.0 copy-start.4
  2.9 0.0 copy-start.5
  2.9 33.3 %all_to_all.20 = f32[128,21,1,128]{3,2,1,0:T(1,128)S(1)} all-to-all(f32[128,21,1,128]{3,2,1,0:T(1,128)S(1)} %bitcast.11), channel_id=1, replica_groups=mesh['px'=8,'py'=16] {'px','py'}, dimensions={0} | all-to-all | bytes 2752512 | tf_op jit(solution)/shard_map/all_to_all | solution.py:401
  36.2 0.0 copy-done
  36.2 0.0 copy-done.1
  36.2 0.0 copy-done.4
  36.2 0.0 copy-done.5
  36.2 3.1 %planes.1 = f32[2048,128]{1,0:T(8,128)S(1)} custom-call(f32[2688,128]{1,0:T(8,128)S(1)} %bitcast.12, bf16[1024,256]{1,0:T(8,128)(2,1)S(1)} %copy-done.1, bf16[1024,256]{1,0:T(8,128)(2,1)S(1)} %copy-done, bf16[512,256]{1,0:T(8,128)(2,1)S(1)} %copy-done.5, bf16[512,256]{1,0:T(8,128)(2,1)S(1)} %copy-done.4), custom_call_target="tpu_custom_call" | custom-call | tf_op jit(solution)/shard_map/planes/pallas_call | solution.py:373
  39.3 0.0 copy-start.2
  39.3 0.0 copy-start.3
  39.3 0.0 copy-start.6
  39.4 0.0 copy-start.7
  39.4 0.0 copy-start.8
  39.4 24.2 %all_to_all.21 = f32[128,16,128]{2,1,0:T(8,128)S(1)} all-to-all(f32[128,16,128]{2,1,0:T(8,128)S(1)} %bitcast.14), channel_id=1, replica_groups=mesh['px'=8,'py'=16] {'px','py'}, dimensions={0} | all-to-all | bytes 2097152 | tf_op jit(solution)/shard_map/all_to_all | solution.py:412
  63.6 0.0 copy-start.9
  63.6 0.0 copy-done.2
  63.6 0.0 copy-done.3
  63.6 0.0 copy-done.6
  63.6 0.0 copy-done.7
  63.6 0.0 copy-done.8
  63.6 1.6 %back_z.1 = (f32[1024,256]{1,0:T(8,128)}, f32[384,128]{1,0:T(8,128)S(1)}) custom-call(f32[2048,128]{1,0:T(8,128)S(1)} %bitcast.13, bf16[256,256]{1,0:T(8,128)(2,1)S(1)} %copy-done.3, bf16[256,256]{1,0:T(8,128)(2,1)S(1)} %copy-done.2, bf16[256,128]{1,0:T(8,128)(2,1)S(1)} %copy-done.6, bf16[128,128]{1,0:T(8,128)(2,1)S(1)} %copy-done.8, ...), custom_call_target="tpu_custom_call" | custom-call | tf_op jit(solution)/shard_map/back_z/pallas_call | solution.py:373
  65.2 10.1 %all_to_all.22.got = f32[16,24,128]{2,1,0:T(8,128)S(1)} all-to-all(f32[16,24,128]{2,1,0:T(8,128)S(1)} %bitcast.15), channel_id=1, replica_groups=mesh['px'=8,'py'=16] {'py'}, dimensions={0} | all-to-all | bytes 393216 | tf_op jit(solution)/shard_map/all_to_all | solution.py:431
  75.4 0.0 copy-done.9
  75.4 0.6 pick.1
  76.0 9.6 %all_to_all.23.got = f32[16,24,128]{2,1,0:T(8,128)S(1)} all-to-all(f32[16,24,128]{2,1,0:T(8,128)S(1)} %pick.1), channel_id=1, replica_groups=mesh['px'=8,'py'=16] {'py'}, dimensions={0} | all-to-all | bytes 393216 | tf_op jit(solution)/shard_map/all_to_all | solution.py:440
  85.6 0.7 unpack.1
Async XLA Ops:
  2.9 33.3 %copy-start = (bf16[1024,256]{1,0:T(8,128)(2,1)S(1)}, bf16[1024,256]{1,0:T(8,128)(2,1)}, u32[]{:S(2)}) copy-start(bf16[1024,256]{1,0:T(8,128)(2,1)} %constant.21.clone.y_low) | copy-start | bytes 1572868
  2.9 33.3 %copy-start.1 = (bf16[1024,256]{1,0:T(8,128)(2,1)S(1)}, bf16[1024,256]{1,0:T(8,128)(2,1)}, u32[]{:S(2)}) copy-start(bf16[1024,256]{1,0:T(8,128)(2,1)} %constant.20.clone.y_high) | copy-start | bytes 1572868
  2.9 33.3 %copy-start.4 = (bf16[512,256]{1,0:T(8,128)(2,1)S(1)}, bf16[512,256]{1,0:T(8,128)(2,1)}, u32[]{:S(2)}) copy-start(bf16[512,256]{1,0:T(8,128)(2,1)} %constant.23.clone.x_back) | copy-start | bytes 786436
  2.9 33.3 %copy-start.5 = (bf16[512,256]{1,0:T(8,128)(2,1)S(1)}, bf16[512,256]{1,0:T(8,128)(2,1)}, u32[]{:S(2)}) copy-start(bf16[512,256]{1,0:T(8,128)(2,1)} %constant.22.clone.x_into) | copy-start | bytes 786436
  39.3 24.3 %copy-start.2 = (bf16[256,256]{1,0:T(8,128)(2,1)S(1)}, bf16[256,256]{1,0:T(8,128)(2,1)}, u32[]{:S(2)}) copy-start(bf16[256,256]{1,0:T(8,128)(2,1)} %constant.19.clone.low_far.b_low) | copy-start | bytes 393220
  39.3 24.2 %copy-start.3 = (bf16[256,256]{1,0:T(8,128)(2,1)S(1)}, bf16[256,256]{1,0:T(8,128)(2,1)}, u32[]{:S(2)}) copy-start(bf16[256,256]{1,0:T(8,128)(2,1)} %constant.18.clone.high_far.b_high) | copy-start | bytes 393220
  39.3 24.2 %copy-start.6 = (bf16[256,128]{1,0:T(8,128)(2,1)S(1)}, bf16[256,128]{1,0:T(8,128)(2,1)}, u32[]{:S(2)}) copy-start(bf16[256,128]{1,0:T(8,128)(2,1)} %constant.24.clone.mean1) | copy-start | bytes 196612
  39.4 24.2 %copy-start.7 = (bf16[128,128]{1,0:T(8,128)(2,1)S(1)}, bf16[128,128]{1,0:T(8,128)(2,1)}, u32[]{:S(2)}) copy-start(bf16[128,128]{1,0:T(8,128)(2,1)} %constant.26.clone.mean3) | copy-start | bytes 98308
  39.4 24.2 %copy-start.8 = (bf16[128,128]{1,0:T(8,128)(2,1)S(1)}, bf16[128,128]{1,0:T(8,128)(2,1)}, u32[]{:S(2)}) copy-start(bf16[128,128]{1,0:T(8,128)(2,1)} %constant.25.clone.mean2) | copy-start | bytes 98308
  63.6 11.8 %copy-start.9 = (s32[3,16]{1,0:T(4,128)S(1)}, s32[3,16]{1,0:T(4,128)}, u32[]{:S(2)}) copy-start(s32[3,16]{1,0:T(4,128)} %table.1) | copy-start | bytes 580

commit v8 on v7

--- a/solution.py
+++ b/solution.py
@@ -14,10 +14,11 @@
 DEVICES = N_PX * N_PY
 SEND_ROWS = 21
 BACK_ROWS = 16
-ROUTE_ROWS = 24
+ROUTE_ROWS = 20
 SIDES = 2
 SIDE_ROWS = NX // SIDES
 VMEM_BYTES = 24 << 20
+ROUTE = (N_PY, ROUTE_ROWS // 4, 4, 128)
 F32 = jnp.float32
 BF16 = jnp.bfloat16
 PLANE_SCRATCH = (pltpu.VMEM((SIDES, 4, 4 * SIDE_ROWS, 256), BF16), pltpu.VMEM((1536, 128), F32))
@@ -59,8 +60,8 @@
     )
 
 
-def pair_mean(size):
-    rows, columns = np.arange(size), np.arange(128)
+def pair_mean(size, first=0):
+    rows, columns = np.arange(size), np.arange(128) - first
     return (0.125 * (rows[:, None] // 2 == columns[None, :])).astype(ml_dtypes.bfloat16)
 
 
@@ -242,6 +243,12 @@
             rows = slice(r * 256, r * 256 + 256)
             made.append(right_product(left[side, r], y_high[rows, :], y_low[rows, :], plain))
         along_y.append(made)
+    for r in range(4):
+        step = N_PY * SEND_ROWS
+        pieces = [got[pl.ds(py * SEND_ROWS + 16 + r, N_PX, stride=step), :] for py in range(N_PY)]
+        for j, block in enumerate(blocks_transposed(pieces)):
+            scale[r * 128 + j * 8 : r * 128 + j * 8 + 8, :] = block
+    unfold(got, scale, (lax.axis_index("px") == 0) & (lax.axis_index("py") == 0))
     spectral = []
     for f in range(2):
         rows = slice(f * SIDE_ROWS, f * SIDE_ROWS + SIDE_ROWS)
@@ -251,12 +258,6 @@
             for made in along_y:
                 parts.append(jnp.concatenate([a[rows, lanes] for a in made], 1))
         spectral.append(left_product(x_into[...], jnp.concatenate(parts, 0)))
-    for r in range(4):
-        step = N_PY * SEND_ROWS
-        pieces = [got[pl.ds(py * SEND_ROWS + 16 + r, N_PX, stride=step), :] for py in range(N_PY)]
-        for j, block in enumerate(blocks_transposed(pieces)):
-            scale[r * 128 + j * 8 : r * 128 + j * 8 + 8, :] = block
-    unfold(got, scale, (lax.axis_index("px") == 0) & (lax.axis_index("py") == 0))
     restored = []
     for f in range(2):
         at = [512 + (f * 4 + r) * 128 for r in range(4)]
@@ -328,31 +329,32 @@
     h, l = split(sums2[pl.ds(0, 64, stride=2), :] + sums2[pl.ds(1, 64, stride=2), :])
     two = product(h, mean2[...]) + product(l, mean2[...])
     sums2[0:64, :] = two
-    for i in range(4):
-        route[pl.ds(16 + i, N_PY, stride=ROUTE_ROWS), :] = sums2[pl.ds(i, N_PY, stride=4), :]
     for k in range(4):
         sums3[k * 8 : k * 8 + 8, :] = two[k * 16 : k * 16 + 8] + two[k * 16 + 8 : k * 16 + 16]
     h, l = split(sums3[pl.ds(0, 16, stride=2), :] + sums3[pl.ds(1, 16, stride=2), :])
-    route[pl.ds(20, N_PY, stride=ROUTE_ROWS), :] = product(h, mean3[...]) + product(l, mean3[...])
-    for i in range(3):
-        route[pl.ds(21 + i, N_PY, stride=ROUTE_ROWS), :] = jnp.zeros((N_PY, 128), F32)
+    three = product(h, mean3[...]) + product(l, mean3[...])
+    for i in range(4):
+        row = sums2[pl.ds(i, N_PY, stride=4), :]
+        route[pl.ds(16 + i, N_PY, stride=ROUTE_ROWS), :] = row if i else row + three
     for copy in copies:
         copy.wait()
 
 
 def pick_kernel(table, got, out):
+    low = lax.broadcasted_iota(jnp.int32, (4, 128), 1) < 64
     for g in range(N_PY):
-        out[g, 0:16, :] = got[table[0, g], 0:16, :]
-        out[g, 16:20, :] = got[table[1, g], 16:20, :]
-        out[g, 20:24, :] = got[table[2, g], 20:24, :]
+        for k in range(4):
+            out[g, k, :, :] = got[table[0, g], k, :, :]
+        out[g, 4, :, :] = jnp.where(low, got[table[1, g], 4, :, :], got[table[2, g], 4, :, :])
 
 
 def unpack_kernel(got, one_far, two_far, three_far, two, three, left):
-    copies = [pltpu.make_async_copy(got.at[:, pl.ds(0, 16), :], one_far, left.at[0])]
+    copies = [pltpu.make_async_copy(got.at[:, pl.ds(0, 4), :, :], one_far, left.at[0])]
     copies[0].start()
     for p in range(N_PY):
-        two[p * 4 : p * 4 + 4, :] = got[p, 16:20, 0:64]
-        three[p : p + 1, :] = got[p, 20:21, 0:32]
+        last = got[p, 4, :, :]
+        two[p * 4 : p * 4 + 4, :] = last[:, 0:64]
+        three[p : p + 1, :] = last[0:1, 64:96]
     copies.append(pltpu.make_async_copy(two, two_far, left.at[1]))
     copies.append(pltpu.make_async_copy(three, three_far, left.at[2]))
     copies[1].start()
@@ -418,7 +420,7 @@
         *tables["into"],
         jnp.asarray(pair_mean(256)[:, :128]),
         jnp.asarray(pair_mean(128)),
-        jnp.asarray(pair_mean(128) * (np.arange(128) < 64)[:, None].astype(ml_dtypes.bfloat16)),
+        jnp.asarray(pair_mean(128, 64)),
         out_specs=[FAR, NEAR],
         scratch=(
             pltpu.VMEM((2, 512, 128), F32),
@@ -428,11 +430,11 @@
             pltpu.SemaphoreType.DMA((8,)),
         ),
     )
-    spread = lax.all_to_all(route.reshape(N_PY, ROUTE_ROWS, 128), "py", 0, 0, tiled=True)
+    spread = lax.all_to_all(route.reshape(ROUTE), "py", 0, 0, tiled=True)
     (picked,) = call(
         pick_kernel,
         "pick",
-        [pltpu.VMEM((N_PY, ROUTE_ROWS, 128), F32)],
+        [pltpu.VMEM(ROUTE, F32)],
         group_table,
         on_chip(spread),
         in_specs=[pl.BlockSpec(memory_space=pltpu.SMEM), NEAR],
@@ -441,7 +443,7 @@
     one, two, three = call(
         unpack_kernel,
         "unpack",
-        [jax.ShapeDtypeStruct(s, F32) for s in ((16, 16, 128), (64, 64), (16, 32))],
+        [jax.ShapeDtypeStruct(s, F32) for s in ((16, 4, 4, 128), (64, 64), (16, 32))],
         on_chip(levels),
         out_specs=[FAR] * 3,
         scratch=(pltpu.VMEM((64, 64), F32), pltpu.VMEM((16, 32), F32), pltpu.SemaphoreType.DMA((3,))),

time: 86.6 us -> 85.8 us (level)
  no operation moved by 1% of the time
where the time goes in v8:
time: 85.8 us; the launch traced here: 85.6 us
  blocking collectives  76.6 us (89%)
  Pallas kernels  8.17 us (10%)
    all_to_all x1, blocking collectives, on_device(): lax.all_to_all(sent.reshape(DEVICES, SEND_ROWS, 1, 128), ('px', 'py'), 0,...  33.3 us
    all_to_all x1, blocking collectives, on_device(): lax.all_to_all(restored.reshape(DEVICES, BACK_ROWS, 128), ('px', 'py'), 0...  24.2 us
    all_to_all x1, blocking collectives, on_device(): spread = lax.all_to_all(route.reshape(ROUTE), 'py', 0, 0, tiled=True)  9.83 us
    all_to_all x1, blocking collectives, on_device(): levels = lax.all_to_all(picked, 'py', 0, 0, tiled=True)  9.31 us
    pallas_call x5, Pallas kernels, call(): pl.pallas_call(body, out_shape=outs, scratch_shapes=list(scratch), name=n...  8.17 us

profile of v8, /device:TPU:1, one launch (start us, length us, event | category | flops | bytes accessed | tf_op | source)
XLA Modules:
  0.0 85.6 jit_solution(1304300109969205196)
XLA Ops:
  0.6 2.2 %into_z.1 = f32[2688,128]{1,0:T(8,128)S(1)} custom-call(f32[1024,256]{1,0:T(8,128)} %bitcast.16, f32[512,256]{1,0:T(8,128)} %bitcast.17, bf16[256,256]{1,0:T(8,128)(2,1)} %constant.18.clone.high_far.b_high, bf16[256,256]{1,0:T(8,128)(2,1)} %constant.19.clone.low_far.b_low), custom_call_target="tpu_custom_call" | custom-call | tf_op jit(solution)/shard_map/into_z/pallas_call | solution.py:375
  2.9 0.0 copy-start
  2.9 0.0 copy-start.1
  2.9 0.0 copy-start.4
  2.9 0.0 copy-start.5
  2.9 33.3 %all_to_all.20 = f32[128,21,1,128]{3,2,1,0:T(1,128)S(1)} all-to-all(f32[128,21,1,128]{3,2,1,0:T(1,128)S(1)} %bitcast.11), channel_id=1, replica_groups=mesh['px'=8,'py'=16] {'px','py'}, dimensions={0} | all-to-all | bytes 2752512 | tf_op jit(solution)/shard_map/all_to_all | solution.py:403
  36.2 0.0 copy-done
  36.2 0.0 copy-done.1
  36.2 0.0 copy-done.4
  36.2 0.0 copy-done.5
  36.2 3.0 %planes.1 = f32[2048,128]{1,0:T(8,128)S(1)} custom-call(f32[2688,128]{1,0:T(8,128)S(1)} %bitcast.12, bf16[1024,256]{1,0:T(8,128)(2,1)S(1)} %copy-done.1, bf16[1024,256]{1,0:T(8,128)(2,1)S(1)} %copy-done, bf16[512,256]{1,0:T(8,128)(2,1)S(1)} %copy-done.5, bf16[512,256]{1,0:T(8,128)(2,1)S(1)} %copy-done.4), custom_call_target="tpu_custom_call" | custom-call | tf_op jit(solution)/shard_map/planes/pallas_call | solution.py:375
  39.2 0.0 copy-start.2
  39.2 0.0 copy-start.3
  39.2 0.0 copy-start.6
  39.2 0.0 copy-start.7
  39.2 0.0 copy-start.8
  39.3 24.2 %all_to_all.21 = f32[128,16,128]{2,1,0:T(8,128)S(1)} all-to-all(f32[128,16,128]{2,1,0:T(8,128)S(1)} %bitcast.14), channel_id=1, replica_groups=mesh['px'=8,'py'=16] {'px','py'}, dimensions={0} | all-to-all | bytes 2097152 | tf_op jit(solution)/shard_map/all_to_all | solution.py:414
  63.4 0.0 copy-start.9
  63.4 0.0 copy-done.2
  63.4 0.0 copy-done.3
  63.4 0.0 copy-done.6
  63.4 0.0 copy-done.7
  63.5 0.0 copy-done.8
  63.5 1.6 %back_z.1 = (f32[1024,256]{1,0:T(8,128)}, f32[320,128]{1,0:T(8,128)S(1)}) custom-call(f32[2048,128]{1,0:T(8,128)S(1)} %bitcast.13, bf16[256,256]{1,0:T(8,128)(2,1)S(1)} %copy-done.3, bf16[256,256]{1,0:T(8,128)(2,1)S(1)} %copy-done.2, bf16[256,128]{1,0:T(8,128)(2,1)S(1)} %copy-done.6, bf16[128,128]{1,0:T(8,128)(2,1)S(1)} %copy-done.8, ...), custom_call_target="tpu_custom_call" | custom-call | tf_op jit(solution)/shard_map/back_z/pallas_call | solution.py:375
  65.1 9.8 %all_to_all.22.got = f32[16,5,4,128]{3,2,1,0:T(4,128)S(1)} all-to-all(f32[16,5,4,128]{3,2,1,0:T(4,128)S(1)} %bitcast.15), channel_id=1, replica_groups=mesh['px'=8,'py'=16] {'py'}, dimensions={0} | all-to-all | bytes 327680 | tf_op jit(solution)/shard_map/all_to_all | solution.py:433
  74.9 0.0 copy-done.9
  74.9 0.6 pick.1
  75.6 9.3 %all_to_all.23.got = f32[16,5,4,128]{3,2,1,0:T(4,128)S(1)} all-to-all(f32[16,5,4,128]{3,2,1,0:T(4,128)S(1)} %pick.1), channel_id=1, replica_groups=mesh['px'=8,'py'=16] {'py'}, dimensions={0} | all-to-all | bytes 327680 | tf_op jit(solution)/shard_map/all_to_all | solution.py:442
  84.9 0.7 unpack.1
Async XLA Ops:
  2.9 33.3 %copy-start = (bf16[1024,256]{1,0:T(8,128)(2,1)S(1)}, bf16[1024,256]{1,0:T(8,128)(2,1)}, u32[]{:S(2)}) copy-start(bf16[1024,256]{1,0:T(8,128)(2,1)} %constant.21.clone.y_low) | copy-start | bytes 1572868
  2.9 33.3 %copy-start.1 = (bf16[1024,256]{1,0:T(8,128)(2,1)S(1)}, bf16[1024,256]{1,0:T(8,128)(2,1)}, u32[]{:S(2)}) copy-start(bf16[1024,256]{1,0:T(8,128)(2,1)} %constant.20.clone.y_high) | copy-start | bytes 1572868
  2.9 33.3 %copy-start.4 = (bf16[512,256]{1,0:T(8,128)(2,1)S(1)}, bf16[512,256]{1,0:T(8,128)(2,1)}, u32[]{:S(2)}) copy-start(bf16[512,256]{1,0:T(8,128)(2,1)} %constant.23.clone.x_back) | copy-start | bytes 786436
  2.9 33.3 %copy-start.5 = (bf16[512,256]{1,0:T(8,128)(2,1)S(1)}, bf16[512,256]{1,0:T(8,128)(2,1)}, u32[]{:S(2)}) copy-start(bf16[512,256]{1,0:T(8,128)(2,1)} %constant.22.clone.x_into) | copy-start | bytes 786436
  39.2 24.2 %copy-start.2 = (bf16[256,256]{1,0:T(8,128)(2,1)S(1)}, bf16[256,256]{1,0:T(8,128)(2,1)}, u32[]{:S(2)}) copy-start(bf16[256,256]{1,0:T(8,128)(2,1)} %constant.19.clone.low_far.b_low) | copy-start | bytes 393220
  39.2 24.2 %copy-start.3 = (bf16[256,256]{1,0:T(8,128)(2,1)S(1)}, bf16[256,256]{1,0:T(8,128)(2,1)}, u32[]{:S(2)}) copy-start(bf16[256,256]{1,0:T(8,128)(2,1)} %constant.18.clone.high_far.b_high) | copy-start | bytes 393220
  39.2 24.2 %copy-start.6 = (bf16[256,128]{1,0:T(8,128)(2,1)S(1)}, bf16[256,128]{1,0:T(8,128)(2,1)}, u32[]{:S(2)}) copy-start(bf16[256,128]{1,0:T(8,128)(2,1)} %constant.24.clone.mean1) | copy-start | bytes 196612
  39.2 24.2 %copy-start.7 = (bf16[128,128]{1,0:T(8,128)(2,1)S(1)}, bf16[128,128]{1,0:T(8,128)(2,1)}, u32[]{:S(2)}) copy-start(bf16[128,128]{1,0:T(8,128)(2,1)} %constant.26.clone.mean3) | copy-start | bytes 98308
  39.2 24.2 %copy-start.8 = (bf16[128,128]{1,0:T(8,128)(2,1)S(1)}, bf16[128,128]{1,0:T(8,128)(2,1)}, u32[]{:S(2)}) copy-start(bf16[128,128]{1,0:T(8,128)(2,1)} %constant.25.clone.mean2) | copy-start | bytes 98308
  63.4 11.5 %copy-start.9 = (s32[3,16]{1,0:T(4,128)S(1)}, s32[3,16]{1,0:T(4,128)}, u32[]{:S(2)}) copy-start(s32[3,16]{1,0:T(4,128)} %table.1) | copy-start | bytes 580

commit v9 on v8

--- a/solution.py
+++ b/solution.py
@@ -340,7 +340,8 @@
         copy.wait()
 
 
-def pick_kernel(table, got, out):
+def pick_kernel(table_row, got, out):
+    table = table_row[...]
     low = lax.broadcasted_iota(jnp.int32, (4, 128), 1) < 64
     for g in range(N_PY):
         for k in range(4):
@@ -435,9 +436,8 @@
         pick_kernel,
         "pick",
         [pltpu.VMEM(ROUTE, F32)],
-        group_table,
+        on_chip(group_table),
         on_chip(spread),
-        in_specs=[pl.BlockSpec(memory_space=pltpu.SMEM), NEAR],
     )
     levels = lax.all_to_all(picked, "py", 0, 0, tiled=True)
     one, two, three = call(

time: 85.8 us -> 85.4 us (level)
  no operation moved by 1% of the time
where the time goes in v9:
time: 85.4 us; the launch traced here: 85.1 us
  blocking collectives  76.6 us (90%)
  Pallas kernels  7.7 us (9%)
    all_to_all x1, blocking collectives, on_device(): lax.all_to_all(sent.reshape(DEVICES, SEND_ROWS, 1, 128), ('px', 'py'), 0,...  33.3 us
    all_to_all x1, blocking collectives, on_device(): lax.all_to_all(restored.reshape(DEVICES, BACK_ROWS, 128), ('px', 'py'), 0...  24.2 us
    all_to_all x1, blocking collectives, on_device(): spread = lax.all_to_all(route.reshape(ROUTE), 'py', 0, 0, tiled=True)  9.83 us
    all_to_all x1, blocking collectives, on_device(): levels = lax.all_to_all(picked, 'py', 0, 0, tiled=True)  9.31 us
    pallas_call x5, Pallas kernels, call(): pl.pallas_call(body, out_shape=outs, scratch_shapes=list(scratch), name=n...  7.7 us

profile of v9, /device:TPU:1, one launch (start us, length us, event | category | flops | bytes accessed | tf_op | source)
XLA Modules:
  0.0 85.1 jit_solution(3763004862863179743)
XLA Ops:
  0.6 2.2 %into_z.1 = f32[2688,128]{1,0:T(8,128)S(1)} custom-call(f32[1024,256]{1,0:T(8,128)} %bitcast.16, f32[512,256]{1,0:T(8,128)} %bitcast.17, bf16[256,256]{1,0:T(8,128)(2,1)} %constant.18.clone.high_far.b_high, bf16[256,256]{1,0:T(8,128)(2,1)} %constant.19.clone.low_far.b_low), custom_call_target="tpu_custom_call" | custom-call | tf_op jit(solution)/shard_map/into_z/pallas_call | solution.py:376
  2.9 0.0 copy-start
  2.9 0.0 copy-start.1
  2.9 0.0 copy-start.4
  2.9 0.0 copy-start.5
  2.9 33.3 %all_to_all.20 = f32[128,21,1,128]{3,2,1,0:T(1,128)S(1)} all-to-all(f32[128,21,1,128]{3,2,1,0:T(1,128)S(1)} %bitcast.11), channel_id=1, replica_groups=mesh['px'=8,'py'=16] {'px','py'}, dimensions={0} | all-to-all | bytes 2752512 | tf_op jit(solution)/shard_map/all_to_all | solution.py:404
  36.2 0.0 copy-done
  36.2 0.0 copy-done.1
  36.2 0.0 copy-done.4
  36.2 0.0 copy-done.5
  36.2 3.0 %planes.1 = f32[2048,128]{1,0:T(8,128)S(1)} custom-call(f32[2688,128]{1,0:T(8,128)S(1)} %bitcast.12, bf16[1024,256]{1,0:T(8,128)(2,1)S(1)} %copy-done.1, bf16[1024,256]{1,0:T(8,128)(2,1)S(1)} %copy-done, bf16[512,256]{1,0:T(8,128)(2,1)S(1)} %copy-done.5, bf16[512,256]{1,0:T(8,128)(2,1)S(1)} %copy-done.4), custom_call_target="tpu_custom_call" | custom-call | tf_op jit(solution)/shard_map/planes/pallas_call | solution.py:376
  39.2 0.0 copy-start.2
  39.2 0.0 copy-start.3
  39.2 0.0 copy-start.6
  39.2 0.0 copy-start.7
  39.2 0.0 copy-start.8
  39.3 24.2 %all_to_all.21 = f32[128,16,128]{2,1,0:T(8,128)S(1)} all-to-all(f32[128,16,128]{2,1,0:T(8,128)S(1)} %bitcast.14), channel_id=1, replica_groups=mesh['px'=8,'py'=16] {'px','py'}, dimensions={0} | all-to-all | bytes 2097152 | tf_op jit(solution)/shard_map/all_to_all | solution.py:415
  63.4 0.0 copy-start.9
  63.4 0.0 copy-done.2
  63.4 0.0 copy-done.3
  63.4 0.0 copy-done.6
  63.4 0.0 copy-done.7
  63.5 0.0 copy-done.8
  63.5 1.6 %back_z.1 = (f32[1024,256]{1,0:T(8,128)}, f32[320,128]{1,0:T(8,128)S(1)}) custom-call(f32[2048,128]{1,0:T(8,128)S(1)} %bitcast.13, bf16[256,256]{1,0:T(8,128)(2,1)S(1)} %copy-done.3, bf16[256,256]{1,0:T(8,128)(2,1)S(1)} %copy-done.2, bf16[256,128]{1,0:T(8,128)(2,1)S(1)} %copy-done.6, bf16[128,128]{1,0:T(8,128)(2,1)S(1)} %copy-done.8, ...), custom_call_target="tpu_custom_call" | custom-call | tf_op jit(solution)/shard_map/back_z/pallas_call | solution.py:376
  65.1 9.8 %all_to_all.22.got = f32[16,5,4,128]{3,2,1,0:T(4,128)S(1)} all-to-all(f32[16,5,4,128]{3,2,1,0:T(4,128)S(1)} %bitcast.15), channel_id=1, replica_groups=mesh['px'=8,'py'=16] {'py'}, dimensions={0} | all-to-all | bytes 327680 | tf_op jit(solution)/shard_map/all_to_all | solution.py:434
  74.9 0.0 copy-done.9
  74.9 0.2 pick.1
  75.1 9.3 %all_to_all.23.got = f32[16,5,4,128]{3,2,1,0:T(4,128)S(1)} all-to-all(f32[16,5,4,128]{3,2,1,0:T(4,128)S(1)} %pick.1), channel_id=1, replica_groups=mesh['px'=8,'py'=16] {'py'}, dimensions={0} | all-to-all | bytes 327680 | tf_op jit(solution)/shard_map/all_to_all | solution.py:442
  84.4 0.7 unpack.1
Async XLA Ops:
  2.9 33.3 %copy-start = (bf16[1024,256]{1,0:T(8,128)(2,1)S(1)}, bf16[1024,256]{1,0:T(8,128)(2,1)}, u32[]{:S(2)}) copy-start(bf16[1024,256]{1,0:T(8,128)(2,1)} %constant.21.clone.y_low) | copy-start | bytes 1572868
  2.9 33.3 %copy-start.1 = (bf16[1024,256]{1,0:T(8,128)(2,1)S(1)}, bf16[1024,256]{1,0:T(8,128)(2,1)}, u32[]{:S(2)}) copy-start(bf16[1024,256]{1,0:T(8,128)(2,1)} %constant.20.clone.y_high) | copy-start | bytes 1572868
  2.9 33.3 %copy-start.4 = (bf16[512,256]{1,0:T(8,128)(2,1)S(1)}, bf16[512,256]{1,0:T(8,128)(2,1)}, u32[]{:S(2)}) copy-start(bf16[512,256]{1,0:T(8,128)(2,1)} %constant.23.clone.x_back) | copy-start | bytes 786436
  2.9 33.3 %copy-start.5 = (bf16[512,256]{1,0:T(8,128)(2,1)S(1)}, bf16[512,256]{1,0:T(8,128)(2,1)}, u32[]{:S(2)}) copy-start(bf16[512,256]{1,0:T(8,128)(2,1)} %constant.22.clone.x_into) | copy-start | bytes 786436
  39.2 24.2 %copy-start.2 = (bf16[256,256]{1,0:T(8,128)(2,1)S(1)}, bf16[256,256]{1,0:T(8,128)(2,1)}, u32[]{:S(2)}) copy-start(bf16[256,256]{1,0:T(8,128)(2,1)} %constant.19.clone.low_far.b_low) | copy-start | bytes 393220
  39.2 24.2 %copy-start.3 = (bf16[256,256]{1,0:T(8,128)(2,1)S(1)}, bf16[256,256]{1,0:T(8,128)(2,1)}, u32[]{:S(2)}) copy-start(bf16[256,256]{1,0:T(8,128)(2,1)} %constant.18.clone.high_far.b_high) | copy-start | bytes 393220
  39.2 24.2 %copy-start.6 = (bf16[256,128]{1,0:T(8,128)(2,1)S(1)}, bf16[256,128]{1,0:T(8,128)(2,1)}, u32[]{:S(2)}) copy-start(bf16[256,128]{1,0:T(8,128)(2,1)} %constant.24.clone.mean1) | copy-start | bytes 196612
  39.2 24.2 %copy-start.7 = (bf16[128,128]{1,0:T(8,128)(2,1)S(1)}, bf16[128,128]{1,0:T(8,128)(2,1)}, u32[]{:S(2)}) copy-start(bf16[128,128]{1,0:T(8,128)(2,1)} %constant.26.clone.mean3) | copy-start | bytes 98308
  39.2 24.2 %copy-start.8 = (bf16[128,128]{1,0:T(8,128)(2,1)S(1)}, bf16[128,128]{1,0:T(8,128)(2,1)}, u32[]{:S(2)}) copy-start(bf16[128,128]{1,0:T(8,128)(2,1)} %constant.25.clone.mean2) | copy-start | bytes 98308
  63.4 11.5 %copy-start.9 = (s32[3,16]{1,0:T(4,128)S(1)}, s32[3,16]{1,0:T(4,128)}, u32[]{:S(2)}) copy-start(s32[3,16]{1,0:T(4,128)} %table_row.1) | copy-start | bytes 580

commit v10 on v9

--- a/solution.py
+++ b/solution.py
@@ -60,9 +60,9 @@
     )
 
 
-def pair_mean(size, first=0):
-    rows, columns = np.arange(size), np.arange(128) - first
-    return (0.125 * (rows[:, None] // 2 == columns[None, :])).astype(ml_dtypes.bfloat16)
+def cell_mean(width, first=0):
+    rows, columns = np.arange(NZ), np.arange(128) - first
+    return (width**-3.0 * (rows[:, None] // width == columns[None, :])).astype(ml_dtypes.bfloat16)
 
 
 def split(values):
@@ -286,8 +286,24 @@
                         out[at : at + 8, :] = block
 
 
-def last_kernel(got, b_high, b_low, mean1, mean2, mean3, modulus_far, route, sums, sums2, sums3, modulus, left):
-    copies = []
+def box_sums(cells, store):
+    for half in range(2):
+        store[half, :, :] = cells[half]
+    count = cells[0].shape[0] // 2
+    return [store[h, pl.ds(0, count, stride=2), :] + store[h, pl.ds(1, count, stride=2), :] for h in range(2)]
+
+
+def cells_joined(cells, count):
+    ends = range(0, cells[0].shape[0], 2 * count)
+    return [jnp.concatenate([v[k : k + count] + v[k + count : k + 2 * count] for k in ends], 0) for v in cells]
+
+
+def averaged(cells, weights):
+    high, low = split(jnp.concatenate(cells, 1))
+    return product(high, weights[...]) + product(low, weights[...])
+
+
+def last_kernel(got, b_high, b_low, mean1, mean2, mean3, modulus, route, sums, sums2, sums3):
     table = b_high[...], b_low[...]
     turn = lax.axis_index("py") % 4
     first_row = lax.broadcasted_iota(jnp.int32, (128, 128), 0) == 0
@@ -312,32 +328,18 @@
                 rows = pl.ds(pl.multiple_of((p + turn) % 2 * 256 + xh * 32, 32), 32)
                 sums[0, rows, :] = both[:, :128]
                 sums[1, rows, :] = both[:, 128:]
-        for f in range(2):
-            rows = pl.ds(f * 512 + pair * 128, 128)
-            copies.append(pltpu.make_async_copy(modulus.at[rows, :], modulus_far.at[rows, :], left.at[len(copies)]))
-            copies[-1].start()
-    one = jnp.zeros((256, 128), F32)
-    for half in range(2):
-        cells = sums[half, pl.ds(0, 256, stride=2), :] + sums[half, pl.ds(1, 256, stride=2), :]
-        weights = mean1[half * 128 : half * 128 + 128, :]
-        h, l = split(cells)
-        one = one + (product(h, weights) + product(l, weights))
+    cells = [sums[h, pl.ds(0, 256, stride=2), :] + sums[h, pl.ds(1, 256, stride=2), :] for h in range(2)]
+    one = averaged(cells, mean1)
     for p in range(N_PY):
         route[p * ROUTE_ROWS : p * ROUTE_ROWS + 16, :] = one[p * 16 : p * 16 + 16]
-    for k in range(8):
-        sums2[k * 16 : k * 16 + 16, :] = one[k * 32 : k * 32 + 16] + one[k * 32 + 16 : k * 32 + 32]
-    h, l = split(sums2[pl.ds(0, 64, stride=2), :] + sums2[pl.ds(1, 64, stride=2), :])
-    two = product(h, mean2[...]) + product(l, mean2[...])
-    sums2[0:64, :] = two
-    for k in range(4):
-        sums3[k * 8 : k * 8 + 8, :] = two[k * 16 : k * 16 + 8] + two[k * 16 + 8 : k * 16 + 16]
-    h, l = split(sums3[pl.ds(0, 16, stride=2), :] + sums3[pl.ds(1, 16, stride=2), :])
-    three = product(h, mean3[...]) + product(l, mean3[...])
+    cells = box_sums(cells_joined(cells, 16), sums2)
+    two = averaged(cells, mean2)
+    cells = box_sums(cells_joined(cells, 8), sums3)
+    three = averaged(cells, mean3)
+    sums[0, 0:64, :] = two
     for i in range(4):
-        row = sums2[pl.ds(i, N_PY, stride=4), :]
+        row = sums[0, pl.ds(i, N_PY, stride=4), :]
         route[pl.ds(16 + i, N_PY, stride=ROUTE_ROWS), :] = row if i else row + three
-    for copy in copies:
-        copy.wait()
 
 
 def pick_kernel(table_row, got, out):
@@ -416,20 +418,11 @@
     modulus, route = call(
         last_kernel,
         "back_z",
-        [jax.ShapeDtypeStruct((1024, NZ), F32), pltpu.VMEM((N_PY * ROUTE_ROWS, 128), F32)],
+        [pltpu.VMEM((1024, NZ), F32), pltpu.VMEM((N_PY * ROUTE_ROWS, 128), F32)],
         on_chip(back.reshape(DEVICES * BACK_ROWS, 128)),
         *tables["into"],
-        jnp.asarray(pair_mean(256)[:, :128]),
-        jnp.asarray(pair_mean(128)),
-        jnp.asarray(pair_mean(128, 64)),
-        out_specs=[FAR, NEAR],
-        scratch=(
-            pltpu.VMEM((2, 512, 128), F32),
-            pltpu.VMEM((128, 128), F32),
-            pltpu.VMEM((32, 128), F32),
-            pltpu.VMEM((1024, NZ), F32),
-            pltpu.SemaphoreType.DMA((8,)),
-        ),
+        *(on_chip(jnp.asarray(cell_mean(*k))) for k in ((2,), (4,), (8, 64))),
+        scratch=(pltpu.VMEM((2, 512, 128), F32), pltpu.VMEM((2, 128, 128), F32), pltpu.VMEM((2, 32, 128), F32)),
     )
     spread = lax.all_to_all(route.reshape(ROUTE), "py", 0, 0, tiled=True)
     (picked,) = call(

time: 85.4 us -> 86.5 us (1.013)
  blocking collectives: 76.6 us -> 67.3 us
  waiting for transfers between devices: 0 us -> 5.54 us
  starting transfers between devices: 0 us -> 3.7 us
  local copies, waits for them, and re-layouts: 0.07 us -> 1.03 us
    all_to_all x1 -> x0, blocking collectives: 9.31 us -> none  [on_device(): levels = lax.all_to_all(picked, 'py', 0, 0, tiled=True)]
    all_to_all x0 -> x1, waiting for transfers between devices: none -> 5.54 us  [on_device(): levels = lax.all_to_all(picked, 'py', 0, 0, tiled=True)]
    all_to_all x0 -> x1, starting transfers between devices: none -> 3.7 us  [on_device(): levels = lax.all_to_all(picked, 'py', 0, 0, tiled=True)]
    unnamed x20 -> x21, local copies, waits for them, and re-layouts: 0.07 us -> 1.03 us
  transfers between devices with their start and end apart: 0 -> 1, of which waited for: 0 -> 1; matrix products, arithmetic and copies ran while one was open for 0% -> 1% of each run, Pallas kernels for 0% -> 0%
where the time goes in v10:
time: 86.5 us; the launch traced here: 86.1 us
  blocking collectives  67.3 us (78%)
  Pallas kernels  7.85 us (9%)
  waiting for transfers between devices  5.54 us (6%)
  starting transfers between devices  3.7 us (4%)
  local copies, waits for them, and re-layouts  1.03 us (1%)
    all_to_all x1, blocking collectives, on_device(): lax.all_to_all(sent.reshape(DEVICES, SEND_ROWS, 1, 128), ('px', 'py'), 0,...  33.3 us
    all_to_all x1, blocking collectives, on_device(): lax.all_to_all(restored.reshape(DEVICES, BACK_ROWS, 128), ('px', 'py'), 0...  24.2 us
    all_to_all x1, blocking collectives, on_device(): spread = lax.all_to_all(route.reshape(ROUTE), 'py', 0, 0, tiled=True)  9.83 us
    pallas_call x5, Pallas kernels, call(): pl.pallas_call(body, out_shape=outs, scratch_shapes=list(scratch), name=n...  7.85 us
    all_to_all x1, waiting for transfers between devices, on_device(): levels = lax.all_to_all(picked, 'py', 0, 0, tiled=True)  5.54 us
    all_to_all x1, starting transfers between devices, on_device(): levels = lax.all_to_all(picked, 'py', 0, 0, tiled=True)  3.7 us
  transfers between devices with their start and end apart: 1, of which 1 were waited for; matrix products, arithmetic and copies ran while one was open for 1% of the time, Pallas kernels for 0%

profile of v10, /device:TPU:1, one launch (start us, length us, event | category | flops | bytes accessed | tf_op | source)
XLA Modules:
  0.0 86.1 jit_solution(6907523114313961299)
XLA Ops:
  0.6 2.2 %into_z.1 = f32[2688,128]{1,0:T(8,128)S(1)} custom-call(f32[1024,256]{1,0:T(8,128)} %bitcast.17, f32[512,256]{1,0:T(8,128)} %bitcast.18, bf16[256,256]{1,0:T(8,128)(2,1)} %constant.18.clone.high_far.b_high, bf16[256,256]{1,0:T(8,128)(2,1)} %constant.19.clone.low_far.b_low), custom_call_target="tpu_custom_call" | custom-call | tf_op jit(solution)/shard_map/into_z/pallas_call | solution.py:378
  2.9 0.0 copy-start
  2.9 0.0 copy-start.1
  2.9 0.0 copy-start.4
  2.9 0.0 copy-start.5
  2.9 33.3 %all_to_all.20 = f32[128,21,1,128]{3,2,1,0:T(1,128)S(1)} all-to-all(f32[128,21,1,128]{3,2,1,0:T(1,128)S(1)} %bitcast.12), channel_id=1, replica_groups=mesh['px'=8,'py'=16] {'px','py'}, dimensions={0} | all-to-all | bytes 2752512 | tf_op jit(solution)/shard_map/all_to_all | solution.py:406
  36.2 0.0 copy-done
  36.2 0.0 copy-done.1
  36.2 0.0 copy-done.4
  36.2 0.0 copy-done.5
  36.2 3.0 %planes.1 = f32[2048,128]{1,0:T(8,128)S(1)} custom-call(f32[2688,128]{1,0:T(8,128)S(1)} %bitcast.13, bf16[1024,256]{1,0:T(8,128)(2,1)S(1)} %copy-done.1, bf16[1024,256]{1,0:T(8,128)(2,1)S(1)} %copy-done, bf16[512,256]{1,0:T(8,128)(2,1)S(1)} %copy-done.5, bf16[512,256]{1,0:T(8,128)(2,1)S(1)} %copy-done.4), custom_call_target="tpu_custom_call" | custom-call | tf_op jit(solution)/shard_map/planes/pallas_call | solution.py:378
  39.2 0.0 copy-start.2
  39.2 0.0 copy-start.3
  39.2 0.0 copy-start.6
  39.2 0.0 copy-start.7
  39.2 0.0 copy-start.8
  39.3 24.2 %all_to_all.21 = f32[128,16,128]{2,1,0:T(8,128)S(1)} all-to-all(f32[128,16,128]{2,1,0:T(8,128)S(1)} %bitcast.15), channel_id=1, replica_groups=mesh['px'=8,'py'=16] {'px','py'}, dimensions={0} | all-to-all | bytes 2097152 | tf_op jit(solution)/shard_map/all_to_all | solution.py:417
  63.4 0.0 copy-start.9
  63.4 0.0 copy-done.2
  63.4 0.0 copy-done.3
  63.4 0.0 copy-done.6
  63.4 0.0 copy-done.7
  63.5 0.0 copy-done.8
  63.5 1.1 %back_z.1 = (f32[1024,256]{1,0:T(8,128)S(1)}, f32[320,128]{1,0:T(8,128)S(1)}) custom-call(f32[2048,128]{1,0:T(8,128)S(1)} %bitcast.14, bf16[256,256]{1,0:T(8,128)(2,1)S(1)} %copy-done.3, bf16[256,256]{1,0:T(8,128)(2,1)S(1)} %copy-done.2, bf16[256,128]{1,0:T(8,128)(2,1)S(1)} %copy-done.8, bf16[256,128]{1,0:T(8,128)(2,1)S(1)} %copy-done.7, ...), custom_call_target="tpu_custom_call" | custom-call | tf_op jit(solution)/shard_map/back_z/pallas_call | solution.py:378
  64.6 9.8 %all_to_all.22.got = f32[16,5,4,128]{3,2,1,0:T(4,128)S(1)} all-to-all(f32[16,5,4,128]{3,2,1,0:T(4,128)S(1)} %bitcast.16), channel_id=1, replica_groups=mesh['px'=8,'py'=16] {'py'}, dimensions={0} | all-to-all | bytes 327680 | tf_op jit(solution)/shard_map/all_to_all | solution.py:427
  74.4 0.0 copy-done.9
  74.4 0.8 pick.1
  75.2 3.7 %all-to-all-start.3 = ((f32[16,5,4,128]{3,2,1,0:T(4,128)}), f32[16,5,4,128]{3,2,1,0:T(4,128)S(1)}, u32[]{:S(2)}, u32[]{:S(2)}) async-start(f32[16,5,4,128]{3,2,1,0:T(4,128)} %pick.1), calls=%async_computation.3 | async-start | bytes 327680 | tf_op jit(solution)/shard_map/all_to_all | solution.py:435
  78.9 1.0 %copy.17 = f32[2,16,32,256]{3,2,1,0:T(8,128)} copy(f32[2,16,32,256]{3,2,1,0:T(8,128)S(1)} %bitcast.11) | data formatting | bytes 2097152
  79.9 5.5 %all-to-all-done.3.got = f32[16,5,4,128]{3,2,1,0:T(4,128)S(1)} async-done(((f32[16,5,4,128]{3,2,1,0:T(4,128)}), f32[16,5,4,128]{3,2,1,0:T(4,128)S(1)}, u32[]{:S(2)}, u32[]{:S(2)}) %all-to-all-start.3) | async-done | bytes 163872 | tf_op jit(solution)/shard_map/all_to_all | solution.py:435
  85.4 0.7 unpack.1
Async XLA Ops:
  2.9 33.3 %copy-start = (bf16[1024,256]{1,0:T(8,128)(2,1)S(1)}, bf16[1024,256]{1,0:T(8,128)(2,1)}, u32[]{:S(2)}) copy-start(bf16[1024,256]{1,0:T(8,128)(2,1)} %constant.21.clone.y_low) | copy-start | bytes 1572868
  2.9 33.3 %copy-start.1 = (bf16[1024,256]{1,0:T(8,128)(2,1)S(1)}, bf16[1024,256]{1,0:T(8,128)(2,1)}, u32[]{:S(2)}) copy-start(bf16[1024,256]{1,0:T(8,128)(2,1)} %constant.20.clone.y_high) | copy-start | bytes 1572868
  2.9 33.3 %copy-start.4 = (bf16[512,256]{1,0:T(8,128)(2,1)S(1)}, bf16[512,256]{1,0:T(8,128)(2,1)}, u32[]{:S(2)}) copy-start(bf16[512,256]{1,0:T(8,128)(2,1)} %constant.23.clone.x_back) | copy-start | bytes 786436
  2.9 33.3 %copy-start.5 = (bf16[512,256]{1,0:T(8,128)(2,1)S(1)}, bf16[512,256]{1,0:T(8,128)(2,1)}, u32[]{:S(2)}) copy-start(bf16[512,256]{1,0:T(8,128)(2,1)} %constant.22.clone.x_into) | copy-start | bytes 786436
  39.2 24.2 %copy-start.2 = (bf16[256,256]{1,0:T(8,128)(2,1)S(1)}, bf16[256,256]{1,0:T(8,128)(2,1)}, u32[]{:S(2)}) copy-start(bf16[256,256]{1,0:T(8,128)(2,1)} %constant.19.clone.low_far.b_low) | copy-start | bytes 393220
  39.2 24.2 %copy-start.3 = (bf16[256,256]{1,0:T(8,128)(2,1)S(1)}, bf16[256,256]{1,0:T(8,128)(2,1)}, u32[]{:S(2)}) copy-start(bf16[256,256]{1,0:T(8,128)(2,1)} %constant.18.clone.high_far.b_high) | copy-start | bytes 393220
  39.2 24.2 %copy-start.6 = (bf16[256,128]{1,0:T(8,128)(2,1)S(1)}, bf16[256,128]{1,0:T(8,128)(2,1)}, u32[]{:S(2)}) copy-start(bf16[256,128]{1,0:T(8,128)(2,1)} %constant.26.clone.mean3) | copy-start | bytes 196612
  39.2 24.2 %copy-start.7 = (bf16[256,128]{1,0:T(8,128)(2,1)S(1)}, bf16[256,128]{1,0:T(8,128)(2,1)}, u32[]{:S(2)}) copy-start(bf16[256,128]{1,0:T(8,128)(2,1)} %constant.25.clone.mean2) | copy-start | bytes 196612
  39.2 24.2 %copy-start.8 = (bf16[256,128]{1,0:T(8,128)(2,1)S(1)}, bf16[256,128]{1,0:T(8,128)(2,1)}, u32[]{:S(2)}) copy-start(bf16[256,128]{1,0:T(8,128)(2,1)} %constant.24.clone.mean1) | copy-start | bytes 196612
  63.4 11.0 %copy-start.9 = (s32[3,16]{1,0:T(4,128)S(1)}, s32[3,16]{1,0:T(4,128)}, u32[]{:S(2)}) copy-start(s32[3,16]{1,0:T(4,128)} %table_row.1) | copy-start | bytes 580
  75.2 10.2 %all-to-all-start.3 = ((f32[16,5,4,128]{3,2,1,0:T(4,128)}), f32[16,5,4,128]{3,2,1,0:T(4,128)S(1)}, u32[]{:S(2)}, u32[]{:S(2)}) async-start(f32[16,5,4,128]{3,2,1,0:T(4,128)} %pick.1), calls=%async_computation.3 | async-start | bytes 327680 | tf_op jit(solution)/shard_map/all_to_all | solution.py:435

commit v11 on v9

--- a/solution.py
+++ b/solution.py
@@ -155,8 +155,19 @@
     for half in range(2):
         columns = spectrum_far.at[:, pl.ds(half * 128, 128)]
         copies.append(pltpu.make_async_copy(columns, spectrum.at[half], arrived.at[len(copies)]))
-    for copy in copies:
+    for copy in copies[6:] + copies[:6]:
         copy.start()
+    for copy in copies[6:]:
+        copy.wait()
+    lower = lax.axis_index("py") < N_PY // 2
+    for r in range(4):
+        plane = spectrum[0, pl.ds(r, 128, stride=4), :].T
+        other = spectrum[1, pl.ds(r, 128, stride=4), :].T[:1]
+        out[pl.ds(16 + r, DEVICES, stride=SEND_ROWS), :] = plane
+        out[16 + r : 17 + r, :] = jnp.where(lower, plane[:1], other)
+        if r == 0:
+            out[pl.ds(20, DEVICES, stride=SEND_ROWS), :] = plane
+            out[20:21, :] = jnp.where(lower, other, plane[:1])
     for copy in copies[:6]:
         copy.wait()
     table = t_high[...], t_low[...]
@@ -175,17 +186,6 @@
             new0, new1 = swapped_parts(part0[:8], part1[:8], turn)
             out[xh : xh + 1, :] = new0[:1]
             out[8 + xh : 9 + xh, :] = new1[:1]
-    for copy in copies[6:]:
-        copy.wait()
-    lower = lax.axis_index("py") < N_PY // 2
-    for r in range(4):
-        plane = spectrum[0, pl.ds(r, 128, stride=4), :].T
-        other = spectrum[1, pl.ds(r, 128, stride=4), :].T[:1]
-        out[pl.ds(16 + r, DEVICES, stride=SEND_ROWS), :] = plane
-        out[16 + r : 17 + r, :] = jnp.where(lower, plane[:1], other)
-        if r == 0:
-            out[pl.ds(20, DEVICES, stride=SEND_ROWS), :] = plane
-            out[20:21, :] = jnp.where(lower, other, plane[:1])
 
 
 def unfold(got, scale, first):

time: 85.4 us -> 85.3 us (level)
  no operation moved by 1% of the time
where the time goes in v11:
time: 85.3 us; the launch traced here: 85 us
  blocking collectives  76.6 us (90%)
  Pallas kernels  7.61 us (9%)
    all_to_all x1, blocking collectives, on_device(): lax.all_to_all(sent.reshape(DEVICES, SEND_ROWS, 1, 128), ('px', 'py'), 0,...  33.2 us
    all_to_all x1, blocking collectives, on_device(): lax.all_to_all(restored.reshape(DEVICES, BACK_ROWS, 128), ('px', 'py'), 0...  24.2 us
    all_to_all x1, blocking collectives, on_device(): spread = lax.all_to_all(route.reshape(ROUTE), 'py', 0, 0, tiled=True)  9.83 us
    all_to_all x1, blocking collectives, on_device(): levels = lax.all_to_all(picked, 'py', 0, 0, tiled=True)  9.31 us
    pallas_call x5, Pallas kernels, call(): pl.pallas_call(body, out_shape=outs, scratch_shapes=list(scratch), name=n...  7.61 us

profile of v11, /device:TPU:1, one launch (start us, length us, event | category | flops | bytes accessed | tf_op | source)
XLA Modules:
  0.0 85.0 jit_solution(12578686481792671732)
XLA Ops:
  0.6 2.2 %into_z.1 = f32[2688,128]{1,0:T(8,128)S(1)} custom-call(f32[1024,256]{1,0:T(8,128)} %bitcast.16, f32[512,256]{1,0:T(8,128)} %bitcast.17, bf16[256,256]{1,0:T(8,128)(2,1)} %constant.18.clone.high_far.b_high, bf16[256,256]{1,0:T(8,128)(2,1)} %constant.19.clone.low_far.b_low), custom_call_target="tpu_custom_call" | custom-call | tf_op jit(solution)/shard_map/into_z/pallas_call | solution.py:376
  2.8 0.0 copy-start
  2.8 0.0 copy-start.1
  2.8 0.0 copy-start.4
  2.8 0.0 copy-start.5
  2.8 33.2 %all_to_all.20 = f32[128,21,1,128]{3,2,1,0:T(1,128)S(1)} all-to-all(f32[128,21,1,128]{3,2,1,0:T(1,128)S(1)} %bitcast.11), channel_id=1, replica_groups=mesh['px'=8,'py'=16] {'px','py'}, dimensions={0} | all-to-all | bytes 2752512 | tf_op jit(solution)/shard_map/all_to_all | solution.py:404
  36.1 0.0 copy-done
  36.1 0.0 copy-done.1
  36.1 0.0 copy-done.4
  36.1 0.0 copy-done.5
  36.1 3.0 %planes.1 = f32[2048,128]{1,0:T(8,128)S(1)} custom-call(f32[2688,128]{1,0:T(8,128)S(1)} %bitcast.12, bf16[1024,256]{1,0:T(8,128)(2,1)S(1)} %copy-done.1, bf16[1024,256]{1,0:T(8,128)(2,1)S(1)} %copy-done, bf16[512,256]{1,0:T(8,128)(2,1)S(1)} %copy-done.5, bf16[512,256]{1,0:T(8,128)(2,1)S(1)} %copy-done.4), custom_call_target="tpu_custom_call" | custom-call | tf_op jit(solution)/shard_map/planes/pallas_call | solution.py:376
  39.1 0.0 copy-start.2
  39.1 0.0 copy-start.3
  39.1 0.0 copy-start.6
  39.1 0.0 copy-start.7
  39.1 0.0 copy-start.8
  39.2 24.2 %all_to_all.21 = f32[128,16,128]{2,1,0:T(8,128)S(1)} all-to-all(f32[128,16,128]{2,1,0:T(8,128)S(1)} %bitcast.14), channel_id=1, replica_groups=mesh['px'=8,'py'=16] {'px','py'}, dimensions={0} | all-to-all | bytes 2097152 | tf_op jit(solution)/shard_map/all_to_all | solution.py:415
  63.3 0.0 copy-start.9
  63.3 0.0 copy-done.2
  63.3 0.0 copy-done.3
  63.3 0.0 copy-done.6
  63.3 0.0 copy-done.7
  63.4 0.0 copy-done.8
  63.4 1.6 %back_z.1 = (f32[1024,256]{1,0:T(8,128)}, f32[320,128]{1,0:T(8,128)S(1)}) custom-call(f32[2048,128]{1,0:T(8,128)S(1)} %bitcast.13, bf16[256,256]{1,0:T(8,128)(2,1)S(1)} %copy-done.3, bf16[256,256]{1,0:T(8,128)(2,1)S(1)} %copy-done.2, bf16[256,128]{1,0:T(8,128)(2,1)S(1)} %copy-done.6, bf16[128,128]{1,0:T(8,128)(2,1)S(1)} %copy-done.8, ...), custom_call_target="tpu_custom_call" | custom-call | tf_op jit(solution)/shard_map/back_z/pallas_call | solution.py:376
  65.0 9.8 %all_to_all.22.got = f32[16,5,4,128]{3,2,1,0:T(4,128)S(1)} all-to-all(f32[16,5,4,128]{3,2,1,0:T(4,128)S(1)} %bitcast.15), channel_id=1, replica_groups=mesh['px'=8,'py'=16] {'py'}, dimensions={0} | all-to-all | bytes 327680 | tf_op jit(solution)/shard_map/all_to_all | solution.py:434
  74.8 0.0 copy-done.9
  74.8 0.2 pick.1
  75.0 9.3 %all_to_all.23.got = f32[16,5,4,128]{3,2,1,0:T(4,128)S(1)} all-to-all(f32[16,5,4,128]{3,2,1,0:T(4,128)S(1)} %pick.1), channel_id=1, replica_groups=mesh['px'=8,'py'=16] {'py'}, dimensions={0} | all-to-all | bytes 327680 | tf_op jit(solution)/shard_map/all_to_all | solution.py:442
  84.3 0.7 unpack.1
Async XLA Ops:
  2.8 33.3 %copy-start = (bf16[1024,256]{1,0:T(8,128)(2,1)S(1)}, bf16[1024,256]{1,0:T(8,128)(2,1)}, u32[]{:S(2)}) copy-start(bf16[1024,256]{1,0:T(8,128)(2,1)} %constant.21.clone.y_low) | copy-start | bytes 1572868
  2.8 33.3 %copy-start.1 = (bf16[1024,256]{1,0:T(8,128)(2,1)S(1)}, bf16[1024,256]{1,0:T(8,128)(2,1)}, u32[]{:S(2)}) copy-start(bf16[1024,256]{1,0:T(8,128)(2,1)} %constant.20.clone.y_high) | copy-start | bytes 1572868
  2.8 33.3 %copy-start.4 = (bf16[512,256]{1,0:T(8,128)(2,1)S(1)}, bf16[512,256]{1,0:T(8,128)(2,1)}, u32[]{:S(2)}) copy-start(bf16[512,256]{1,0:T(8,128)(2,1)} %constant.23.clone.x_back) | copy-start | bytes 786436
  2.8 33.3 %copy-start.5 = (bf16[512,256]{1,0:T(8,128)(2,1)S(1)}, bf16[512,256]{1,0:T(8,128)(2,1)}, u32[]{:S(2)}) copy-start(bf16[512,256]{1,0:T(8,128)(2,1)} %constant.22.clone.x_into) | copy-start | bytes 786436
  39.1 24.2 %copy-start.2 = (bf16[256,256]{1,0:T(8,128)(2,1)S(1)}, bf16[256,256]{1,0:T(8,128)(2,1)}, u32[]{:S(2)}) copy-start(bf16[256,256]{1,0:T(8,128)(2,1)} %constant.19.clone.low_far.b_low) | copy-start | bytes 393220
  39.1 24.2 %copy-start.3 = (bf16[256,256]{1,0:T(8,128)(2,1)S(1)}, bf16[256,256]{1,0:T(8,128)(2,1)}, u32[]{:S(2)}) copy-start(bf16[256,256]{1,0:T(8,128)(2,1)} %constant.18.clone.high_far.b_high) | copy-start | bytes 393220
  39.1 24.2 %copy-start.6 = (bf16[256,128]{1,0:T(8,128)(2,1)S(1)}, bf16[256,128]{1,0:T(8,128)(2,1)}, u32[]{:S(2)}) copy-start(bf16[256,128]{1,0:T(8,128)(2,1)} %constant.24.clone.mean1) | copy-start | bytes 196612
  39.1 24.2 %copy-start.7 = (bf16[128,128]{1,0:T(8,128)(2,1)S(1)}, bf16[128,128]{1,0:T(8,128)(2,1)}, u32[]{:S(2)}) copy-start(bf16[128,128]{1,0:T(8,128)(2,1)} %constant.26.clone.mean3) | copy-start | bytes 98308
  39.1 24.2 %copy-start.8 = (bf16[128,128]{1,0:T(8,128)(2,1)S(1)}, bf16[128,128]{1,0:T(8,128)(2,1)}, u32[]{:S(2)}) copy-start(bf16[128,128]{1,0:T(8,128)(2,1)} %constant.25.clone.mean2) | copy-start | bytes 98308
  63.3 11.5 %copy-start.9 = (s32[3,16]{1,0:T(4,128)S(1)}, s32[3,16]{1,0:T(4,128)}, u32[]{:S(2)}) copy-start(s32[3,16]{1,0:T(4,128)} %table_row.1) | copy-start | bytes 580

commit v12 on v11

--- a/solution.py
+++ b/solution.py
@@ -15,7 +15,7 @@
 SEND_ROWS = 21
 BACK_ROWS = 16
 ROUTE_ROWS = 20
-SIDES = 2
+SIDES = 1
 SIDE_ROWS = NX // SIDES
 VMEM_BYTES = 24 << 20
 ROUTE = (N_PY, ROUTE_ROWS // 4, 4, 128)

time: 85.3 us -> 85.2 us (level)
  no operation moved by 1% of the time
where the time goes in v12:
time: 85.2 us; the launch traced here: 84.9 us
  blocking collectives  76.6 us (90%)
  Pallas kernels  7.49 us (9%)
    all_to_all x1, blocking collectives, on_device(): lax.all_to_all(sent.reshape(DEVICES, SEND_ROWS, 1, 128), ('px', 'py'), 0,...  33.2 us
    all_to_all x1, blocking collectives, on_device(): lax.all_to_all(restored.reshape(DEVICES, BACK_ROWS, 128), ('px', 'py'), 0...  24.2 us
    all_to_all x1, blocking collectives, on_device(): spread = lax.all_to_all(route.reshape(ROUTE), 'py', 0, 0, tiled=True)  9.83 us
    all_to_all x1, blocking collectives, on_device(): levels = lax.all_to_all(picked, 'py', 0, 0, tiled=True)  9.31 us
    pallas_call x5, Pallas kernels, call(): pl.pallas_call(body, out_shape=outs, scratch_shapes=list(scratch), name=n...  7.49 us

profile of v12, /device:TPU:1, one launch (start us, length us, event | category | flops | bytes accessed | tf_op | source)
XLA Modules:
  0.0 84.9 jit_solution(7735053615812262858)
XLA Ops:
  0.6 2.2 %into_z.1 = f32[2688,128]{1,0:T(8,128)S(1)} custom-call(f32[1024,256]{1,0:T(8,128)} %bitcast.16, f32[512,256]{1,0:T(8,128)} %bitcast.17, bf16[256,256]{1,0:T(8,128)(2,1)} %constant.18.clone.high_far.b_high, bf16[256,256]{1,0:T(8,128)(2,1)} %constant.19.clone.low_far.b_low), custom_call_target="tpu_custom_call" | custom-call | tf_op jit(solution)/shard_map/into_z/pallas_call | solution.py:376
  2.8 0.0 copy-start
  2.8 0.0 copy-start.1
  2.8 0.0 copy-start.4
  2.8 0.0 copy-start.5
  2.8 33.2 %all_to_all.20 = f32[128,21,1,128]{3,2,1,0:T(1,128)S(1)} all-to-all(f32[128,21,1,128]{3,2,1,0:T(1,128)S(1)} %bitcast.11), channel_id=1, replica_groups=mesh['px'=8,'py'=16] {'px','py'}, dimensions={0} | all-to-all | bytes 2752512 | tf_op jit(solution)/shard_map/all_to_all | solution.py:404
  36.1 0.0 copy-done
  36.1 0.0 copy-done.1
  36.1 0.0 copy-done.4
  36.1 0.0 copy-done.5
  36.1 2.9 %planes.1 = f32[2048,128]{1,0:T(8,128)S(1)} custom-call(f32[2688,128]{1,0:T(8,128)S(1)} %bitcast.12, bf16[1024,256]{1,0:T(8,128)(2,1)S(1)} %copy-done.1, bf16[1024,256]{1,0:T(8,128)(2,1)S(1)} %copy-done, bf16[512,256]{1,0:T(8,128)(2,1)S(1)} %copy-done.5, bf16[512,256]{1,0:T(8,128)(2,1)S(1)} %copy-done.4), custom_call_target="tpu_custom_call" | custom-call | tf_op jit(solution)/shard_map/planes/pallas_call | solution.py:376
  39.0 0.0 copy-start.2
  39.0 0.0 copy-start.3
  39.0 0.0 copy-start.6
  39.0 0.0 copy-start.7
  39.0 0.0 copy-start.8
  39.0 24.2 %all_to_all.21 = f32[128,16,128]{2,1,0:T(8,128)S(1)} all-to-all(f32[128,16,128]{2,1,0:T(8,128)S(1)} %bitcast.14), channel_id=1, replica_groups=mesh['px'=8,'py'=16] {'px','py'}, dimensions={0} | all-to-all | bytes 2097152 | tf_op jit(solution)/shard_map/all_to_all | solution.py:415
  63.2 0.0 copy-start.9
  63.2 0.0 copy-done.2
  63.2 0.0 copy-done.3
  63.2 0.0 copy-done.6
  63.2 0.0 copy-done.7
  63.2 0.0 copy-done.8
  63.3 1.6 %back_z.1 = (f32[1024,256]{1,0:T(8,128)}, f32[320,128]{1,0:T(8,128)S(1)}) custom-call(f32[2048,128]{1,0:T(8,128)S(1)} %bitcast.13, bf16[256,256]{1,0:T(8,128)(2,1)S(1)} %copy-done.3, bf16[256,256]{1,0:T(8,128)(2,1)S(1)} %copy-done.2, bf16[256,128]{1,0:T(8,128)(2,1)S(1)} %copy-done.6, bf16[128,128]{1,0:T(8,128)(2,1)S(1)} %copy-done.8, ...), custom_call_target="tpu_custom_call" | custom-call | tf_op jit(solution)/shard_map/back_z/pallas_call | solution.py:376
  64.9 9.8 %all_to_all.22.got = f32[16,5,4,128]{3,2,1,0:T(4,128)S(1)} all-to-all(f32[16,5,4,128]{3,2,1,0:T(4,128)S(1)} %bitcast.15), channel_id=1, replica_groups=mesh['px'=8,'py'=16] {'py'}, dimensions={0} | all-to-all | bytes 327680 | tf_op jit(solution)/shard_map/all_to_all | solution.py:434
  74.7 0.0 copy-done.9
  74.7 0.2 pick.1
  74.9 9.3 %all_to_all.23.got = f32[16,5,4,128]{3,2,1,0:T(4,128)S(1)} all-to-all(f32[16,5,4,128]{3,2,1,0:T(4,128)S(1)} %pick.1), channel_id=1, replica_groups=mesh['px'=8,'py'=16] {'py'}, dimensions={0} | all-to-all | bytes 327680 | tf_op jit(solution)/shard_map/all_to_all | solution.py:442
  84.2 0.7 unpack.1
Async XLA Ops:
  2.8 33.3 %copy-start = (bf16[1024,256]{1,0:T(8,128)(2,1)S(1)}, bf16[1024,256]{1,0:T(8,128)(2,1)}, u32[]{:S(2)}) copy-start(bf16[1024,256]{1,0:T(8,128)(2,1)} %constant.21.clone.y_low) | copy-start | bytes 1572868
  2.8 33.3 %copy-start.1 = (bf16[1024,256]{1,0:T(8,128)(2,1)S(1)}, bf16[1024,256]{1,0:T(8,128)(2,1)}, u32[]{:S(2)}) copy-start(bf16[1024,256]{1,0:T(8,128)(2,1)} %constant.20.clone.y_high) | copy-start | bytes 1572868
  2.8 33.3 %copy-start.4 = (bf16[512,256]{1,0:T(8,128)(2,1)S(1)}, bf16[512,256]{1,0:T(8,128)(2,1)}, u32[]{:S(2)}) copy-start(bf16[512,256]{1,0:T(8,128)(2,1)} %constant.23.clone.x_back) | copy-start | bytes 786436
  2.8 33.3 %copy-start.5 = (bf16[512,256]{1,0:T(8,128)(2,1)S(1)}, bf16[512,256]{1,0:T(8,128)(2,1)}, u32[]{:S(2)}) copy-start(bf16[512,256]{1,0:T(8,128)(2,1)} %constant.22.clone.x_into) | copy-start | bytes 786436
  39.0 24.2 %copy-start.2 = (bf16[256,256]{1,0:T(8,128)(2,1)S(1)}, bf16[256,256]{1,0:T(8,128)(2,1)}, u32[]{:S(2)}) copy-start(bf16[256,256]{1,0:T(8,128)(2,1)} %constant.19.clone.low_far.b_low) | copy-start | bytes 393220
  39.0 24.2 %copy-start.3 = (bf16[256,256]{1,0:T(8,128)(2,1)S(1)}, bf16[256,256]{1,0:T(8,128)(2,1)}, u32[]{:S(2)}) copy-start(bf16[256,256]{1,0:T(8,128)(2,1)} %constant.18.clone.high_far.b_high) | copy-start | bytes 393220
  39.0 24.2 %copy-start.6 = (bf16[256,128]{1,0:T(8,128)(2,1)S(1)}, bf16[256,128]{1,0:T(8,128)(2,1)}, u32[]{:S(2)}) copy-start(bf16[256,128]{1,0:T(8,128)(2,1)} %constant.24.clone.mean1) | copy-start | bytes 196612
  39.0 24.2 %copy-start.7 = (bf16[128,128]{1,0:T(8,128)(2,1)S(1)}, bf16[128,128]{1,0:T(8,128)(2,1)}, u32[]{:S(2)}) copy-start(bf16[128,128]{1,0:T(8,128)(2,1)} %constant.26.clone.mean3) | copy-start | bytes 98308
  39.0 24.2 %copy-start.8 = (bf16[128,128]{1,0:T(8,128)(2,1)S(1)}, bf16[128,128]{1,0:T(8,128)(2,1)}, u32[]{:S(2)}) copy-start(bf16[128,128]{1,0:T(8,128)(2,1)} %constant.25.clone.mean2) | copy-start | bytes 98308
  63.2 11.5 %copy-start.9 = (s32[3,16]{1,0:T(4,128)S(1)}, s32[3,16]{1,0:T(4,128)}, u32[]{:S(2)}) copy-start(s32[3,16]{1,0:T(4,128)} %table_row.1) | copy-start | bytes 580
